TPU v7x, 32 devices: a whole 2x2x4 slice. The times are simulated.
32 devices in a mesh: seq: 8 (over z, y), head: 4 (over x, core).
Axes of the slice: x: 2, y: 2, z: 4, core: 2. Of those that a mesh axis runs over, the one named last changes fastest.
Arguments:
- query: bfloat16 [8, 40, 128], P(None, 'head'), may hold values from -400 to 400
- key_cache: bfloat16 [8, 4096, 8, 128], P(None, 'seq', 'head'), may hold values from -6 to 6
- value_cache: bfloat16 [8, 4096, 8, 128], P(None, 'seq', 'head'), may hold values from -6 to 6
- new_key: bfloat16 [8, 8, 128], P(None, 'head'), may hold values from -6 to 6
- new_value: bfloat16 [8, 8, 128], P(None, 'head'), may hold values from -6 to 6
- lengths: int32 [8], replicated, may hold values from 1024 to 4096, as said below
- out_weight: bfloat16 [5120, 5120], P('head', 'seq'), may hold values from -0.078125 to 0.078125
Outputs:
- projected: float32 [8, 5120], P(None, 'seq')
Inputs may be any that keep to these rules, and one draw needn't show every extreme that they name: `lengths`: some sequence has exactly 4096 cached tokens.
All inputs are finite; a program needn't handle non-finite values.
Results may differ from a plain program's by a relative error of at most 0.0064.
Values sent between devices are 32-bit elements; how exact they have to be, the bound alone decides.
No kernel may reach another device: no remote copies, remote signals or barrier semaphores. Data moves between devices by JAX's collectives and lax.ppermute only.
A program may use at most 64 MiB of HBM per device.

v0:
```python
import math

import jax
import jax.numpy as jnp
from jax import lax
from jax.sharding import PartitionSpec as P

THETA_BASE = 10000000.0
NEG_FILL = -1e30


def apply_rotary(values, positions):
    half_width = values.shape[-1] // 2
    frequency = jnp.exp(
        jnp.arange(half_width, dtype=jnp.float32)
        * jnp.float32(-2.0 * math.log(THETA_BASE) / values.shape[-1])
    )
    angles = positions[..., None] * frequency
    cos_part = jnp.cos(angles)
    sin_part = jnp.sin(angles)
    lower_section = values[..., :half_width]
    upper_half = values[..., half_width:]
    return jnp.concatenate(
        [
            lower_section * cos_part - upper_half * sin_part,
            upper_half * cos_part + lower_section * sin_part,
        ],
        axis=-1,
    )


def query_positions(lengths, stretch_len):
    remainder = lengths % stretch_len
    return jnp.stack(
        [
            remainder,
            remainder + stretch_len,
            jnp.zeros_like(remainder) + (stretch_len + stretch_len // 2),
        ],
        axis=-1,
    ).astype(jnp.float32)


def body(query, key_cache, value_cache, new_key, new_value, lengths, out_weight):
    seq_count = lax.axis_size("seq")
    batch, span_len, kv_local, head_width = key_cache.shape
    heads_local = query.shape[1]
    group_size = heads_local // kv_local
    stretch_len = span_len * seq_count // 8
    scaling = 1.0 / math.sqrt(head_width)
    positions = lax.axis_index("seq") * span_len + jnp.arange(span_len, dtype=jnp.int32)
    query_pos = query_positions(lengths, stretch_len)
    query_rot = apply_rotary(query.astype(jnp.float32)[:, None], query_pos[:, :, None]).astype(
        jnp.bfloat16
    )
    key_rot = apply_rotary(
        key_cache.astype(jnp.float32), (positions % stretch_len).astype(jnp.float32)[None, :, None]
    ).astype(jnp.bfloat16)
    query_by_group = query_rot.reshape(batch, 3, kv_local, group_size, head_width)
    query_stretch = lengths // stretch_len
    key_stretch = positions // stretch_len
    key_class = jnp.where(
        key_stretch[None] == query_stretch[:, None],
        0,
        jnp.where(key_stretch[None] == query_stretch[:, None] - 1, 1, 2),
    )
    block_class = key_class[:, 0][:, None, None, None]
    picked = jnp.where(
        block_class == 0,
        query_by_group[:, 0],
        jnp.where(block_class == 1, query_by_group[:, 1], query_by_group[:, 2]),
    )
    selected_branch = (
        jnp.einsum("bkgd,bpkd->bkgp", picked, key_rot, preferred_element_type=jnp.float32) * scaling
    )
    live_mask = (positions[None] < lengths[:, None])[:, None, None, :]
    masked = jnp.where(live_mask, selected_branch, NEG_FILL)
    block_max = jnp.max(masked, axis=-1)
    weights = jnp.where(live_mask, jnp.exp(masked - block_max[..., None]), 0.0)
    block_total = jnp.sum(weights, axis=-1)
    block_acc = jnp.einsum(
        "bkgp,bpkd->bkgd",
        weights.astype(jnp.bfloat16),
        value_cache,
        preferred_element_type=jnp.float32,
    )
    current_key = apply_rotary(new_key.astype(jnp.float32), query_pos[:, 0][:, None]).astype(
        jnp.bfloat16
    )
    self_score = (
        jnp.einsum(
            "lmzu,lmu->lmz", query_by_group[:, 0], current_key, preferred_element_type=jnp.float32
        )
        * scaling
    )
    fresh_values = new_value.astype(jnp.float32)[:, :, None, :]
    top_score = lax.pmax(jnp.maximum(block_max, self_score), "seq")
    factor = jnp.exp(block_max - top_score)
    summed_total, summed_acc = lax.psum(
        (block_total * factor, block_acc * factor[..., None]), "seq"
    )
    self_factor = jnp.exp(self_score - top_score)
    total = summed_total + self_factor
    accum = summed_acc + fresh_values * self_factor[..., None]
    attended = (
        (accum / total[..., None]).reshape(batch, heads_local * head_width).astype(jnp.bfloat16)
    )
    partial_value = jnp.dot(attended, out_weight, preferred_element_type=jnp.float32)
    return lax.psum(partial_value, "head")


def solution(mesh):
    placed = (
        P(None, "head", None),
        P(None, "seq", "head", None),
        P(None, "seq", "head", None),
        P(None, "head", None),
        P(None, "head", None),
        P(),
        P("head", "seq"),
    )
    return jax.shard_map(
        body, mesh=mesh, in_specs=placed, out_specs=P(None, "seq"), check_vma=False
    )
```

profile of v0, /device:TPU:0, one launch (start us, length us, event | category | flops | bytes accessed | tf_op | source)
XLA Modules:
  0.0 84.6 jit_solution(15212608247679977557)
XLA Ops:
  0.0 0.0 copy-start
  0.0 4.1 %copy_convert_fusion = f32[8,512,2,128]{3,1,2,0:T(8,128)} fusion(bf16[8,512,2,128]{3,2,1,0:T(2,128)(2,1)} %param.8), kind=kLoop, calls=%fused_computation.8 | loop fusion | flops 1048576 | bytes 6291456 | tf_op jit(solution)/shard_map/convert_element_type | solution.py:57
  4.1 1.0 %multiply_cosine_fusion = (f32[512,64]{1,0:T(8,128)S(1)}, f32[512,64]{1,0:T(8,128)S(1)}) fusion(f32[64]{0:T(128)S(1)} %multiply_exponential_fusion, f32[512]{0:T(512)S(1)} %get-tuple-element.35), kind=kLoop, calls=%fused_computation.13 | loop fusion | flops 32768 | bytes 264448 | tf_op jit(solution)/shard_map/cos | solution.py:19
  5.1 0.0 copy-start.4
  5.1 0.0 copy-start.1
  5.1 4.9 %subtract_convert_fusion = (bf16[8,512,2,64]{3,1,2,0:T(8,128)(2,1)S(1)}, bf16[8,512,2,64]{3,1,2,0:T(8,128)(2,1)S(1)}) fusion(f32[8,512,2,128]{3,1,2,0:T(8,128)} %copy_convert_fusion, f32[512,64]{1,0:T(8,128)S(1)} %get-tuple-element.27, f32[512,64]{1,0:T(8,128)S(1)} %get-tuple-element.26), kind=kLoop, calls=%fused_computation.1 | loop fusion | flops 4194304 | bytes 6553600 | tf_op jit(solution)/shard_map/convert.3
  10.1 0.0 copy-done.4
  10.1 0.1 pad.8.clone
  10.2 0.1 add_convert_fusion.3
  10.3 0.1 multiply_cosine_fusion.1
  10.4 0.0 copy-done.1
  10.4 0.1 fusion.46
  10.5 0.1 add_convert_fusion.1
  10.6 0.5 slice.45
  11.1 0.7 compare_bitcast_fusion.1
  11.8 0.1 broadcast_compare_fusion
  11.9 0.0 copy-start.2
  11.9 1.4 %fusion.47 = (f32[8,2,5]{2,1,0:T(2,128)S(1)}, f32[8,2,5,512]{3,2,1,0:T(8,128)S(1)}) fusion(bf16[8,512,2,64]{3,1,2,0:T(8,128)(2,1)S(1)} %get-tuple-element.17, bf16[8,512,2,64]{3,1,2,0:T(8,128)(2,1)S(1)} %get-tuple-element.16, bf16[8,3,2,5,64]{4,3,2,0,1:T(8,128)(2,1)S(1)} %get-tuple-element.19, bf16[8,3,2,5,64]{4,3,2,0,1:T(8,128)(2,1)S(1)} %get-tuple-element.18, ...), kind=kOutput, calls=%fused_computation.83 | convolution fusion | flops 14946224 | bytes 2326864 | tf_op jit(solution)/shard_map/bkgd,bpkd->bkgp/dot_general | solution.py:74
  13.3 0.0 copy-start.3
  13.3 0.2 fusion.15
  13.5 0.0 copy-done.2
  13.5 0.1 multiply_cosine_fusion.2
  13.6 0.1 subtract_convert_fusion.2
  13.7 0.1 maximum_bitcast_fusion
  13.8 0.2 fusion.33
  14.0 23.4 %pmax.7 = f32[8,2,5]{2,1,0:T(2,128)S(1)} all-reduce(f32[8,2,5]{2,1,0:T(2,128)S(1)} %multiply_maximum_fusion), channel_id=1, replica_groups=mesh['seq'=8,'head'=4] {'seq'}, use_global_device_ids=true, to_apply=%region_1.2 | all-reduce | flops 80 | bytes 640 | tf_op jit(solution)/shard_map/pmax | solution.py:97
  37.5 0.0 copy-done
  37.5 0.4 fusion.12
  37.9 33.9 %all-reduce = (f32[8,2,5,128]{3,2,1,0:T(8,128)S(1)}, f32[8,2,5]{2,1,0:T(2,128)S(1)}) all-reduce(f32[8,2,5,128]{3,2,1,0:T(8,128)S(1)} %fusion.12, f32[8,2,5]{2,1,0:T(2,128)S(1)} %bitcast.58), channel_id=1, replica_groups=mesh['seq'=8,'head'=4] {'seq'}, use_global_device_ids=true, to_apply=%region_2.3 | all-reduce | flops 10320 | bytes 82560 | tf_op jit(solution)/shard_map/psum | solution.py:99
  71.9 0.0 copy-done.3
  71.9 0.1 divide_convert_fusion
  72.0 1.8 %fusion.48 = f32[8,640]{1,0:T(8,128)S(1)} fusion(bf16[8,1280]{1,0:T(8,128)(2,1)S(1)} %convert_element_type.44, bf16[1280,640]{1,0:T(8,128)(2,1)} %param.13), kind=kOutput, calls=%fused_computation.84 | convolution fusion | flops 13107200 | bytes 1679360 | tf_op jit(solution)/shard_map/dot_general | solution.py:108
  73.8 10.9 %psum.23 = f32[8,640]{1,0:T(8,128)} all-reduce(f32[8,640]{1,0:T(8,128)S(1)} %fusion.48), channel_id=1, replica_groups=mesh['seq'=8,'head'=4] {'head'}, use_global_device_ids=true, to_apply=%region_5.6 | all-reduce | flops 5120 | bytes 40960 | tf_op jit(solution)/shard_map/psum | solution.py:109
  (16 shorter events, 0.2 us)
Async XLA Ops:
  0.0 37.5 %copy-start = (bf16[8,512,2,128]{3,2,1,0:T(2,128)(2,1)S(1)}, bf16[8,512,2,128]{3,2,1,0:T(2,128)(2,1)}, u32[]{:S(2)}) copy-start(bf16[8,512,2,128]{3,2,1,0:T(2,128)(2,1)} %param.9) | copy-start | bytes 6291460
  5.1 5.0 %copy-start.4 = (s32[8]{0:T(128)S(1)}, s32[8]{0:T(128)}, u32[]{:S(2)}) copy-start(s32[8]{0:T(128)} %param.12) | copy-start | bytes 100
  5.1 5.3 %copy-start.1 = (bf16[8,10,128]{2,0,1:T(8,128)(2,1)S(1)}, bf16[8,10,128]{2,0,1:T(8,128)(2,1)}, u32[]{:S(2)}) copy-start(bf16[8,10,128]{2,0,1:T(8,128)(2,1)} %param.7) | copy-start | bytes 61444
  11.9 1.6 %copy-start.2 = (bf16[8,2,128]{2,1,0:T(2,128)(2,1)S(1)}, bf16[8,2,128]{2,1,0:T(2,128)(2,1)}, u32[]{:S(2)}) copy-start(bf16[8,2,128]{2,1,0:T(2,128)(2,1)} %param.10) | copy-start | bytes 12292
  13.3 58.6 %copy-start.3 = (bf16[8,2,128]{2,1,0:T(2,128)(2,1)S(1)}, bf16[8,2,128]{2,1,0:T(2,128)(2,1)}, u32[]{:S(2)}) copy-start(bf16[8,2,128]{2,1,0:T(2,128)(2,1)} %param.11) | copy-start | bytes 12292
where the time goes:
time: 84.9 us; the launch traced here: 84.6 us
  blocking collectives  68.2 us (80%)
  other arithmetic  11.7 us (14%)
  matrix products  3.78 us (4%)
    psum x1, blocking collectives, body(): lax.psum((block_total * factor, block_acc * factor[..., None]), 'seq')  33.9 us
    pmax x1, blocking collectives, body(): top_score = lax.pmax(jnp.maximum(block_max, self_score), 'seq')  23.4 us
    psum x1, blocking collectives, body(): return lax.psum(partial_value, 'head')  10.9 us
    another operation x3, other arithmetic  5.08 us
    convert_element_type x1, other arithmetic, body(): key_cache.astype(jnp.float32)  4.08 us
    dot_general x1, matrix products, body(): jnp.dot(attended, out_weight, preferred_element_type=jnp.float32)  1.75 us

commit v1 on v0

v1 whole, which is shorter than its diff:
```python
import functools
import math

import jax
import jax.numpy as jnp
from jax import lax
from jax.experimental import pallas as pl
from jax.experimental.pallas import tpu as pltpu
from jax.sharding import PartitionSpec as P

THETA_BASE = 10000000.0
NEG_FILL = -1e30
SLOT = 16
F32 = jnp.float32
BF16 = jnp.bfloat16


def frequencies(shape):
    width = shape[-1]
    half = width // 2
    lane = lax.broadcasted_iota(jnp.int32, shape, len(shape) - 1)
    index = jnp.where(lane < half, lane, lane - half).astype(F32)
    return jnp.exp(index * F32(-2.0 * math.log(THETA_BASE) / width))


def half_sign(shape):
    lane = lax.broadcasted_iota(jnp.int32, shape, len(shape) - 1)
    return jnp.where(lane < shape[-1] // 2, F32(-1.0), F32(1.0))


def rotate(values, cos_part, signed_sin):
    return values * cos_part + pltpu.roll(values, values.shape[-1] // 2, 1) * signed_sin


def rows_of_scalars(scalars, shape):
    row = lax.broadcasted_iota(jnp.int32, shape, 0)
    out = jnp.zeros(shape, scalars[0].dtype)
    for i, s in enumerate(scalars):
        out = jnp.where(row == i, s, out)
    return out


def attention_kernel(
    lens_ref, place_ref, q_ref, nk_ref, nv_ref, k_hbm, v_hbm,
    out_ref,
    kbuf, vbuf, kcat, qbd, qin, scores, cos_tab, sin_tab, coarse_c, coarse_s, ksem, vsem,
    *, stretch, kv, chunks,
):
    batch, rows, width = kbuf.shape
    heads = q_ref.shape[1]
    group = heads // kv
    lanes = batch * SLOT
    span = rows // kv
    chunk = rows // chunks
    pairs = batch // 2

    def kcopy(c):
        return pltpu.make_async_copy(
            k_hbm.at[:, pl.ds(c * chunk, chunk), :], kbuf.at[:, pl.ds(c * chunk, chunk), :], ksem.at[c]
        )

    def vcopy(c):
        return pltpu.make_async_copy(
            v_hbm.at[pl.ds(2 * c, 2)], vbuf.at[pl.ds(2 * c, 2)], vsem.at[c]
        )

    for c in range(chunks):
        kcopy(c).start()
    for c in range(pairs):
        vcopy(c).start()

    place = place_ref[0]
    base = place * span
    key_stretch = base // stretch

    freq8 = frequencies((8, width))
    sign8 = half_sign((8, width))
    row8 = lax.broadcasted_iota(jnp.int32, (8, width), 0)
    per8 = 8 // kv
    fine = (row8 // kv).astype(F32) * freq8
    fine_c, fine_s = jnp.cos(fine), jnp.sin(fine) * sign8
    n8 = rows // 8
    start = (base % stretch).astype(F32)
    coarse_pos = start + (lax.broadcasted_iota(jnp.int32, (n8, width), 0) * per8).astype(F32)
    coarse = coarse_pos * frequencies((n8, width))
    coarse_c[...] = jnp.cos(coarse)
    coarse_s[...] = jnp.sin(coarse) * half_sign((n8, width))

    def table(i, carry):
        cc = coarse_c[pl.ds(i, 1), :]
        cs = coarse_s[pl.ds(i, 1), :]
        cos_tab[pl.ds(pl.multiple_of(i * 8, 8), 8), :] = cc * fine_c - cs * fine_s
        sin_tab[pl.ds(pl.multiple_of(i * 8, 8), 8), :] = cs * fine_c + cc * fine_s
        return carry

    lax.fori_loop(0, n8, table, 0, unroll=8)

    picked, intra, limit = [], [], []
    for b in range(batch):
        p = lens_ref[b]
        qc = p // stretch
        r = p - qc * stretch
        intra.append(r.astype(F32))
        inter = stretch + stretch // 2
        picked.append(
            jnp.where(key_stretch == qc, r, jnp.where(key_stretch == qc - 1, r + stretch, inter)).astype(F32)
        )
        limit.append((p - base) * kv)
    angle_p = rows_of_scalars(picked, (8, width)) * freq8
    angle_r = rows_of_scalars(intra, (8, width)) * freq8
    cp, sp = jnp.cos(angle_p), jnp.sin(angle_p) * sign8
    cr, sr = jnp.cos(angle_r), jnp.sin(angle_r) * sign8

    qbd[...] = jnp.zeros_like(qbd)
    qin[...] = jnp.zeros_like(qin)
    for b in range(batch):
        q = q_ref[b].astype(F32)
        qbd[b * SLOT : b * SLOT + heads, b * width : (b + 1) * width] = rotate(
            q, cp[b : b + 1], sp[b : b + 1]
        ).astype(BF16)
        qin[b * SLOT : b * SLOT + heads, :] = rotate(q, cr[b : b + 1], sr[b : b + 1]).astype(BF16)

    scaling = F32(1.0 / math.sqrt(width))

    own_rows = batch * kv
    knew = jnp.concatenate(
        [rotate(nk_ref[b].astype(F32), cr[b : b + 1], sr[b : b + 1]) for b in range(batch)], axis=0
    ).astype(BF16)
    own_all = lax.dot_general(
        knew, qin[...], (((1,), (1,)), ((), ())), preferred_element_type=F32
    ) * scaling
    own_row = lax.broadcasted_iota(jnp.int32, (own_rows, lanes), 0)
    own_lane = lax.broadcasted_iota(jnp.int32, (own_rows, lanes), 1)
    own_kv = jnp.minimum((own_lane % SLOT) // group, kv - 1)
    own_mask = (own_row // kv == own_lane // SLOT) & (own_row % kv == own_kv)
    own = jnp.sum(jnp.where(own_mask, own_all, 0.0), axis=0, keepdims=True)
    first = place == 0
    own = jnp.where(first, own, F32(NEG_FILL))

    lane1 = lax.broadcasted_iota(jnp.int32, (1, lanes), 1)
    bound = jnp.zeros((1, lanes), jnp.int32)
    for b in range(batch):
        bound = jnp.where(lane1 // SLOT == b, limit[b], bound)
    lane_kv = jnp.minimum((lane1 % SLOT) // group, kv - 1)
    row_c = lax.broadcasted_iota(jnp.int32, (chunk, lanes), 0)
    fits = row_c % kv == lane_kv

    top = own
    for c in range(chunks):
        kcopy(c).wait()

        def turn(i, carry):
            at = pl.multiple_of(i * 64, 64)
            cc = cos_tab[pl.ds(c * chunk + at, 64), :]
            ss = sin_tab[pl.ds(c * chunk + at, 64), :]
            for b in range(batch):
                k = kbuf[b, pl.ds(c * chunk + at, 64), :].astype(F32)
                kcat[pl.ds(at, 64), b * width : (b + 1) * width] = rotate(k, cc, ss).astype(BF16)
            return carry

        lax.fori_loop(0, chunk // 64, turn, 0)
        s = lax.dot_general(
            kcat[...], qbd[...], (((1,), (1,)), ((), ())), preferred_element_type=F32
        ) * scaling
        s = jnp.where(fits & (row_c + c * chunk < bound), s, F32(NEG_FILL))
        scores[c * chunk : (c + 1) * chunk, :] = s
        top = jnp.maximum(top, jnp.max(s, axis=0, keepdims=True))

    own_w = jnp.where(first, jnp.exp(own - top), 0.0)
    total = own_w
    parts = []
    for c in range(chunks):
        s = scores[c * chunk : (c + 1) * chunk, :]
        w = jnp.where(s > F32(0.5 * NEG_FILL), jnp.exp(s - top), 0.0)
        total = total + jnp.sum(w, axis=0, keepdims=True)
        parts.append(jnp.transpose(w.astype(BF16)))
    wt = jnp.concatenate(parts, axis=1)

    own_wt = jnp.transpose(jnp.where(own_mask, own_w, 0.0))
    nv = jnp.concatenate([nv_ref[b].astype(F32) for b in range(batch)], axis=0)
    own_acc = lax.dot_general(
        own_wt, nv, (((1,), (0,)), ((), ())), preferred_element_type=F32,
        precision=lax.Precision.HIGHEST,
    )

    for c in range(pairs):
        vcopy(c).wait()
        v = jnp.concatenate([vbuf[2 * c], vbuf[2 * c + 1]], axis=1)
        acc = jnp.dot(wt[2 * c * SLOT : (2 * c + 2) * SLOT, :], v, preferred_element_type=F32)
        for j in range(2):
            b = 2 * c + j
            part = acc[j * SLOT : (j + 1) * SLOT, j * width : (j + 1) * width]
            part = part + own_acc[b * SLOT : (b + 1) * SLOT, :]
            out_ref[pl.ds(b, heads, stride=batch), :] = part[:heads]

    lane_b = lax.broadcasted_iota(jnp.int32, (batch, lanes), 1)
    row_b = lax.broadcasted_iota(jnp.int32, (batch, lanes), 0)
    stats = jnp.zeros((batch, lanes), F32)
    for b in range(batch):
        m_b = pltpu.roll(top, (lanes - b * SLOT) % lanes, 1) if b else top
        l_b = pltpu.roll(total, (lanes + SLOT - b * SLOT) % lanes, 1) if b != 1 else total
        stats = jnp.where(row_b == b, jnp.where(lane_b < SLOT, m_b, l_b), stats)
    out_ref[heads * batch :, :] = stats


def merge(a_ref, b_ref, heads, batch):
    a = a_ref[heads * batch :, :]
    b = b_ref[heads * batch :, :]
    top = jnp.maximum(a, b)
    fa, fb = jnp.exp(a - top), jnp.exp(b - top)
    total = a * pltpu.roll(fa, SLOT, 1) + b * pltpu.roll(fb, SLOT, 1)
    lane = lax.broadcasted_iota(jnp.int32, top.shape, 1)
    stats = jnp.where(lane < SLOT, top, total)
    sums = []
    for h in range(heads):
        rows = slice(h * batch, (h + 1) * batch)
        sums.append(a_ref[rows, :] * fa[:, h : h + 1] + b_ref[rows, :] * fb[:, h : h + 1])
    return sums, stats


def merge_kernel(a_ref, b_ref, out_ref, *, heads, batch):
    sums, stats = merge(a_ref, b_ref, heads, batch)
    for h in range(heads):
        out_ref[h * batch : (h + 1) * batch, :] = sums[h]
    out_ref[heads * batch :, :] = stats


def project_kernel(a_ref, b_ref, w_ref, out_ref, *, heads, batch):
    sums, stats = merge(a_ref, b_ref, heads, batch)
    attended = jnp.concatenate(
        [(sums[h] / stats[:, SLOT + h : SLOT + h + 1]).astype(BF16) for h in range(heads)], axis=1
    )
    out_ref[...] = jnp.dot(attended, w_ref[...], preferred_element_type=F32)


def in_vmem(count):
    return [pl.BlockSpec(memory_space=pltpu.VMEM)] * count


def butterfly(values, axis):
    size = lax.axis_size(axis)
    assert size & (size - 1) == 0
    return [[(i, i ^ (1 << k)) for i in range(size)] for k in range(size.bit_length() - 1)]


def body(query, key_cache, value_cache, new_key, new_value, lengths, out_weight):
    seq_count = lax.axis_size("seq")
    batch, span, kv, width = key_cache.shape
    heads = query.shape[1]
    stretch = span * seq_count // 8
    rows = span * kv
    chunks = 4
    lanes = batch * SLOT
    place = lax.axis_index("seq").astype(jnp.int32).reshape(1)
    packed_rows = heads * batch + batch
    any_space = pl.BlockSpec(memory_space=pl.ANY)
    smem = pl.BlockSpec(memory_space=pltpu.SMEM)
    packed = pl.pallas_call(
        functools.partial(attention_kernel, stretch=stretch, kv=kv, chunks=chunks),
        out_shape=jax.ShapeDtypeStruct((packed_rows, width), F32),
        in_specs=[smem, smem] + in_vmem(3) + [any_space, any_space],
        out_specs=pl.BlockSpec(memory_space=pltpu.VMEM),
        scratch_shapes=[
            pltpu.VMEM((batch, rows, width), BF16),
            pltpu.VMEM((batch, rows, width), BF16),
            pltpu.VMEM((rows // chunks, batch * width), BF16),
            pltpu.VMEM((lanes, batch * width), BF16),
            pltpu.VMEM((lanes, width), BF16),
            pltpu.VMEM((rows, lanes), F32),
            pltpu.VMEM((rows, width), F32),
            pltpu.VMEM((rows, width), F32),
            pltpu.VMEM((rows // 8, width), F32),
            pltpu.VMEM((rows // 8, width), F32),
            pltpu.SemaphoreType.DMA((chunks,)),
            pltpu.SemaphoreType.DMA((batch // 2,)),
        ],
        name="attention",
    )(
        lengths, place, query, new_key, new_value,
        key_cache.reshape(batch, rows, width), value_cache.reshape(batch, rows, width),
    )
    steps = butterfly(packed, "seq")
    for pairs in steps[:-1]:
        other = lax.ppermute(packed, "seq", pairs)
        packed = pl.pallas_call(
            functools.partial(merge_kernel, heads=heads, batch=batch),
            out_shape=jax.ShapeDtypeStruct(packed.shape, F32),
            in_specs=in_vmem(2),
            out_specs=pl.BlockSpec(memory_space=pltpu.VMEM),
            name="merge",
        )(packed, other)
    other = lax.ppermute(packed, "seq", steps[-1])
    partial_out = pl.pallas_call(
        functools.partial(project_kernel, heads=heads, batch=batch),
        out_shape=jax.ShapeDtypeStruct((batch, out_weight.shape[1]), F32),
        in_specs=in_vmem(3),
        out_specs=pl.BlockSpec(memory_space=pltpu.VMEM),
        name="project",
    )(packed, other, out_weight)
    for pairs in reversed(butterfly(partial_out, "head")):
        partial_out = partial_out + lax.ppermute(partial_out, "head", pairs)
    return partial_out


def solution(mesh):
    placed = (
        P(None, "head", None),
        P(None, "seq", "head", None),
        P(None, "seq", "head", None),
        P(None, "head", None),
        P(None, "head", None),
        P(),
        P("head", "seq"),
    )
    return jax.shard_map(
        body, mesh=mesh, in_specs=placed, out_specs=P(None, "seq"), check_vma=False
    )
```

time: 84.9 us -> 37.9 us (0.45)
  blocking collectives: 68.2 us -> 0 us
  Pallas kernels: 0 us -> 12.9 us
  other arithmetic: 11.7 us -> 1.34 us
  waiting for transfers between devices: 0 us -> 10.1 us
  starting transfers between devices: 0 us -> 10 us
  matrix products: 3.78 us -> 0 us
  local copies, waits for them, and re-layouts: 0.76 us -> 3.19 us
    psum x2 -> x0, blocking collectives: 44.8 us -> none  [the longest x1 33.9 us: body(): lax.psum((block_total * factor, block_acc * factor[..., None]), 'seq')]
    pmax x1 -> x0, blocking collectives: 23.4 us -> none  [body(): top_score = lax.pmax(jnp.maximum(block_max, self_score), 'seq')]
    pallas_call x0 -> x4, Pallas kernels: none -> 12.9 us  [the longest x1 7.28 us: body(): pl.pallas_call(functools.partial(attention_kernel, stretch=stretch, kv=kv...]
    ppermute x0 -> x5, waiting for transfers between devices: none -> 10.1 us  [the longest x2 4.47 us: body(): other = lax.ppermute(packed, 'seq', pairs)]
    ppermute x0 -> x5, starting transfers between devices: none -> 10 us  [the longest x2 5.14 us: body(): other = lax.ppermute(packed, 'seq', pairs)]
    another operation x4 -> x0, other arithmetic: 5.09 us -> none
    convert_element_type x5 -> x0, other arithmetic: 4.26 us -> none  [the longest x1 4.08 us: body(): key_cache.astype(jnp.float32)]
    dot_general x4 -> x0, matrix products: 3.78 us -> none  [the longest x1 1.75 us: body(): jnp.dot(attended, out_weight, preferred_element_type=jnp.float32)]
  transfers between devices with their start and end apart: 0 -> 5, of which waited for: 0 -> 5; matrix products, arithmetic and copies ran while one was open for 0% -> 0% of each run, Pallas kernels for 0% -> 0%
where the time goes in v1:
time: 37.9 us; the launch traced here: 37.5 us
  Pallas kernels  12.9 us (34%)
  waiting for transfers between devices  10.1 us (27%)
  starting transfers between devices  10 us (26%)
  local copies, waits for them, and re-layouts  3.19 us (8%)
  other arithmetic  1.34 us (4%)
    pallas_call x1, Pallas kernels, body(): pl.pallas_call(functools.partial(attention_kernel, stretch=stretch, kv=kv...  7.28 us
    ppermute x2, starting transfers between devices, body(): other = lax.ppermute(packed, 'seq', pairs)  5.14 us
    ppermute x2, waiting for transfers between devices, body(): other = lax.ppermute(packed, 'seq', pairs)  4.47 us
    ppermute x2, waiting for transfers between devices, body(): partial_out = partial_out + lax.ppermute(partial_out, 'head', pairs)  3.35 us
    unnamed x7, local copies, waits for them, and re-layouts  3.19 us
    pallas_call x2, Pallas kernels, body(): pl.pallas_call(functools.partial(merge_kernel, heads=heads, batch=batch),...  3.07 us
    ppermute x1, starting transfers between devices, body(): other = lax.ppermute(packed, 'seq', steps[-1])  3.04 us
    pallas_call x1, Pallas kernels, body(): pl.pallas_call(functools.partial(project_kernel, heads=heads, batch=batch...  2.55 us
  transfers between devices with their start and end apart: 5, of which 5 were waited for; matrix products, arithmetic and copies ran while one was open for 0% of the time, Pallas kernels for 0%

profile of v1, /device:TPU:0, one launch (start us, length us, event | category | flops | bytes accessed | tf_op | source)
XLA Modules:
  0.0 37.5 jit_solution(15755169922792507355)
XLA Ops:
  0.0 1.3 %copy.8.q_ref = bf16[8,10,128]{2,1,0:T(8,128)(2,1)} copy(bf16[8,10,128]{2,0,1:T(8,128)(2,1)} %param.7) | data formatting | bytes 40960 | tf_op args[0]
  1.3 7.3 %attention.1.a_ref = f32[88,128]{1,0:T(8,128)} custom-call(s32[8]{0:T(128)} %lens_ref.1, s32[1]{0:T(128)} %bitcast.place_ref, bf16[8,10,128]{2,1,0:T(8,128)(2,1)} %copy.8.q_ref, bf16[8,2,128]{2,1,0:T(2,128)(2,1)} %nk_ref.1, bf16[8,2,128]{2,1,0:T(2,128)(2,1)} %nv_ref.1, bf16[8,1024,128]{2,1,0:T(8,128)(2,1)} %bitcast.3, bf16[8,1024,128]{2,1,0:T(8,128)(2,1)} %bitcast.4), custom_call_target="tpu_custom_call" | custom-call | tf_op jit(solution)/shard_map/attention/pallas_call | solution.py:258
  8.6 3.1 %collective-permute-start = (f32[88,128]{1,0:T(8,128)}, f32[88,128]{1,0:T(8,128)S(1)}, u32[]{:S(2)}, u32[]{:S(2)}) collective-permute-start(f32[88,128]{1,0:T(8,128)} %attention.1.a_ref), channel_id=1, source_target_pairs={{0,4},{4,0},{8,12},{12,8},{16,20},{20,16},{24,28},{28,24},{1,5},{5... | collective-permute-start | bytes 135176 | tf_op jit(solution)/shard_map/ppermute | solution.py:284
  11.7 2.2 %collective-permute-done.b_ref = f32[88,128]{1,0:T(8,128)S(1)} collective-permute-done((f32[88,128]{1,0:T(8,128)}, f32[88,128]{1,0:T(8,128)S(1)}, u32[]{:S(2)}, u32[]{:S(2)}) %collective-permute-start) | collective-permute-done | bytes 45088 | tf_op jit(solution)/shard_map/ppermute | solution.py:284
  13.9 0.0 copy-start.1
  13.9 0.6 %copy-done.1 = f32[88,128]{1,0:T(8,128)} copy-done((f32[88,128]{1,0:T(8,128)}, f32[88,128]{1,0:T(8,128)S(1)}, u32[]{:S(2)}) %copy-start.1) | copy-done | bytes 45080
  14.5 1.5 %merge.2.a_ref = f32[88,128]{1,0:T(8,128)} custom-call(f32[88,128]{1,0:T(8,128)} %attention.1.a_ref, f32[88,128]{1,0:T(8,128)} %copy-done.1), custom_call_target="tpu_custom_call" | custom-call | tf_op jit(solution)/shard_map/merge/pallas_call | solution.py:285
  16.1 2.1 %collective-permute-start.1 = (f32[88,128]{1,0:T(8,128)}, f32[88,128]{1,0:T(8,128)S(1)}, u32[]{:S(2)}, u32[]{:S(2)}) collective-permute-start(f32[88,128]{1,0:T(8,128)} %merge.2.a_ref), channel_id=1, source_target_pairs={{0,8},{4,12},{8,0},{12,4},{16,24},{20,28},{24,16},{28,20},{1,9},{5... | collective-permute-start | bytes 135176 | tf_op jit(solution)/shard_map/ppermute | solution.py:284
  18.1 2.2 %collective-permute-done.1.b_ref = f32[88,128]{1,0:T(8,128)S(1)} collective-permute-done((f32[88,128]{1,0:T(8,128)}, f32[88,128]{1,0:T(8,128)S(1)}, u32[]{:S(2)}, u32[]{:S(2)}) %collective-permute-start.1) | collective-permute-done | bytes 45088 | tf_op jit(solution)/shard_map/ppermute | solution.py:284
  20.4 0.0 copy-start.2
  20.4 0.6 %copy-done.2 = f32[88,128]{1,0:T(8,128)} copy-done((f32[88,128]{1,0:T(8,128)}, f32[88,128]{1,0:T(8,128)S(1)}, u32[]{:S(2)}) %copy-start.2) | copy-done | bytes 45080
  21.0 1.5 %merge.3.a_ref = f32[88,128]{1,0:T(8,128)} custom-call(f32[88,128]{1,0:T(8,128)} %merge.2.a_ref, f32[88,128]{1,0:T(8,128)} %copy-done.2), custom_call_target="tpu_custom_call" | custom-call | tf_op jit(solution)/shard_map/merge/pallas_call | solution.py:285
  22.5 3.0 %collective-permute-start.2 = (f32[88,128]{1,0:T(8,128)}, f32[88,128]{1,0:T(8,128)S(1)}, u32[]{:S(2)}, u32[]{:S(2)}) collective-permute-start(f32[88,128]{1,0:T(8,128)} %merge.3.a_ref), channel_id=1, source_target_pairs={{0,16},{4,20},{8,24},{12,28},{16,0},{20,4},{24,8},{28,12},{1,17},{... | collective-permute-start | bytes 135176 | tf_op jit(solution)/shard_map/ppermute | solution.py:292
  25.6 2.2 %collective-permute-done.2.b_ref = f32[88,128]{1,0:T(8,128)S(1)} collective-permute-done((f32[88,128]{1,0:T(8,128)}, f32[88,128]{1,0:T(8,128)S(1)}, u32[]{:S(2)}, u32[]{:S(2)}) %collective-permute-start.2) | collective-permute-done | bytes 45088 | tf_op jit(solution)/shard_map/ppermute | solution.py:292
  27.8 0.0 copy-start
  27.8 0.6 %copy-done = f32[88,128]{1,0:T(8,128)} copy-done((f32[88,128]{1,0:T(8,128)}, f32[88,128]{1,0:T(8,128)S(1)}, u32[]{:S(2)}) %copy-start) | copy-done | bytes 45080
  28.4 2.6 %project.1 = f32[8,640]{1,0:T(8,128)} custom-call(f32[88,128]{1,0:T(8,128)} %merge.3.a_ref, f32[88,128]{1,0:T(8,128)} %copy-done, bf16[1280,640]{1,0:T(8,128)(2,1)} %w_ref.1), custom_call_target="tpu_custom_call" | custom-call | tf_op jit(solution)/shard_map/project/pallas_call | solution.py:293
  31.0 1.8 %collective-permute-start.3 = (f32[8,640]{1,0:T(8,128)}, f32[8,640]{1,0:T(8,128)S(1)}, u32[]{:S(2)}, u32[]{:S(2)}) collective-permute-start(f32[8,640]{1,0:T(8,128)} %project.1), channel_id=1, source_target_pairs={{0,2},{1,3},{2,0},{3,1},{4,6},{5,7},{6,4},{7,5},{8,10},{9,11},{10,... | collective-permute-start | bytes 61448 | tf_op jit(solution)/shard_map/ppermute | solution.py:301
  32.8 2.2 %collective-permute-done.3 = f32[8,640]{1,0:T(8,128)S(1)} collective-permute-done((f32[8,640]{1,0:T(8,128)}, f32[8,640]{1,0:T(8,128)S(1)}, u32[]{:S(2)}, u32[]{:S(2)}) %collective-permute-start.3) | collective-permute-done | bytes 20512 | tf_op jit(solution)/shard_map/ppermute | solution.py:301
  35.0 0.7 %add.6 = f32[8,640]{1,0:T(8,128)S(1)} add(f32[8,640]{1,0:T(8,128)} %project.1, f32[8,640]{1,0:T(8,128)S(1)} %collective-permute-done.3) | non-fusion elementwise | flops 5120 | bytes 61440 | tf_op jit(solution)/shard_map/add | solution.py:301
  35.7 0.0 collective-permute-start.4
  35.7 1.2 %collective-permute-done.4 = f32[8,640]{1,0:T(8,128)S(1)} collective-permute-done((f32[8,640]{1,0:T(8,128)S(1)}, f32[8,640]{1,0:T(8,128)S(1)}, u32[]{:S(2)}, u32[]{:S(2)}) %collective-permute-start.4) | collective-permute-done | bytes 20512 | tf_op jit(solution)/shard_map/ppermute | solution.py:301
  36.9 0.6 %add.7 = f32[8,640]{1,0:T(8,128)} add(f32[8,640]{1,0:T(8,128)S(1)} %add.6, f32[8,640]{1,0:T(8,128)S(1)} %collective-permute-done.4) | non-fusion elementwise | flops 5120 | bytes 61440 | tf_op jit(solution)/shard_map/add | solution.py:301
Async XLA Ops:
  8.6 5.3 %collective-permute-start = (f32[88,128]{1,0:T(8,128)}, f32[88,128]{1,0:T(8,128)S(1)}, u32[]{:S(2)}, u32[]{:S(2)}) collective-permute-start(f32[88,128]{1,0:T(8,128)} %attention.1.a_ref), channel_id=1, source_target_pairs={{0,4},{4,0},{8,12},{12,8},{16,20},{20,16},{24,28},{28,24},{1,5},{5... | collective-permute-start | bytes 135176 | tf_op jit(solution)/shard_map/ppermute | solution.py:284
  13.9 0.6 %copy-start.1 = (f32[88,128]{1,0:T(8,128)}, f32[88,128]{1,0:T(8,128)S(1)}, u32[]{:S(2)}) copy-start(f32[88,128]{1,0:T(8,128)S(1)} %collective-permute-done.b_ref) | copy-start | bytes 135172
  16.1 4.3 %collective-permute-start.1 = (f32[88,128]{1,0:T(8,128)}, f32[88,128]{1,0:T(8,128)S(1)}, u32[]{:S(2)}, u32[]{:S(2)}) collective-permute-start(f32[88,128]{1,0:T(8,128)} %merge.2.a_ref), channel_id=1, source_target_pairs={{0,8},{4,12},{8,0},{12,4},{16,24},{20,28},{24,16},{28,20},{1,9},{5... | collective-permute-start | bytes 135176 | tf_op jit(solution)/shard_map/ppermute | solution.py:284
  20.4 0.6 %copy-start.2 = (f32[88,128]{1,0:T(8,128)}, f32[88,128]{1,0:T(8,128)S(1)}, u32[]{:S(2)}) copy-start(f32[88,128]{1,0:T(8,128)S(1)} %collective-permute-done.1.b_ref) | copy-start | bytes 135172
  22.5 5.3 %collective-permute-start.2 = (f32[88,128]{1,0:T(8,128)}, f32[88,128]{1,0:T(8,128)S(1)}, u32[]{:S(2)}, u32[]{:S(2)}) collective-permute-start(f32[88,128]{1,0:T(8,128)} %merge.3.a_ref), channel_id=1, source_target_pairs={{0,16},{4,20},{8,24},{12,28},{16,0},{20,4},{24,8},{28,12},{1,17},{... | collective-permute-start | bytes 135176 | tf_op jit(solution)/shard_map/ppermute | solution.py:292
  27.8 0.6 %copy-start = (f32[88,128]{1,0:T(8,128)}, f32[88,128]{1,0:T(8,128)S(1)}, u32[]{:S(2)}) copy-start(f32[88,128]{1,0:T(8,128)S(1)} %collective-permute-done.2.b_ref) | copy-start | bytes 135172
  31.0 4.0 %collective-permute-start.3 = (f32[8,640]{1,0:T(8,128)}, f32[8,640]{1,0:T(8,128)S(1)}, u32[]{:S(2)}, u32[]{:S(2)}) collective-permute-start(f32[8,640]{1,0:T(8,128)} %project.1), channel_id=1, source_target_pairs={{0,2},{1,3},{2,0},{3,1},{4,6},{5,7},{6,4},{7,5},{8,10},{9,11},{10,... | collective-permute-start | bytes 61448 | tf_op jit(solution)/shard_map/ppermute | solution.py:301
  35.7 1.2 %collective-permute-start.4 = (f32[8,640]{1,0:T(8,128)S(1)}, f32[8,640]{1,0:T(8,128)S(1)}, u32[]{:S(2)}, u32[]{:S(2)}) collective-permute-start(f32[8,640]{1,0:T(8,128)S(1)} %add.6), channel_id=1, source_target_pairs={{0,1},{1,0},{2,3},{3,2},{4,5},{5,4},{6,7},{7,6},{8,9},{9,8},{10,11... | collective-permute-start | bytes 61448 | tf_op jit(solution)/shard_map/ppermute | solution.py:301

commit v2 on v1

--- a/solution.py
+++ b/solution.py
@@ -7,6 +7,7 @@
 from jax.experimental import pallas as pl
 from jax.experimental.pallas import tpu as pltpu
 from jax.sharding import PartitionSpec as P
+import numpy as np
 
 THETA_BASE = 10000000.0
 NEG_FILL = -1e30
@@ -41,63 +42,67 @@
 
 
 def attention_kernel(
-    lens_ref, place_ref, q_ref, nk_ref, nv_ref, k_hbm, v_hbm,
+    tab_hbm, lens_hbm, q_hbm, nk_hbm, nv_hbm, k_hbm, v_hbm,
     out_ref,
-    kbuf, vbuf, kcat, qbd, qin, scores, cos_tab, sin_tab, coarse_c, coarse_s, ksem, vsem,
+    tab, lens, qbuf, nkbuf, nvbuf, kbuf, vbuf, kcat0, kcat1, qbd, qin, qrot, scores,
+    tsem, ksem, vsem, lsem, qsem, nksem, nvsem,
     *, stretch, kv, chunks,
 ):
     batch, rows, width = kbuf.shape
-    heads = q_ref.shape[1]
+    heads = qbuf.shape[0]
     group = heads // kv
     lanes = batch * SLOT
     span = rows // kv
     chunk = rows // chunks
     pairs = batch // 2
+    whole_stretch = span == stretch
+    kcats = (kcat0, kcat1)
+
+    def tcopy(c):
+        part = pl.ds(c * chunk, chunk)
+        return pltpu.make_async_copy(tab_hbm.at[:, part, :], tab.at[:, part, :], tsem.at[c])
 
     def kcopy(c):
-        return pltpu.make_async_copy(
-            k_hbm.at[:, pl.ds(c * chunk, chunk), :], kbuf.at[:, pl.ds(c * chunk, chunk), :], ksem.at[c]
-        )
+        part = pl.ds(c * chunk, chunk)
+        return pltpu.make_async_copy(k_hbm.at[:, part, :], kbuf.at[:, part, :], ksem.at[c])
 
     def vcopy(c):
-        return pltpu.make_async_copy(
-            v_hbm.at[pl.ds(2 * c, 2)], vbuf.at[pl.ds(2 * c, 2)], vsem.at[c]
-        )
-
+        part = pl.ds(2 * c, 2)
+        return pltpu.make_async_copy(v_hbm.at[part], vbuf.at[part], vsem.at[c])
+
+    lcopy = pltpu.make_async_copy(lens_hbm, lens, lsem)
+    qcopy = pltpu.make_async_copy(q_hbm, qbuf, qsem)
+    nkcopy = pltpu.make_async_copy(nk_hbm, nkbuf, nksem)
+    nvcopy = pltpu.make_async_copy(nv_hbm, nvbuf, nvsem)
+    lcopy.start()
+    qcopy.start()
+    nkcopy.start()
     for c in range(chunks):
+        if whole_stretch:
+            tcopy(c).start()
         kcopy(c).start()
+    nvcopy.start()
     for c in range(pairs):
         vcopy(c).start()
 
-    place = place_ref[0]
+    place = lax.axis_index("seq").astype(jnp.int32)
     base = place * span
     key_stretch = base // stretch
 
-    freq8 = frequencies((8, width))
-    sign8 = half_sign((8, width))
-    row8 = lax.broadcasted_iota(jnp.int32, (8, width), 0)
-    per8 = 8 // kv
-    fine = (row8 // kv).astype(F32) * freq8
-    fine_c, fine_s = jnp.cos(fine), jnp.sin(fine) * sign8
-    n8 = rows // 8
-    start = (base % stretch).astype(F32)
-    coarse_pos = start + (lax.broadcasted_iota(jnp.int32, (n8, width), 0) * per8).astype(F32)
-    coarse = coarse_pos * frequencies((n8, width))
-    coarse_c[...] = jnp.cos(coarse)
-    coarse_s[...] = jnp.sin(coarse) * half_sign((n8, width))
-
-    def table(i, carry):
-        cc = coarse_c[pl.ds(i, 1), :]
-        cs = coarse_s[pl.ds(i, 1), :]
-        cos_tab[pl.ds(pl.multiple_of(i * 8, 8), 8), :] = cc * fine_c - cs * fine_s
-        sin_tab[pl.ds(pl.multiple_of(i * 8, 8), 8), :] = cs * fine_c + cc * fine_s
-        return carry
-
-    lax.fori_loop(0, n8, table, 0, unroll=8)
-
+    qbd[...] = jnp.zeros_like(qbd)
+    qin[...] = jnp.zeros_like(qin)
+    freq8 = frequencies((batch, width))
+    sign8 = half_sign((batch, width))
+    if not whole_stretch:
+        row = lax.broadcasted_iota(jnp.int32, (rows, width), 0)
+        angle = (base % stretch + row // kv).astype(F32) * frequencies((rows, width))
+        tab[0] = jnp.cos(angle)
+        tab[1] = jnp.sin(angle) * half_sign((rows, width))
+
+    lcopy.wait()
     picked, intra, limit = [], [], []
     for b in range(batch):
-        p = lens_ref[b]
+        p = lens[b]
         qc = p // stretch
         r = p - qc * stretch
         intra.append(r.astype(F32))
@@ -106,25 +111,29 @@
             jnp.where(key_stretch == qc, r, jnp.where(key_stretch == qc - 1, r + stretch, inter)).astype(F32)
         )
         limit.append((p - base) * kv)
-    angle_p = rows_of_scalars(picked, (8, width)) * freq8
-    angle_r = rows_of_scalars(intra, (8, width)) * freq8
+    angle_p = rows_of_scalars(picked, (batch, width)) * freq8
+    angle_r = rows_of_scalars(intra, (batch, width)) * freq8
     cp, sp = jnp.cos(angle_p), jnp.sin(angle_p) * sign8
     cr, sr = jnp.cos(angle_r), jnp.sin(angle_r) * sign8
 
-    qbd[...] = jnp.zeros_like(qbd)
-    qin[...] = jnp.zeros_like(qin)
+    qcopy.wait()
+    for h in range(heads):
+        q = qbuf[h].astype(F32)
+        at = slice(h * batch, (h + 1) * batch)
+        qrot[0, at, :] = rotate(q, cp, sp)
+        qrot[1, at, :] = rotate(q, cr, sr)
     for b in range(batch):
-        q = q_ref[b].astype(F32)
-        qbd[b * SLOT : b * SLOT + heads, b * width : (b + 1) * width] = rotate(
-            q, cp[b : b + 1], sp[b : b + 1]
-        ).astype(BF16)
-        qin[b * SLOT : b * SLOT + heads, :] = rotate(q, cr[b : b + 1], sr[b : b + 1]).astype(BF16)
+        mine = pl.ds(b, heads, stride=batch)
+        at = slice(b * SLOT, b * SLOT + heads)
+        qbd[at, b * width : (b + 1) * width] = qrot[0, mine, :].astype(BF16)
+        qin[at, :] = qrot[1, mine, :].astype(BF16)
 
     scaling = F32(1.0 / math.sqrt(width))
 
     own_rows = batch * kv
+    nkcopy.wait()
     knew = jnp.concatenate(
-        [rotate(nk_ref[b].astype(F32), cr[b : b + 1], sr[b : b + 1]) for b in range(batch)], axis=0
+        [rotate(nkbuf[b].astype(F32), cr[b : b + 1], sr[b : b + 1]) for b in range(batch)], axis=0
     ).astype(BF16)
     own_all = lax.dot_general(
         knew, qin[...], (((1,), (1,)), ((), ())), preferred_element_type=F32
@@ -145,26 +154,29 @@
     row_c = lax.broadcasted_iota(jnp.int32, (chunk, lanes), 0)
     fits = row_c % kv == lane_kv
 
-    top = own
-    for c in range(chunks):
-        kcopy(c).wait()
-
-        def turn(i, carry):
-            at = pl.multiple_of(i * 64, 64)
-            cc = cos_tab[pl.ds(c * chunk + at, 64), :]
-            ss = sin_tab[pl.ds(c * chunk + at, 64), :]
-            for b in range(batch):
-                k = kbuf[b, pl.ds(c * chunk + at, 64), :].astype(F32)
-                kcat[pl.ds(at, 64), b * width : (b + 1) * width] = rotate(k, cc, ss).astype(BF16)
-            return carry
-
-        lax.fori_loop(0, chunk // 64, turn, 0)
+    def rotate_keys(c):
+        part = slice(c * chunk, (c + 1) * chunk)
+        for b in range(batch):
+            k = kbuf[b, part, :].astype(F32)
+            kcats[c % 2][:, b * width : (b + 1) * width] = rotate(k, tab[0, part, :], tab[1, part, :]).astype(BF16)
+
+    def score(c, top):
         s = lax.dot_general(
-            kcat[...], qbd[...], (((1,), (1,)), ((), ())), preferred_element_type=F32
+            kcats[c % 2][...], qbd[...], (((1,), (1,)), ((), ())), preferred_element_type=F32
         ) * scaling
         s = jnp.where(fits & (row_c + c * chunk < bound), s, F32(NEG_FILL))
         scores[c * chunk : (c + 1) * chunk, :] = s
-        top = jnp.maximum(top, jnp.max(s, axis=0, keepdims=True))
+        return jnp.maximum(top, jnp.max(s, axis=0, keepdims=True))
+
+    top = own
+    for c in range(chunks):
+        if whole_stretch:
+            tcopy(c).wait()
+        kcopy(c).wait()
+        rotate_keys(c)
+        if c:
+            top = score(c - 1, top)
+    top = score(chunks - 1, top)
 
     own_w = jnp.where(first, jnp.exp(own - top), 0.0)
     total = own_w
@@ -176,8 +188,9 @@
         parts.append(jnp.transpose(w.astype(BF16)))
     wt = jnp.concatenate(parts, axis=1)
 
+    nvcopy.wait()
     own_wt = jnp.transpose(jnp.where(own_mask, own_w, 0.0))
-    nv = jnp.concatenate([nv_ref[b].astype(F32) for b in range(batch)], axis=0)
+    nv = jnp.concatenate([nvbuf[b].astype(F32) for b in range(batch)], axis=0)
     own_acc = lax.dot_general(
         own_wt, nv, (((1,), (0,)), ((), ())), preferred_element_type=F32,
         precision=lax.Precision.HIGHEST,
@@ -233,14 +246,28 @@
     out_ref[...] = jnp.dot(attended, w_ref[...], preferred_element_type=F32)
 
 
+def vmem(x):
+    return pltpu.with_memory_space_constraint(x, pltpu.VMEM)
+
+
 def in_vmem(count):
     return [pl.BlockSpec(memory_space=pltpu.VMEM)] * count
 
 
-def butterfly(values, axis):
+def butterfly(axis):
     size = lax.axis_size(axis)
     assert size & (size - 1) == 0
     return [[(i, i ^ (1 << k)) for i in range(size)] for k in range(size.bit_length() - 1)]
+
+
+def rope_tables(span, kv, width):
+    half = width // 2
+    index = np.arange(half, dtype=np.float32)
+    freq = np.exp(index * np.float32(-2.0 * math.log(THETA_BASE) / width)).astype(np.float32)
+    angle = np.arange(span, dtype=np.float32)[:, None] * freq
+    cos_part, sin_part = np.cos(angle.astype(np.float64)), np.sin(angle.astype(np.float64))
+    both = np.stack([np.concatenate([cos_part, cos_part], 1), np.concatenate([-sin_part, sin_part], 1)])
+    return np.repeat(both, kv, axis=1).astype(np.float32)
 
 
 def body(query, key_cache, value_cache, new_key, new_value, lengths, out_weight):
@@ -251,55 +278,59 @@
     rows = span * kv
     chunks = 4
     lanes = batch * SLOT
-    place = lax.axis_index("seq").astype(jnp.int32).reshape(1)
     packed_rows = heads * batch + batch
-    any_space = pl.BlockSpec(memory_space=pl.ANY)
-    smem = pl.BlockSpec(memory_space=pltpu.SMEM)
+    if span == stretch:
+        tables = jnp.asarray(rope_tables(span, kv, width))
+    else:
+        tables = jnp.zeros((2, 8, width), F32)
+    dma = pltpu.SemaphoreType.DMA
     packed = pl.pallas_call(
         functools.partial(attention_kernel, stretch=stretch, kv=kv, chunks=chunks),
-        out_shape=jax.ShapeDtypeStruct((packed_rows, width), F32),
-        in_specs=[smem, smem] + in_vmem(3) + [any_space, any_space],
+        out_shape=pltpu.VMEM((packed_rows, width), F32),
+        in_specs=[pl.BlockSpec(memory_space=pl.ANY)] * 7,
         out_specs=pl.BlockSpec(memory_space=pltpu.VMEM),
         scratch_shapes=[
+            pltpu.VMEM((2, rows, width), F32),
+            pltpu.SMEM((batch,), jnp.int32),
+            pltpu.VMEM((heads, batch, width), BF16),
+            pltpu.VMEM((batch, kv, width), BF16),
+            pltpu.VMEM((batch, kv, width), BF16),
             pltpu.VMEM((batch, rows, width), BF16),
             pltpu.VMEM((batch, rows, width), BF16),
             pltpu.VMEM((rows // chunks, batch * width), BF16),
+            pltpu.VMEM((rows // chunks, batch * width), BF16),
             pltpu.VMEM((lanes, batch * width), BF16),
             pltpu.VMEM((lanes, width), BF16),
+            pltpu.VMEM((2, heads * batch, width), F32),
             pltpu.VMEM((rows, lanes), F32),
-            pltpu.VMEM((rows, width), F32),
-            pltpu.VMEM((rows, width), F32),
-            pltpu.VMEM((rows // 8, width), F32),
-            pltpu.VMEM((rows // 8, width), F32),
-            pltpu.SemaphoreType.DMA((chunks,)),
-            pltpu.SemaphoreType.DMA((batch // 2,)),
+            dma((chunks,)), dma((chunks,)), dma((batch // 2,)), dma, dma, dma, dma,
         ],
         name="attention",
     )(
-        lengths, place, query, new_key, new_value,
+        tables, lengths, jnp.transpose(query, (1, 0, 2)), new_key, new_value,
         key_cache.reshape(batch, rows, width), value_cache.reshape(batch, rows, width),
     )
-    steps = butterfly(packed, "seq")
+    steps = butterfly("seq")
     for pairs in steps[:-1]:
         other = lax.ppermute(packed, "seq", pairs)
         packed = pl.pallas_call(
             functools.partial(merge_kernel, heads=heads, batch=batch),
-            out_shape=jax.ShapeDtypeStruct(packed.shape, F32),
+            out_shape=pltpu.VMEM(packed.shape, F32),
             in_specs=in_vmem(2),
             out_specs=pl.BlockSpec(memory_space=pltpu.VMEM),
             name="merge",
-        )(packed, other)
+        )(vmem(packed), vmem(other))
     other = lax.ppermute(packed, "seq", steps[-1])
-    partial_out = pl.pallas_call(
+    share = pl.pallas_call(
         functools.partial(project_kernel, heads=heads, batch=batch),
-        out_shape=jax.ShapeDtypeStruct((batch, out_weight.shape[1]), F32),
+        out_shape=pltpu.VMEM((batch, out_weight.shape[1]), F32),
         in_specs=in_vmem(3),
         out_specs=pl.BlockSpec(memory_space=pltpu.VMEM),
         name="project",
-    )(packed, other, out_weight)
-    for pairs in reversed(butterfly(partial_out, "head")):
-        partial_out = partial_out + lax.ppermute(partial_out, "head", pairs)
-    return partial_out
+    )(vmem(packed), vmem(other), vmem(out_weight))
+    for pairs in reversed(butterfly("head")):
+        share = share + lax.ppermute(share, "head", pairs)
+    return share
 
 
 def solution(mesh):

time: 37.9 us -> 26.6 us (0.70)
  Pallas kernels: 12.9 us -> 6.4 us
  local copies, waits for them, and re-layouts: 3.19 us -> 0.01 us
  waiting for transfers between devices: 10.1 us -> 9.23 us
  other arithmetic: 1.34 us -> 0.61 us
    unnamed x7 -> x2, local copies, waits for them, and re-layouts: 3.19 us -> 0.01 us
    pallas_call x2, Pallas kernels: 3.07 us -> 0.21 us  [body(): pl.pallas_call(functools.partial(merge_kernel, heads=heads, batch=batch),...]
    pallas_call x1, Pallas kernels: 2.55 us -> 0.45 us  [body(): pl.pallas_call(functools.partial(project_kernel, heads=heads, batch=batch...]
    pallas_call x1, Pallas kernels: 7.28 us -> 5.74 us  [body(): pl.pallas_call(functools.partial(attention_kernel, stretch=stretch, kv=kv...]
    add x2, other arithmetic: 1.34 us -> 0.61 us  [body(): share = share + lax.ppermute(share, 'head', pairs)]
    ppermute x2, waiting for transfers between devices: 4.47 us -> 4.05 us  [body(): other = lax.ppermute(packed, 'seq', pairs)]
where the time goes in v2:
time: 26.6 us; the launch traced here: 26.4 us
  starting transfers between devices  10.2 us (38%)
  waiting for transfers between devices  9.23 us (35%)
  Pallas kernels  6.4 us (24%)
  other arithmetic  0.61 us (2%)
    pallas_call x1, Pallas kernels, body(): pl.pallas_call(functools.partial(attention_kernel, stretch=stretch, kv=kv...  5.74 us
    ppermute x2, starting transfers between devices, body(): other = lax.ppermute(packed, 'seq', pairs)  5.2 us
    ppermute x2, waiting for transfers between devices, body(): other = lax.ppermute(packed, 'seq', pairs)  4.05 us
    ppermute x2, waiting for transfers between devices, body(): share = share + lax.ppermute(share, 'head', pairs)  3.15 us
    ppermute x1, starting transfers between devices, body(): other = lax.ppermute(packed, 'seq', steps[-1])  3.1 us
    ppermute x1, waiting for transfers between devices, body(): other = lax.ppermute(packed, 'seq', steps[-1])  2.03 us
    ppermute x2, starting transfers between devices, body(): share = share + lax.ppermute(share, 'head', pairs)  1.87 us
    add x2, other arithmetic, body(): share = share + lax.ppermute(share, 'head', pairs)  0.61 us
  transfers between devices with their start and end apart: 5, of which 5 were waited for; matrix products, arithmetic and copies ran while one was open for 0% of the time, Pallas kernels for 0%

profile of v2, /device:TPU:0, one launch (start us, length us, event | category | flops | bytes accessed | tf_op | source)
XLA Modules:
  0.0 26.4 jit_solution(9581058143401898944)
XLA Ops:
  0.0 0.0 copy-start
  0.0 5.7 %attention.1.a_ref = f32[88,128]{1,0:T(8,128)S(1)} custom-call(f32[2,1024,128]{2,1,0:T(8,128)} %constant.2.clone.tab_hbm, s32[8]{0:T(128)} %lens_hbm.1, bf16[10,8,128]{2,1,0:T(8,128)(2,1)} %bitcast.5, bf16[8,2,128]{2,1,0:T(2,128)(2,1)} %nk_hbm.1, bf16[8,2,128]{2,1,0:T(2,128)(2,1)} %nv_hbm.1, bf16[8,1024,128]{2,1,0:T(8,128)(2,1)} %bitcast.3, ...), custom_call_target="tpu_custom_call" | custom-call | tf_op jit(solution)/shard_map/attention/pallas_call | solution.py:287
  5.7 3.1 %collective-permute-start = (f32[88,128]{1,0:T(8,128)S(1)}, f32[88,128]{1,0:T(8,128)S(1)}, u32[]{:S(2)}, u32[]{:S(2)}) collective-permute-start(f32[88,128]{1,0:T(8,128)S(1)} %attention.1.a_ref), channel_id=1, source_target_pairs={{0,4},{4,0},{8,12},{12,8},{16,20},{20,16},{24,28},{28,24},{1,5},{5... | collective-permute-start | bytes 135176 | tf_op jit(solution)/shard_map/ppermute | solution.py:315
  8.8 2.0 %collective-permute-done.b_ref = f32[88,128]{1,0:T(8,128)S(1)} collective-permute-done((f32[88,128]{1,0:T(8,128)S(1)}, f32[88,128]{1,0:T(8,128)S(1)}, u32[]{:S(2)}, u32[]{:S(2)}) %collective-permute-start) | collective-permute-done | bytes 45088 | tf_op jit(solution)/shard_map/ppermute | solution.py:315
  10.8 0.1 merge.2.a_ref
  10.9 2.1 %collective-permute-start.1 = (f32[88,128]{1,0:T(8,128)S(1)}, f32[88,128]{1,0:T(8,128)S(1)}, u32[]{:S(2)}, u32[]{:S(2)}) collective-permute-start(f32[88,128]{1,0:T(8,128)S(1)} %merge.2.a_ref), channel_id=1, source_target_pairs={{0,8},{4,12},{8,0},{12,4},{16,24},{20,28},{24,16},{28,20},{1,9},{5... | collective-permute-start | bytes 135176 | tf_op jit(solution)/shard_map/ppermute | solution.py:315
  13.1 2.0 %collective-permute-done.1.b_ref = f32[88,128]{1,0:T(8,128)S(1)} collective-permute-done((f32[88,128]{1,0:T(8,128)S(1)}, f32[88,128]{1,0:T(8,128)S(1)}, u32[]{:S(2)}, u32[]{:S(2)}) %collective-permute-start.1) | collective-permute-done | bytes 45088 | tf_op jit(solution)/shard_map/ppermute | solution.py:315
  15.1 0.1 merge.3.a_ref
  15.2 3.1 %collective-permute-start.2 = (f32[88,128]{1,0:T(8,128)S(1)}, f32[88,128]{1,0:T(8,128)S(1)}, u32[]{:S(2)}, u32[]{:S(2)}) collective-permute-start(f32[88,128]{1,0:T(8,128)S(1)} %merge.3.a_ref), channel_id=1, source_target_pairs={{0,16},{4,20},{8,24},{12,28},{16,0},{20,4},{24,8},{28,12},{1,17},{... | collective-permute-start | bytes 135176 | tf_op jit(solution)/shard_map/ppermute | solution.py:323
  18.3 2.0 %collective-permute-done.2.b_ref = f32[88,128]{1,0:T(8,128)S(1)} collective-permute-done((f32[88,128]{1,0:T(8,128)S(1)}, f32[88,128]{1,0:T(8,128)S(1)}, u32[]{:S(2)}, u32[]{:S(2)}) %collective-permute-start.2) | collective-permute-done | bytes 45088 | tf_op jit(solution)/shard_map/ppermute | solution.py:323
  20.4 0.0 copy-done
  20.4 0.4 %project.1 = f32[8,640]{1,0:T(8,128)S(1)} custom-call(f32[88,128]{1,0:T(8,128)S(1)} %merge.3.a_ref, f32[88,128]{1,0:T(8,128)S(1)} %collective-permute-done.2.b_ref, bf16[1280,640]{1,0:T(8,128)(2,1)S(1)} %copy-done), custom_call_target="tpu_custom_call" | custom-call | tf_op jit(solution)/shard_map/project/pallas_call | solution.py:324
  20.8 1.9 %collective-permute-start.3 = (f32[8,640]{1,0:T(8,128)S(1)}, f32[8,640]{1,0:T(8,128)S(1)}, u32[]{:S(2)}, u32[]{:S(2)}) collective-permute-start(f32[8,640]{1,0:T(8,128)S(1)} %project.1), channel_id=1, source_target_pairs={{0,2},{1,3},{2,0},{3,1},{4,6},{5,7},{6,4},{7,5},{8,10},{9,11},{10,... | collective-permute-start | bytes 61448 | tf_op jit(solution)/shard_map/ppermute | solution.py:332
  22.7 2.0 %collective-permute-done.3 = f32[8,640]{1,0:T(8,128)S(1)} collective-permute-done((f32[8,640]{1,0:T(8,128)S(1)}, f32[8,640]{1,0:T(8,128)S(1)}, u32[]{:S(2)}, u32[]{:S(2)}) %collective-permute-start.3) | collective-permute-done | bytes 20512 | tf_op jit(solution)/shard_map/ppermute | solution.py:332
  24.6 0.0 collective-permute-start.4
  24.6 1.2 %collective-permute-done.4 = f32[8,640]{1,0:T(8,128)S(1)} collective-permute-done((f32[8,640]{1,0:T(8,128)S(1)}, f32[8,640]{1,0:T(8,128)S(1)}, u32[]{:S(2)}, u32[]{:S(2)}) %collective-permute-start.4) | collective-permute-done | bytes 20512 | tf_op jit(solution)/shard_map/ppermute | solution.py:332
  25.8 0.6 %add.7 = f32[8,640]{1,0:T(8,128)} add(f32[8,640]{1,0:T(8,128)S(1)} %add.6, f32[8,640]{1,0:T(8,128)S(1)} %collective-permute-done.4) | non-fusion elementwise | flops 5120 | bytes 61440 | tf_op jit(solution)/shard_map/add | solution.py:332
  (1 shorter events, 0.0 us)
Async XLA Ops:
  0.0 20.4 %copy-start = (bf16[1280,640]{1,0:T(8,128)(2,1)S(1)}, bf16[1280,640]{1,0:T(8,128)(2,1)}, u32[]{:S(2)}) copy-start(bf16[1280,640]{1,0:T(8,128)(2,1)} %w_ref.1) | copy-start | bytes 4915204
  5.7 5.1 %collective-permute-start = (f32[88,128]{1,0:T(8,128)S(1)}, f32[88,128]{1,0:T(8,128)S(1)}, u32[]{:S(2)}, u32[]{:S(2)}) collective-permute-start(f32[88,128]{1,0:T(8,128)S(1)} %attention.1.a_ref), channel_id=1, source_target_pairs={{0,4},{4,0},{8,12},{12,8},{16,20},{20,16},{24,28},{28,24},{1,5},{5... | collective-permute-start | bytes 135176 | tf_op jit(solution)/shard_map/ppermute | solution.py:315
  10.9 4.2 %collective-permute-start.1 = (f32[88,128]{1,0:T(8,128)S(1)}, f32[88,128]{1,0:T(8,128)S(1)}, u32[]{:S(2)}, u32[]{:S(2)}) collective-permute-start(f32[88,128]{1,0:T(8,128)S(1)} %merge.2.a_ref), channel_id=1, source_target_pairs={{0,8},{4,12},{8,0},{12,4},{16,24},{20,28},{24,16},{28,20},{1,9},{5... | collective-permute-start | bytes 135176 | tf_op jit(solution)/shard_map/ppermute | solution.py:315
  15.2 5.1 %collective-permute-start.2 = (f32[88,128]{1,0:T(8,128)S(1)}, f32[88,128]{1,0:T(8,128)S(1)}, u32[]{:S(2)}, u32[]{:S(2)}) collective-permute-start(f32[88,128]{1,0:T(8,128)S(1)} %merge.3.a_ref), channel_id=1, source_target_pairs={{0,16},{4,20},{8,24},{12,28},{16,0},{20,4},{24,8},{28,12},{1,17},{... | collective-permute-start | bytes 135176 | tf_op jit(solution)/shard_map/ppermute | solution.py:323
  20.8 3.8 %collective-permute-start.3 = (f32[8,640]{1,0:T(8,128)S(1)}, f32[8,640]{1,0:T(8,128)S(1)}, u32[]{:S(2)}, u32[]{:S(2)}) collective-permute-start(f32[8,640]{1,0:T(8,128)S(1)} %project.1), channel_id=1, source_target_pairs={{0,2},{1,3},{2,0},{3,1},{4,6},{5,7},{6,4},{7,5},{8,10},{9,11},{10,... | collective-permute-start | bytes 61448 | tf_op jit(solution)/shard_map/ppermute | solution.py:332
  24.6 1.2 %collective-permute-start.4 = (f32[8,640]{1,0:T(8,128)S(1)}, f32[8,640]{1,0:T(8,128)S(1)}, u32[]{:S(2)}, u32[]{:S(2)}) collective-permute-start(f32[8,640]{1,0:T(8,128)S(1)} %add.6), channel_id=1, source_target_pairs={{0,1},{1,0},{2,3},{3,2},{4,5},{5,4},{6,7},{7,6},{8,9},{9,8},{10,11... | collective-permute-start | bytes 61448 | tf_op jit(solution)/shard_map/ppermute | solution.py:332

commit v3 on v2

--- a/solution.py
+++ b/solution.py
@@ -42,10 +42,10 @@
 
 
 def attention_kernel(
-    tab_hbm, lens_hbm, q_hbm, nk_hbm, nv_hbm, k_hbm, v_hbm,
-    out_ref,
+    tab_hbm, lens_hbm, q_hbm, nk_hbm, nv_hbm, k_hbm, v_hbm, w_hbm,
+    out_ref, w_ref,
     tab, lens, qbuf, nkbuf, nvbuf, kbuf, vbuf, kcat0, kcat1, qbd, qin, qrot, scores,
-    tsem, ksem, vsem, lsem, qsem, nksem, nvsem,
+    tsem, ksem, vsem, lsem, qsem, nksem, nvsem, wsem,
     *, stretch, kv, chunks,
 ):
     batch, rows, width = kbuf.shape
@@ -69,6 +69,8 @@
     def vcopy(c):
         part = pl.ds(2 * c, 2)
         return pltpu.make_async_copy(v_hbm.at[part], vbuf.at[part], vsem.at[c])
+
+    wcopy = pltpu.make_async_copy(w_hbm, w_ref, wsem)
 
     lcopy = pltpu.make_async_copy(lens_hbm, lens, lsem)
     qcopy = pltpu.make_async_copy(q_hbm, qbuf, qsem)
@@ -82,8 +84,6 @@
             tcopy(c).start()
         kcopy(c).start()
     nvcopy.start()
-    for c in range(pairs):
-        vcopy(c).start()
 
     place = lax.axis_index("seq").astype(jnp.int32)
     base = place * span
@@ -158,11 +158,12 @@
         part = slice(c * chunk, (c + 1) * chunk)
         for b in range(batch):
             k = kbuf[b, part, :].astype(F32)
-            kcats[c % 2][:, b * width : (b + 1) * width] = rotate(k, tab[0, part, :], tab[1, part, :]).astype(BF16)
+            kcats[c % 2][b] = rotate(k, tab[0, part, :], tab[1, part, :]).astype(BF16)
 
     def score(c, top):
+        keys = jnp.concatenate([kcats[c % 2][b] for b in range(batch)], axis=1)
         s = lax.dot_general(
-            kcats[c % 2][...], qbd[...], (((1,), (1,)), ((), ())), preferred_element_type=F32
+            keys, qbd[...], (((1,), (1,)), ((), ())), preferred_element_type=F32
         ) * scaling
         s = jnp.where(fits & (row_c + c * chunk < bound), s, F32(NEG_FILL))
         scores[c * chunk : (c + 1) * chunk, :] = s
@@ -173,6 +174,11 @@
         if whole_stretch:
             tcopy(c).wait()
         kcopy(c).wait()
+        if c == 0:
+            for i in range(pairs):
+                vcopy(i).start()
+        if c == chunks - 1:
+            wcopy.start()
         rotate_keys(c)
         if c:
             top = score(c - 1, top)
@@ -198,6 +204,7 @@
 
     for c in range(pairs):
         vcopy(c).wait()
+    for c in range(pairs):
         v = jnp.concatenate([vbuf[2 * c], vbuf[2 * c + 1]], axis=1)
         acc = jnp.dot(wt[2 * c * SLOT : (2 * c + 2) * SLOT, :], v, preferred_element_type=F32)
         for j in range(2):
@@ -214,32 +221,39 @@
         l_b = pltpu.roll(total, (lanes + SLOT - b * SLOT) % lanes, 1) if b != 1 else total
         stats = jnp.where(row_b == b, jnp.where(lane_b < SLOT, m_b, l_b), stats)
     out_ref[heads * batch :, :] = stats
-
-
-def merge(a_ref, b_ref, heads, batch):
-    a = a_ref[heads * batch :, :]
-    b = b_ref[heads * batch :, :]
-    top = jnp.maximum(a, b)
-    fa, fb = jnp.exp(a - top), jnp.exp(b - top)
-    total = a * pltpu.roll(fa, SLOT, 1) + b * pltpu.roll(fb, SLOT, 1)
+    wcopy.wait()
+
+
+def balanced_sum(values):
+    while len(values) > 1:
+        values = [values[i] + values[i + 1] for i in range(0, len(values), 2)]
+    return values[0]
+
+
+def merge(parts, heads, batch):
+    stats = [p[heads * batch :, :] for p in parts]
+    top = functools.reduce(jnp.maximum, stats)
+    factors = [jnp.exp(s - top) for s in stats]
+    total = balanced_sum([s * pltpu.roll(f, SLOT, 1) for s, f in zip(stats, factors)])
     lane = lax.broadcasted_iota(jnp.int32, top.shape, 1)
-    stats = jnp.where(lane < SLOT, top, total)
     sums = []
     for h in range(heads):
         rows = slice(h * batch, (h + 1) * batch)
-        sums.append(a_ref[rows, :] * fa[:, h : h + 1] + b_ref[rows, :] * fb[:, h : h + 1])
-    return sums, stats
-
-
-def merge_kernel(a_ref, b_ref, out_ref, *, heads, batch):
-    sums, stats = merge(a_ref, b_ref, heads, batch)
+        sums.append(balanced_sum([p[rows, :] * f[:, h : h + 1] for p, f in zip(parts, factors)]))
+    return sums, jnp.where(lane < SLOT, top, total)
+
+
+def merge_kernel(*refs, heads, batch):
+    out_ref = refs[-1]
+    sums, stats = merge(refs[:-1], heads, batch)
     for h in range(heads):
         out_ref[h * batch : (h + 1) * batch, :] = sums[h]
     out_ref[heads * batch :, :] = stats
 
 
-def project_kernel(a_ref, b_ref, w_ref, out_ref, *, heads, batch):
-    sums, stats = merge(a_ref, b_ref, heads, batch)
+def project_kernel(*refs, heads, batch):
+    w_ref, out_ref = refs[-2:]
+    sums, stats = merge(refs[:-2], heads, batch)
     attended = jnp.concatenate(
         [(sums[h] / stats[:, SLOT + h : SLOT + h + 1]).astype(BF16) for h in range(heads)], axis=1
     )
@@ -254,10 +268,19 @@
     return [pl.BlockSpec(memory_space=pltpu.VMEM)] * count
 
 
-def butterfly(axis):
+def exchange_steps(axis):
     size = lax.axis_size(axis)
     assert size & (size - 1) == 0
-    return [[(i, i ^ (1 << k)) for i in range(size)] for k in range(size.bit_length() - 1)]
+    steps, low = [], 1
+    while low < size:
+        steps.append([low, 2 * low, 3 * low] if 4 * low <= size else [low])
+        low *= len(steps[-1]) + 1
+    return steps
+
+
+def gather_from(value, axis, distances):
+    size = lax.axis_size(axis)
+    return [value] + [lax.ppermute(value, axis, [(i, i ^ d) for i in range(size)]) for d in distances]
 
 
 def rope_tables(span, kv, width):
@@ -284,11 +307,11 @@
     else:
         tables = jnp.zeros((2, 8, width), F32)
     dma = pltpu.SemaphoreType.DMA
-    packed = pl.pallas_call(
+    packed, weight = pl.pallas_call(
         functools.partial(attention_kernel, stretch=stretch, kv=kv, chunks=chunks),
-        out_shape=pltpu.VMEM((packed_rows, width), F32),
-        in_specs=[pl.BlockSpec(memory_space=pl.ANY)] * 7,
-        out_specs=pl.BlockSpec(memory_space=pltpu.VMEM),
+        out_shape=[pltpu.VMEM((packed_rows, width), F32), pltpu.VMEM(out_weight.shape, BF16)],
+        in_specs=[pl.BlockSpec(memory_space=pl.ANY)] * 8,
+        out_specs=in_vmem(2),
         scratch_shapes=[
             pltpu.VMEM((2, rows, width), F32),
             pltpu.SMEM((batch,), jnp.int32),
@@ -297,39 +320,40 @@
             pltpu.VMEM((batch, kv, width), BF16),
             pltpu.VMEM((batch, rows, width), BF16),
             pltpu.VMEM((batch, rows, width), BF16),
-            pltpu.VMEM((rows // chunks, batch * width), BF16),
-            pltpu.VMEM((rows // chunks, batch * width), BF16),
+            pltpu.VMEM((batch, rows // chunks, width), BF16),
+            pltpu.VMEM((batch, rows // chunks, width), BF16),
             pltpu.VMEM((lanes, batch * width), BF16),
             pltpu.VMEM((lanes, width), BF16),
             pltpu.VMEM((2, heads * batch, width), F32),
             pltpu.VMEM((rows, lanes), F32),
-            dma((chunks,)), dma((chunks,)), dma((batch // 2,)), dma, dma, dma, dma,
+            dma((chunks,)), dma((chunks,)), dma((batch // 2,)), dma, dma, dma, dma, dma,
         ],
         name="attention",
     )(
         tables, lengths, jnp.transpose(query, (1, 0, 2)), new_key, new_value,
         key_cache.reshape(batch, rows, width), value_cache.reshape(batch, rows, width),
-    )
-    steps = butterfly("seq")
-    for pairs in steps[:-1]:
-        other = lax.ppermute(packed, "seq", pairs)
+        out_weight,
+    )
+    steps = exchange_steps("seq")
+    for distances in steps[:-1]:
+        parts = gather_from(packed, "seq", distances)
         packed = pl.pallas_call(
             functools.partial(merge_kernel, heads=heads, batch=batch),
             out_shape=pltpu.VMEM(packed.shape, F32),
-            in_specs=in_vmem(2),
-            out_specs=pl.BlockSpec(memory_space=pltpu.VMEM),
+            in_specs=in_vmem(len(parts)),
+            out_specs=in_vmem(1)[0],
             name="merge",
-        )(vmem(packed), vmem(other))
-    other = lax.ppermute(packed, "seq", steps[-1])
+        )(*map(vmem, parts))
+    parts = gather_from(packed, "seq", steps[-1])
     share = pl.pallas_call(
         functools.partial(project_kernel, heads=heads, batch=batch),
         out_shape=pltpu.VMEM((batch, out_weight.shape[1]), F32),
-        in_specs=in_vmem(3),
-        out_specs=pl.BlockSpec(memory_space=pltpu.VMEM),
+        in_specs=in_vmem(len(parts) + 1),
+        out_specs=in_vmem(1)[0],
         name="project",
-    )(vmem(packed), vmem(other), vmem(out_weight))
-    for pairs in reversed(butterfly("head")):
-        share = share + lax.ppermute(share, "head", pairs)
+    )(*map(vmem, parts), vmem(weight))
+    for distances in exchange_steps("head"):
+        share = balanced_sum(gather_from(share, "head", distances))
     return share
 
 

time: 26.6 us -> 23.4 us (0.88)
  Pallas kernels: 6.4 us -> 5.14 us
  waiting for transfers between devices: 9.23 us -> 8.21 us
  starting transfers between devices: 10.2 us -> 9.27 us
    pallas_call x1, Pallas kernels: 5.74 us -> 4.55 us  [body(): pl.pallas_call(functools.partial(attention_kernel, stretch=stretch, kv=kv...]
    ppermute x5 -> x7, waiting for transfers between devices: 9.23 us -> 8.21 us  [gather_from(): lax.ppermute(value, axis, [(i, i ^ d) for i in range(size)])]
    ppermute x5 -> x7, starting transfers between devices: 10.2 us -> 9.27 us  [gather_from(): lax.ppermute(value, axis, [(i, i ^ d) for i in range(size)])]
    add x2 -> x1, other arithmetic: 0.61 us -> 0.61 us  [balanced_sum(): values = [values[i] + values[i + 1] for i in range(0, len(values), 2)]]
  transfers between devices with their start and end apart: 5 -> 7, of which waited for: 5 -> 6; matrix products, arithmetic and copies ran while one was open for 0% -> 0% of each run, Pallas kernels for 0% -> 0%
where the time goes in v3:
time: 23.4 us; the launch traced here: 23.3 us
  starting transfers between devices  9.27 us (40%)
  waiting for transfers between devices  8.21 us (35%)
  Pallas kernels  5.14 us (22%)
  other arithmetic  0.61 us (3%)
    ppermute x7, starting transfers between devices, gather_from(): lax.ppermute(value, axis, [(i, i ^ d) for i in range(size)])  9.27 us
    ppermute x7, waiting for transfers between devices, gather_from(): lax.ppermute(value, axis, [(i, i ^ d) for i in range(size)])  8.21 us
    pallas_call x1, Pallas kernels, body(): pl.pallas_call(functools.partial(attention_kernel, stretch=stretch, kv=kv...  4.55 us
    add x1, other arithmetic, balanced_sum(): values = [values[i] + values[i + 1] for i in range(0, len(values), 2)]  0.61 us
  transfers between devices with their start and end apart: 7, of which 6 were waited for; matrix products, arithmetic and copies ran while one was open for 0% of the time, Pallas kernels for 0%

profile of v3, /device:TPU:0, one launch (start us, length us, event | category | flops | bytes accessed | tf_op | source)
XLA Modules:
  0.0 23.3 jit_solution(8515243954753385063)
XLA Ops:
  0.0 4.5 %attention.1 = (f32[88,128]{1,0:T(8,128)S(1)}, bf16[1280,640]{1,0:T(8,128)(2,1)S(1)}) custom-call(f32[2,1024,128]{2,1,0:T(8,128)} %constant.2.clone.tab_hbm, s32[8]{0:T(128)} %lens_hbm.1, bf16[10,8,128]{2,1,0:T(8,128)(2,1)} %bitcast.5, bf16[8,2,128]{2,1,0:T(2,128)(2,1)} %nk_hbm.1, bf16[8,2,128]{2,1,0:T(2,128)(2,1)} %nv_hbm.1, bf16[8,1024,128]{2,1,0:T(8,128)(2,1)} %bitcast.3, ...), custom_call_target="tpu_custom_call" | custom-call | tf_op jit(solution)/shard_map/attention/pallas_call | solution.py:310
  4.6 4.1 %collective-permute-start.2 = (f32[88,128]{1,0:T(8,128)S(1)}, f32[88,128]{1,0:T(8,128)S(1)}, u32[]{:S(2)}, u32[]{:S(2)}) collective-permute-start(f32[88,128]{1,0:T(8,128)S(1)} %get-tuple-element.7.refs_0_), channel_id=1, source_target_pairs={{0,12},{4,8},{8,4},{12,0},{16,28},{20,24},{24,20},{28,16},{1,13},{... | collective-permute-start | bytes 135176 | tf_op jit(solution)/shard_map/ppermute | solution.py:283
  8.6 0.4 %collective-permute-start.1 = (f32[88,128]{1,0:T(8,128)S(1)}, f32[88,128]{1,0:T(8,128)S(1)}, u32[]{:S(2)}, u32[]{:S(2)}) collective-permute-start(f32[88,128]{1,0:T(8,128)S(1)} %get-tuple-element.7.refs_0_), channel_id=1, source_target_pairs={{0,8},{4,12},{8,0},{12,4},{16,24},{20,28},{24,16},{28,20},{1,9},{5... | collective-permute-start | bytes 135176 | tf_op jit(solution)/shard_map/ppermute | solution.py:283
  9.1 0.2 collective-permute-start
  9.3 1.4 %collective-permute-done.2.refs_3_ = f32[88,128]{1,0:T(8,128)S(1)} collective-permute-done((f32[88,128]{1,0:T(8,128)S(1)}, f32[88,128]{1,0:T(8,128)S(1)}, u32[]{:S(2)}, u32[]{:S(2)}) %collective-permute-start.2) | collective-permute-done | bytes 45088 | tf_op jit(solution)/shard_map/ppermute | solution.py:283
  10.7 2.0 %collective-permute-done.1.refs_2_ = f32[88,128]{1,0:T(8,128)S(1)} collective-permute-done((f32[88,128]{1,0:T(8,128)S(1)}, f32[88,128]{1,0:T(8,128)S(1)}, u32[]{:S(2)}, u32[]{:S(2)}) %collective-permute-start.1) | collective-permute-done | bytes 45088 | tf_op jit(solution)/shard_map/ppermute | solution.py:283
  12.7 0.4 %collective-permute-done.refs_1_ = f32[88,128]{1,0:T(8,128)S(1)} collective-permute-done((f32[88,128]{1,0:T(8,128)S(1)}, f32[88,128]{1,0:T(8,128)S(1)}, u32[]{:S(2)}, u32[]{:S(2)}) %collective-permute-start) | collective-permute-done | bytes 45088 | tf_op jit(solution)/shard_map/ppermute | solution.py:283
  13.1 0.1 merge.1.refs_0_
  13.3 2.7 %collective-permute-start.3 = (f32[88,128]{1,0:T(8,128)S(1)}, f32[88,128]{1,0:T(8,128)S(1)}, u32[]{:S(2)}, u32[]{:S(2)}) collective-permute-start(f32[88,128]{1,0:T(8,128)S(1)} %merge.1.refs_0_), channel_id=1, source_target_pairs={{0,16},{4,20},{8,24},{12,28},{16,0},{20,4},{24,8},{28,12},{1,17},{... | collective-permute-start | bytes 135176 | tf_op jit(solution)/shard_map/ppermute | solution.py:283
  15.9 2.4 %collective-permute-done.3.refs_1_ = f32[88,128]{1,0:T(8,128)S(1)} collective-permute-done((f32[88,128]{1,0:T(8,128)S(1)}, f32[88,128]{1,0:T(8,128)S(1)}, u32[]{:S(2)}, u32[]{:S(2)}) %collective-permute-start.3) | collective-permute-done | bytes 45088 | tf_op jit(solution)/shard_map/ppermute | solution.py:283
  18.3 0.4 %project.1 = f32[8,640]{1,0:T(8,128)S(1)} custom-call(f32[88,128]{1,0:T(8,128)S(1)} %merge.1.refs_0_, f32[88,128]{1,0:T(8,128)S(1)} %collective-permute-done.3.refs_1_, bf16[1280,640]{1,0:T(8,128)(2,1)S(1)} %get-tuple-element.8.refs_2_), custom_call_target="tpu_custom_call" | custom-call | tf_op jit(solution)/shard_map/project/pallas_call | solution.py:348
  18.7 0.1 collective-permute-start.6
  18.8 1.6 %collective-permute-start.5 = (f32[8,640]{1,0:T(8,128)S(1)}, f32[8,640]{1,0:T(8,128)S(1)}, u32[]{:S(2)}, u32[]{:S(2)}) collective-permute-start(f32[8,640]{1,0:T(8,128)S(1)} %project.1), channel_id=1, source_target_pairs={{0,2},{1,3},{2,0},{3,1},{4,6},{5,7},{6,4},{7,5},{8,10},{9,11},{10,... | collective-permute-start | bytes 61448 | tf_op jit(solution)/shard_map/ppermute | solution.py:283
  20.4 0.3 %collective-permute-start.4 = (f32[8,640]{1,0:T(8,128)S(1)}, f32[8,640]{1,0:T(8,128)S(1)}, u32[]{:S(2)}, u32[]{:S(2)}) collective-permute-start(f32[8,640]{1,0:T(8,128)S(1)} %project.1), channel_id=1, source_target_pairs={{0,1},{1,0},{2,3},{3,2},{4,5},{5,4},{6,7},{7,6},{8,9},{9,8},{10,11... | collective-permute-start | bytes 61448 | tf_op jit(solution)/shard_map/ppermute | solution.py:283
  20.6 1.5 %collective-permute-done.6 = f32[8,640]{1,0:T(8,128)S(1)} collective-permute-done((f32[8,640]{1,0:T(8,128)S(1)}, f32[8,640]{1,0:T(8,128)S(1)}, u32[]{:S(2)}, u32[]{:S(2)}) %collective-permute-start.6) | collective-permute-done | bytes 20512 | tf_op jit(solution)/shard_map/ppermute | solution.py:283
  22.2 0.5 %collective-permute-done.5 = f32[8,640]{1,0:T(8,128)S(1)} collective-permute-done((f32[8,640]{1,0:T(8,128)S(1)}, f32[8,640]{1,0:T(8,128)S(1)}, u32[]{:S(2)}, u32[]{:S(2)}) %collective-permute-start.5) | collective-permute-done | bytes 20512 | tf_op jit(solution)/shard_map/ppermute | solution.py:283
  22.6 0.0 collective-permute-done.4
  22.6 0.6 %add_add_fusion = f32[8,640]{1,0:T(8,128)} fusion(f32[8,640]{1,0:T(8,128)S(1)} %collective-permute-done.5, f32[8,640]{1,0:T(8,128)S(1)} %collective-permute-done.6, f32[8,640]{1,0:T(8,128)S(1)} %project.1, f32[8,640]{1,0:T(8,128)S(1)} %collective-permute-done.4), kind=kLoop, calls=%fused_computation | loop fusion | flops 15360 | bytes 102400 | tf_op jit(solution)/shard_map/add | solution.py:229
Async XLA Ops:
  4.6 6.1 %collective-permute-start.2 = (f32[88,128]{1,0:T(8,128)S(1)}, f32[88,128]{1,0:T(8,128)S(1)}, u32[]{:S(2)}, u32[]{:S(2)}) collective-permute-start(f32[88,128]{1,0:T(8,128)S(1)} %get-tuple-element.7.refs_0_), channel_id=1, source_target_pairs={{0,12},{4,8},{8,4},{12,0},{16,28},{20,24},{24,20},{28,16},{1,13},{... | collective-permute-start | bytes 135176 | tf_op jit(solution)/shard_map/ppermute | solution.py:283
  8.6 4.0 %collective-permute-start.1 = (f32[88,128]{1,0:T(8,128)S(1)}, f32[88,128]{1,0:T(8,128)S(1)}, u32[]{:S(2)}, u32[]{:S(2)}) collective-permute-start(f32[88,128]{1,0:T(8,128)S(1)} %get-tuple-element.7.refs_0_), channel_id=1, source_target_pairs={{0,8},{4,12},{8,0},{12,4},{16,24},{20,28},{24,16},{28,20},{1,9},{5... | collective-permute-start | bytes 135176 | tf_op jit(solution)/shard_map/ppermute | solution.py:283
  9.1 4.0 %collective-permute-start = (f32[88,128]{1,0:T(8,128)S(1)}, f32[88,128]{1,0:T(8,128)S(1)}, u32[]{:S(2)}, u32[]{:S(2)}) collective-permute-start(f32[88,128]{1,0:T(8,128)S(1)} %get-tuple-element.7.refs_0_), channel_id=1, source_target_pairs={{0,4},{4,0},{8,12},{12,8},{16,20},{20,16},{24,28},{28,24},{1,5},{5... | collective-permute-start | bytes 135176 | tf_op jit(solution)/shard_map/ppermute | solution.py:283
  13.3 5.0 %collective-permute-start.3 = (f32[88,128]{1,0:T(8,128)S(1)}, f32[88,128]{1,0:T(8,128)S(1)}, u32[]{:S(2)}, u32[]{:S(2)}) collective-permute-start(f32[88,128]{1,0:T(8,128)S(1)} %merge.1.refs_0_), channel_id=1, source_target_pairs={{0,16},{4,20},{8,24},{12,28},{16,0},{20,4},{24,8},{28,12},{1,17},{... | collective-permute-start | bytes 135176 | tf_op jit(solution)/shard_map/ppermute | solution.py:283
  18.7 3.4 %collective-permute-start.6 = (f32[8,640]{1,0:T(8,128)S(1)}, f32[8,640]{1,0:T(8,128)S(1)}, u32[]{:S(2)}, u32[]{:S(2)}) collective-permute-start(f32[8,640]{1,0:T(8,128)S(1)} %project.1), channel_id=1, source_target_pairs={{0,3},{1,2},{2,1},{3,0},{4,7},{5,6},{6,5},{7,4},{8,11},{9,10},{10,... | collective-permute-start | bytes 61448 | tf_op jit(solution)/shard_map/ppermute | solution.py:283
  18.8 3.8 %collective-permute-start.5 = (f32[8,640]{1,0:T(8,128)S(1)}, f32[8,640]{1,0:T(8,128)S(1)}, u32[]{:S(2)}, u32[]{:S(2)}) collective-permute-start(f32[8,640]{1,0:T(8,128)S(1)} %project.1), channel_id=1, source_target_pairs={{0,2},{1,3},{2,0},{3,1},{4,6},{5,7},{6,4},{7,5},{8,10},{9,11},{10,... | collective-permute-start | bytes 61448 | tf_op jit(solution)/shard_map/ppermute | solution.py:283
  20.4 2.3 %collective-permute-start.4 = (f32[8,640]{1,0:T(8,128)S(1)}, f32[8,640]{1,0:T(8,128)S(1)}, u32[]{:S(2)}, u32[]{:S(2)}) collective-permute-start(f32[8,640]{1,0:T(8,128)S(1)} %project.1), channel_id=1, source_target_pairs={{0,1},{1,0},{2,3},{3,2},{4,5},{5,4},{6,7},{7,6},{8,9},{9,8},{10,11... | collective-permute-start | bytes 61448 | tf_op jit(solution)/shard_map/ppermute | solution.py:283

commit v4 on v3

--- a/solution.py
+++ b/solution.py
@@ -44,8 +44,8 @@
 def attention_kernel(
     tab_hbm, lens_hbm, q_hbm, nk_hbm, nv_hbm, k_hbm, v_hbm, w_hbm,
     out_ref, w_ref,
-    tab, lens, qbuf, nkbuf, nvbuf, kbuf, vbuf, kcat0, kcat1, qbd, qin, qrot, scores,
-    tsem, ksem, vsem, lsem, qsem, nksem, nvsem, wsem,
+    tab_raw, tab, lens, qbuf, nkbuf, nvbuf, kbuf, vbuf, kcat0, kcat1, qbd, qin, qrot, scores,
+    tsem, ksem, vsem, lsem, qsem, nksem, nvsem, wsem, order,
     *, stretch, kv, chunks,
 ):
     batch, rows, width = kbuf.shape
@@ -58,32 +58,28 @@
     whole_stretch = span == stretch
     kcats = (kcat0, kcat1)
 
-    def tcopy(c):
-        part = pl.ds(c * chunk, chunk)
-        return pltpu.make_async_copy(tab_hbm.at[:, part, :], tab.at[:, part, :], tsem.at[c])
-
     def kcopy(c):
         part = pl.ds(c * chunk, chunk)
         return pltpu.make_async_copy(k_hbm.at[:, part, :], kbuf.at[:, part, :], ksem.at[c])
 
-    def vcopy(c):
-        part = pl.ds(2 * c, 2)
-        return pltpu.make_async_copy(v_hbm.at[part], vbuf.at[part], vsem.at[c])
-
+    vcopy = pltpu.make_async_copy(v_hbm, vbuf, vsem)
+    tcopy = pltpu.make_async_copy(tab_hbm, tab_raw, tsem)
     wcopy = pltpu.make_async_copy(w_hbm, w_ref, wsem)
 
     lcopy = pltpu.make_async_copy(lens_hbm, lens, lsem)
     qcopy = pltpu.make_async_copy(q_hbm, qbuf, qsem)
     nkcopy = pltpu.make_async_copy(nk_hbm, nkbuf, nksem)
     nvcopy = pltpu.make_async_copy(nv_hbm, nvbuf, nvsem)
-    lcopy.start()
-    qcopy.start()
-    nkcopy.start()
+    small = (lcopy, qcopy, nkcopy, nvcopy)
+    for copy in small:
+        copy.start()
+    if whole_stretch:
+        tcopy.start()
+    pl.semaphore_signal(order, 1)
+    pl.semaphore_wait(order, 1)
     for c in range(chunks):
-        if whole_stretch:
-            tcopy(c).start()
         kcopy(c).start()
-    nvcopy.start()
+    vcopy.start()
 
     place = lax.axis_index("seq").astype(jnp.int32)
     base = place * span
@@ -99,7 +95,19 @@
         tab[0] = jnp.cos(angle)
         tab[1] = jnp.sin(angle) * half_sign((rows, width))
 
-    lcopy.wait()
+    for copy in small:
+        copy.wait()
+    if whole_stretch:
+        tcopy.wait()
+        lower = lax.broadcasted_iota(jnp.int32, (8, width), 1) < width // 2
+        for i in range(span // 8):
+            t = tab_raw[8 * i : 8 * i + 8, :]
+            other = pltpu.roll(t, width // 2, 1)
+            cos_part, sin_part = jnp.where(lower, t, other), jnp.where(lower, -other, t)
+            for j in range(kv):
+                at = pl.ds(8 * kv * i + j, 8, stride=kv)
+                tab[0, at, :] = cos_part
+                tab[1, at, :] = sin_part
     picked, intra, limit = [], [], []
     for b in range(batch):
         p = lens[b]
@@ -116,7 +124,6 @@
     cp, sp = jnp.cos(angle_p), jnp.sin(angle_p) * sign8
     cr, sr = jnp.cos(angle_r), jnp.sin(angle_r) * sign8
 
-    qcopy.wait()
     for h in range(heads):
         q = qbuf[h].astype(F32)
         at = slice(h * batch, (h + 1) * batch)
@@ -130,22 +137,6 @@
 
     scaling = F32(1.0 / math.sqrt(width))
 
-    own_rows = batch * kv
-    nkcopy.wait()
-    knew = jnp.concatenate(
-        [rotate(nkbuf[b].astype(F32), cr[b : b + 1], sr[b : b + 1]) for b in range(batch)], axis=0
-    ).astype(BF16)
-    own_all = lax.dot_general(
-        knew, qin[...], (((1,), (1,)), ((), ())), preferred_element_type=F32
-    ) * scaling
-    own_row = lax.broadcasted_iota(jnp.int32, (own_rows, lanes), 0)
-    own_lane = lax.broadcasted_iota(jnp.int32, (own_rows, lanes), 1)
-    own_kv = jnp.minimum((own_lane % SLOT) // group, kv - 1)
-    own_mask = (own_row // kv == own_lane // SLOT) & (own_row % kv == own_kv)
-    own = jnp.sum(jnp.where(own_mask, own_all, 0.0), axis=0, keepdims=True)
-    first = place == 0
-    own = jnp.where(first, own, F32(NEG_FILL))
-
     lane1 = lax.broadcasted_iota(jnp.int32, (1, lanes), 1)
     bound = jnp.zeros((1, lanes), jnp.int32)
     for b in range(batch):
@@ -157,31 +148,48 @@
     def rotate_keys(c):
         part = slice(c * chunk, (c + 1) * chunk)
         for b in range(batch):
-            k = kbuf[b, part, :].astype(F32)
-            kcats[c % 2][b] = rotate(k, tab[0, part, :], tab[1, part, :]).astype(BF16)
+            k = kbuf[b, part, :]
+            turned = pltpu.roll(k, width // 2, 1).astype(F32)
+            k = k.astype(F32) * tab[0, part, :] + turned * tab[1, part, :]
+            kcats[c % 2][b] = k.astype(BF16)
 
     def score(c, top):
-        keys = jnp.concatenate([kcats[c % 2][b] for b in range(batch)], axis=1)
-        s = lax.dot_general(
-            keys, qbd[...], (((1,), (1,)), ((), ())), preferred_element_type=F32
-        ) * scaling
+        sums = []
+        for g in range(2):
+            keys = jnp.concatenate([kcats[c % 2][b, g*chunk//2:(g+1)*chunk//2] for b in range(batch)], axis=1)
+            sums.append(lax.dot_general(
+                keys, qbd[...],
+                (((1,), (1,)), ((), ())), preferred_element_type=F32,
+            ))
+        s = jnp.concatenate(sums, axis=0) * scaling
         s = jnp.where(fits & (row_c + c * chunk < bound), s, F32(NEG_FILL))
         scores[c * chunk : (c + 1) * chunk, :] = s
         return jnp.maximum(top, jnp.max(s, axis=0, keepdims=True))
 
-    top = own
     for c in range(chunks):
-        if whole_stretch:
-            tcopy(c).wait()
         kcopy(c).wait()
-        if c == 0:
-            for i in range(pairs):
-                vcopy(i).start()
         if c == chunks - 1:
             wcopy.start()
         rotate_keys(c)
+        if c == 1:
+            own_rows = batch * kv
+            knew = jnp.concatenate(
+                [rotate(nkbuf[b].astype(F32), cr[b : b + 1], sr[b : b + 1]) for b in range(batch)], axis=0
+            ).astype(BF16)
+            own_all = lax.dot_general(
+                knew, qin[...], (((1,), (1,)), ((), ())), preferred_element_type=F32
+            ) * scaling
+            own_row = lax.broadcasted_iota(jnp.int32, (own_rows, lanes), 0)
+            own_lane = lax.broadcasted_iota(jnp.int32, (own_rows, lanes), 1)
+            own_kv = jnp.minimum((own_lane % SLOT) // group, kv - 1)
+            own_mask = (own_row // kv == own_lane // SLOT) & (own_row % kv == own_kv)
+            own = jnp.sum(jnp.where(own_mask, own_all, 0.0), axis=0, keepdims=True)
+            first = place == 0
+            own = jnp.where(first, own, F32(NEG_FILL))
+            top = own
         if c:
             top = score(c - 1, top)
+    vcopy.wait()
     top = score(chunks - 1, top)
 
     own_w = jnp.where(first, jnp.exp(own - top), 0.0)
@@ -194,7 +202,6 @@
         parts.append(jnp.transpose(w.astype(BF16)))
     wt = jnp.concatenate(parts, axis=1)
 
-    nvcopy.wait()
     own_wt = jnp.transpose(jnp.where(own_mask, own_w, 0.0))
     nv = jnp.concatenate([nvbuf[b].astype(F32) for b in range(batch)], axis=0)
     own_acc = lax.dot_general(
@@ -202,8 +209,6 @@
         precision=lax.Precision.HIGHEST,
     )
 
-    for c in range(pairs):
-        vcopy(c).wait()
     for c in range(pairs):
         v = jnp.concatenate([vbuf[2 * c], vbuf[2 * c + 1]], axis=1)
         acc = jnp.dot(wt[2 * c * SLOT : (2 * c + 2) * SLOT, :], v, preferred_element_type=F32)
@@ -283,14 +288,12 @@
     return [value] + [lax.ppermute(value, axis, [(i, i ^ d) for i in range(size)]) for d in distances]
 
 
-def rope_tables(span, kv, width):
+def rope_table(span, width):
     half = width // 2
     index = np.arange(half, dtype=np.float32)
     freq = np.exp(index * np.float32(-2.0 * math.log(THETA_BASE) / width)).astype(np.float32)
-    angle = np.arange(span, dtype=np.float32)[:, None] * freq
-    cos_part, sin_part = np.cos(angle.astype(np.float64)), np.sin(angle.astype(np.float64))
-    both = np.stack([np.concatenate([cos_part, cos_part], 1), np.concatenate([-sin_part, sin_part], 1)])
-    return np.repeat(both, kv, axis=1).astype(np.float32)
+    angle = (np.arange(span, dtype=np.float32)[:, None] * freq).astype(np.float64)
+    return np.concatenate([np.cos(angle), np.sin(angle)], axis=1).astype(np.float32)
 
 
 def body(query, key_cache, value_cache, new_key, new_value, lengths, out_weight):
@@ -303,9 +306,9 @@
     lanes = batch * SLOT
     packed_rows = heads * batch + batch
     if span == stretch:
-        tables = jnp.asarray(rope_tables(span, kv, width))
+        tables = jnp.asarray(rope_table(span, width))
     else:
-        tables = jnp.zeros((2, 8, width), F32)
+        tables = jnp.zeros((8, width), F32)
     dma = pltpu.SemaphoreType.DMA
     packed, weight = pl.pallas_call(
         functools.partial(attention_kernel, stretch=stretch, kv=kv, chunks=chunks),
@@ -313,6 +316,7 @@
         in_specs=[pl.BlockSpec(memory_space=pl.ANY)] * 8,
         out_specs=in_vmem(2),
         scratch_shapes=[
+            pltpu.VMEM(tables.shape, F32),
             pltpu.VMEM((2, rows, width), F32),
             pltpu.SMEM((batch,), jnp.int32),
             pltpu.VMEM((heads, batch, width), BF16),
@@ -326,7 +330,7 @@
             pltpu.VMEM((lanes, width), BF16),
             pltpu.VMEM((2, heads * batch, width), F32),
             pltpu.VMEM((rows, lanes), F32),
-            dma((chunks,)), dma((chunks,)), dma((batch // 2,)), dma, dma, dma, dma, dma,
+            dma, dma((chunks,)), dma, dma, dma, dma, dma, dma, pltpu.SemaphoreType.REGULAR,
         ],
         name="attention",
     )(

time: 23.4 us -> 22.6 us (0.966)
  Pallas kernels: 5.14 us -> 4.36 us
    pallas_call x1, Pallas kernels: 4.55 us -> 3.77 us  [body(): pl.pallas_call(functools.partial(attention_kernel, stretch=stretch, kv=kv...]
where the time goes in v4:
time: 22.6 us; the launch traced here: 22.5 us
  starting transfers between devices  9.28 us (41%)
  waiting for transfers between devices  8.21 us (36%)
  Pallas kernels  4.36 us (19%)
  other arithmetic  0.61 us (3%)
    ppermute x7, starting transfers between devices, gather_from(): lax.ppermute(value, axis, [(i, i ^ d) for i in range(size)])  9.28 us
    ppermute x7, waiting for transfers between devices, gather_from(): lax.ppermute(value, axis, [(i, i ^ d) for i in range(size)])  8.21 us
    pallas_call x1, Pallas kernels, body(): pl.pallas_call(functools.partial(attention_kernel, stretch=stretch, kv=kv...  3.77 us
    add x1, other arithmetic, balanced_sum(): values = [values[i] + values[i + 1] for i in range(0, len(values), 2)]  0.61 us
  transfers between devices with their start and end apart: 7, of which 6 were waited for; matrix products, arithmetic and copies ran while one was open for 0% of the time, Pallas kernels for 0%

profile of v4, /device:TPU:0, one launch (start us, length us, event | category | flops | bytes accessed | tf_op | source)
XLA Modules:
  0.0 22.5 jit_solution(6411553615925602406)
XLA Ops:
  0.0 3.8 %attention.1 = (f32[88,128]{1,0:T(8,128)S(1)}, bf16[1280,640]{1,0:T(8,128)(2,1)S(1)}) custom-call(f32[512,128]{1,0:T(8,128)} %constant.2.clone.tab_hbm, s32[8]{0:T(128)} %lens_hbm.1, bf16[10,8,128]{2,1,0:T(8,128)(2,1)} %bitcast.5, bf16[8,2,128]{2,1,0:T(2,128)(2,1)} %nk_hbm.1, bf16[8,2,128]{2,1,0:T(2,128)(2,1)} %nv_hbm.1, bf16[8,1024,128]{2,1,0:T(8,128)(2,1)} %bitcast.3, ...), custom_call_target="tpu_custom_call" | custom-call | tf_op jit(solution)/shard_map/attention/pallas_call | solution.py:313
  3.8 4.1 %collective-permute-start.2 = (f32[88,128]{1,0:T(8,128)S(1)}, f32[88,128]{1,0:T(8,128)S(1)}, u32[]{:S(2)}, u32[]{:S(2)}) collective-permute-start(f32[88,128]{1,0:T(8,128)S(1)} %get-tuple-element.7.refs_0_), channel_id=1, source_target_pairs={{0,12},{4,8},{8,4},{12,0},{16,28},{20,24},{24,20},{28,16},{1,13},{... | collective-permute-start | bytes 135176 | tf_op jit(solution)/shard_map/ppermute | solution.py:288
  7.9 0.5 %collective-permute-start.1 = (f32[88,128]{1,0:T(8,128)S(1)}, f32[88,128]{1,0:T(8,128)S(1)}, u32[]{:S(2)}, u32[]{:S(2)}) collective-permute-start(f32[88,128]{1,0:T(8,128)S(1)} %get-tuple-element.7.refs_0_), channel_id=1, source_target_pairs={{0,8},{4,12},{8,0},{12,4},{16,24},{20,28},{24,16},{28,20},{1,9},{5... | collective-permute-start | bytes 135176 | tf_op jit(solution)/shard_map/ppermute | solution.py:288
  8.3 0.2 collective-permute-start
  8.5 1.4 %collective-permute-done.2.refs_3_ = f32[88,128]{1,0:T(8,128)S(1)} collective-permute-done((f32[88,128]{1,0:T(8,128)S(1)}, f32[88,128]{1,0:T(8,128)S(1)}, u32[]{:S(2)}, u32[]{:S(2)}) %collective-permute-start.2) | collective-permute-done | bytes 45088 | tf_op jit(solution)/shard_map/ppermute | solution.py:288
  9.9 2.0 %collective-permute-done.1.refs_2_ = f32[88,128]{1,0:T(8,128)S(1)} collective-permute-done((f32[88,128]{1,0:T(8,128)S(1)}, f32[88,128]{1,0:T(8,128)S(1)}, u32[]{:S(2)}, u32[]{:S(2)}) %collective-permute-start.1) | collective-permute-done | bytes 45088 | tf_op jit(solution)/shard_map/ppermute | solution.py:288
  11.9 0.5 %collective-permute-done.refs_1_ = f32[88,128]{1,0:T(8,128)S(1)} collective-permute-done((f32[88,128]{1,0:T(8,128)S(1)}, f32[88,128]{1,0:T(8,128)S(1)}, u32[]{:S(2)}, u32[]{:S(2)}) %collective-permute-start) | collective-permute-done | bytes 45088 | tf_op jit(solution)/shard_map/ppermute | solution.py:288
  12.4 0.1 merge.1.refs_0_
  12.5 2.7 %collective-permute-start.3 = (f32[88,128]{1,0:T(8,128)S(1)}, f32[88,128]{1,0:T(8,128)S(1)}, u32[]{:S(2)}, u32[]{:S(2)}) collective-permute-start(f32[88,128]{1,0:T(8,128)S(1)} %merge.1.refs_0_), channel_id=1, source_target_pairs={{0,16},{4,20},{8,24},{12,28},{16,0},{20,4},{24,8},{28,12},{1,17},{... | collective-permute-start | bytes 135176 | tf_op jit(solution)/shard_map/ppermute | solution.py:288
  15.2 2.4 %collective-permute-done.3.refs_1_ = f32[88,128]{1,0:T(8,128)S(1)} collective-permute-done((f32[88,128]{1,0:T(8,128)S(1)}, f32[88,128]{1,0:T(8,128)S(1)}, u32[]{:S(2)}, u32[]{:S(2)}) %collective-permute-start.3) | collective-permute-done | bytes 45088 | tf_op jit(solution)/shard_map/ppermute | solution.py:288
  17.5 0.4 %project.1 = f32[8,640]{1,0:T(8,128)S(1)} custom-call(f32[88,128]{1,0:T(8,128)S(1)} %merge.1.refs_0_, f32[88,128]{1,0:T(8,128)S(1)} %collective-permute-done.3.refs_1_, bf16[1280,640]{1,0:T(8,128)(2,1)S(1)} %get-tuple-element.8.refs_2_), custom_call_target="tpu_custom_call" | custom-call | tf_op jit(solution)/shard_map/project/pallas_call | solution.py:352
  18.0 0.1 collective-permute-start.6
  18.0 1.6 %collective-permute-start.5 = (f32[8,640]{1,0:T(8,128)S(1)}, f32[8,640]{1,0:T(8,128)S(1)}, u32[]{:S(2)}, u32[]{:S(2)}) collective-permute-start(f32[8,640]{1,0:T(8,128)S(1)} %project.1), channel_id=1, source_target_pairs={{0,2},{1,3},{2,0},{3,1},{4,6},{5,7},{6,4},{7,5},{8,10},{9,11},{10,... | collective-permute-start | bytes 61448 | tf_op jit(solution)/shard_map/ppermute | solution.py:288
  19.6 0.3 %collective-permute-start.4 = (f32[8,640]{1,0:T(8,128)S(1)}, f32[8,640]{1,0:T(8,128)S(1)}, u32[]{:S(2)}, u32[]{:S(2)}) collective-permute-start(f32[8,640]{1,0:T(8,128)S(1)} %project.1), channel_id=1, source_target_pairs={{0,1},{1,0},{2,3},{3,2},{4,5},{5,4},{6,7},{7,6},{8,9},{9,8},{10,11... | collective-permute-start | bytes 61448 | tf_op jit(solution)/shard_map/ppermute | solution.py:288
  19.9 1.5 %collective-permute-done.6 = f32[8,640]{1,0:T(8,128)S(1)} collective-permute-done((f32[8,640]{1,0:T(8,128)S(1)}, f32[8,640]{1,0:T(8,128)S(1)}, u32[]{:S(2)}, u32[]{:S(2)}) %collective-permute-start.6) | collective-permute-done | bytes 20512 | tf_op jit(solution)/shard_map/ppermute | solution.py:288
  21.4 0.5 %collective-permute-done.5 = f32[8,640]{1,0:T(8,128)S(1)} collective-permute-done((f32[8,640]{1,0:T(8,128)S(1)}, f32[8,640]{1,0:T(8,128)S(1)}, u32[]{:S(2)}, u32[]{:S(2)}) %collective-permute-start.5) | collective-permute-done | bytes 20512 | tf_op jit(solution)/shard_map/ppermute | solution.py:288
  21.9 0.0 collective-permute-done.4
  21.9 0.6 %add_add_fusion = f32[8,640]{1,0:T(8,128)} fusion(f32[8,640]{1,0:T(8,128)S(1)} %collective-permute-done.5, f32[8,640]{1,0:T(8,128)S(1)} %collective-permute-done.6, f32[8,640]{1,0:T(8,128)S(1)} %project.1, f32[8,640]{1,0:T(8,128)S(1)} %collective-permute-done.4), kind=kLoop, calls=%fused_computation | loop fusion | flops 15360 | bytes 102400 | tf_op jit(solution)/shard_map/add | solution.py:234
Async XLA Ops:
  3.8 6.1 %collective-permute-start.2 = (f32[88,128]{1,0:T(8,128)S(1)}, f32[88,128]{1,0:T(8,128)S(1)}, u32[]{:S(2)}, u32[]{:S(2)}) collective-permute-start(f32[88,128]{1,0:T(8,128)S(1)} %get-tuple-element.7.refs_0_), channel_id=1, source_target_pairs={{0,12},{4,8},{8,4},{12,0},{16,28},{20,24},{24,20},{28,16},{1,13},{... | collective-permute-start | bytes 135176 | tf_op jit(solution)/shard_map/ppermute | solution.py:288
  7.9 4.0 %collective-permute-start.1 = (f32[88,128]{1,0:T(8,128)S(1)}, f32[88,128]{1,0:T(8,128)S(1)}, u32[]{:S(2)}, u32[]{:S(2)}) collective-permute-start(f32[88,128]{1,0:T(8,128)S(1)} %get-tuple-element.7.refs_0_), channel_id=1, source_target_pairs={{0,8},{4,12},{8,0},{12,4},{16,24},{20,28},{24,16},{28,20},{1,9},{5... | collective-permute-start | bytes 135176 | tf_op jit(solution)/shard_map/ppermute | solution.py:288
  8.3 4.0 %collective-permute-start = (f32[88,128]{1,0:T(8,128)S(1)}, f32[88,128]{1,0:T(8,128)S(1)}, u32[]{:S(2)}, u32[]{:S(2)}) collective-permute-start(f32[88,128]{1,0:T(8,128)S(1)} %get-tuple-element.7.refs_0_), channel_id=1, source_target_pairs={{0,4},{4,0},{8,12},{12,8},{16,20},{20,16},{24,28},{28,24},{1,5},{5... | collective-permute-start | bytes 135176 | tf_op jit(solution)/shard_map/ppermute | solution.py:288
  12.5 5.0 %collective-permute-start.3 = (f32[88,128]{1,0:T(8,128)S(1)}, f32[88,128]{1,0:T(8,128)S(1)}, u32[]{:S(2)}, u32[]{:S(2)}) collective-permute-start(f32[88,128]{1,0:T(8,128)S(1)} %merge.1.refs_0_), channel_id=1, source_target_pairs={{0,16},{4,20},{8,24},{12,28},{16,0},{20,4},{24,8},{28,12},{1,17},{... | collective-permute-start | bytes 135176 | tf_op jit(solution)/shard_map/ppermute | solution.py:288
  18.0 3.4 %collective-permute-start.6 = (f32[8,640]{1,0:T(8,128)S(1)}, f32[8,640]{1,0:T(8,128)S(1)}, u32[]{:S(2)}, u32[]{:S(2)}) collective-permute-start(f32[8,640]{1,0:T(8,128)S(1)} %project.1), channel_id=1, source_target_pairs={{0,3},{1,2},{2,1},{3,0},{4,7},{5,6},{6,5},{7,4},{8,11},{9,10},{10,... | collective-permute-start | bytes 61448 | tf_op jit(solution)/shard_map/ppermute | solution.py:288
  18.0 3.8 %collective-permute-start.5 = (f32[8,640]{1,0:T(8,128)S(1)}, f32[8,640]{1,0:T(8,128)S(1)}, u32[]{:S(2)}, u32[]{:S(2)}) collective-permute-start(f32[8,640]{1,0:T(8,128)S(1)} %project.1), channel_id=1, source_target_pairs={{0,2},{1,3},{2,0},{3,1},{4,6},{5,7},{6,4},{7,5},{8,10},{9,11},{10,... | collective-permute-start | bytes 61448 | tf_op jit(solution)/shard_map/ppermute | solution.py:288
  19.6 2.3 %collective-permute-start.4 = (f32[8,640]{1,0:T(8,128)S(1)}, f32[8,640]{1,0:T(8,128)S(1)}, u32[]{:S(2)}, u32[]{:S(2)}) collective-permute-start(f32[8,640]{1,0:T(8,128)S(1)} %project.1), channel_id=1, source_target_pairs={{0,1},{1,0},{2,3},{3,2},{4,5},{5,4},{6,7},{7,6},{8,9},{9,8},{10,11... | collective-permute-start | bytes 61448 | tf_op jit(solution)/shard_map/ppermute | solution.py:288

commit v5 on v4

--- a/solution.py
+++ b/solution.py
@@ -7,10 +7,10 @@
 from jax.experimental import pallas as pl
 from jax.experimental.pallas import tpu as pltpu
 from jax.sharding import PartitionSpec as P
-import numpy as np
 
 THETA_BASE = 10000000.0
 NEG_FILL = -1e30
+RUN = 32
 SLOT = 16
 F32 = jnp.float32
 BF16 = jnp.bfloat16
@@ -42,28 +42,27 @@
 
 
 def attention_kernel(
-    tab_hbm, lens_hbm, q_hbm, nk_hbm, nv_hbm, k_hbm, v_hbm, w_hbm,
+    lens_hbm, q_hbm, nk_hbm, nv_hbm, k_hbm, v_hbm, w_hbm,
     out_ref, w_ref,
-    tab_raw, tab, lens, qbuf, nkbuf, nvbuf, kbuf, vbuf, kcat0, kcat1, qbd, qin, qrot, scores,
-    tsem, ksem, vsem, lsem, qsem, nksem, nvsem, wsem, order,
-    *, stretch, kv, chunks,
+    tab, lens, qbuf, nkbuf, nvbuf, kbuf, vbuf, kcat0, kcat1, qbd, qin, qrot, scores,
+    ksem, vsem, lsem, qsem, nksem, nvsem, wsem, order,
+    *, stretch, kv, sizes,
 ):
     batch, rows, width = kbuf.shape
     heads = qbuf.shape[0]
     group = heads // kv
     lanes = batch * SLOT
     span = rows // kv
-    chunk = rows // chunks
+    chunks = len(sizes)
+    parts_at = [slice(sum(sizes[:c]), sum(sizes[: c + 1])) for c in range(chunks)]
     pairs = batch // 2
-    whole_stretch = span == stretch
     kcats = (kcat0, kcat1)
 
     def kcopy(c):
-        part = pl.ds(c * chunk, chunk)
+        part = pl.ds(parts_at[c].start, sizes[c])
         return pltpu.make_async_copy(k_hbm.at[:, part, :], kbuf.at[:, part, :], ksem.at[c])
 
     vcopy = pltpu.make_async_copy(v_hbm, vbuf, vsem)
-    tcopy = pltpu.make_async_copy(tab_hbm, tab_raw, tsem)
     wcopy = pltpu.make_async_copy(w_hbm, w_ref, wsem)
 
     lcopy = pltpu.make_async_copy(lens_hbm, lens, lsem)
@@ -73,8 +72,6 @@
     small = (lcopy, qcopy, nkcopy, nvcopy)
     for copy in small:
         copy.start()
-    if whole_stretch:
-        tcopy.start()
     pl.semaphore_signal(order, 1)
     pl.semaphore_wait(order, 1)
     for c in range(chunks):
@@ -89,25 +86,25 @@
     qin[...] = jnp.zeros_like(qin)
     freq8 = frequencies((batch, width))
     sign8 = half_sign((batch, width))
-    if not whole_stretch:
-        row = lax.broadcasted_iota(jnp.int32, (rows, width), 0)
-        angle = (base % stretch + row // kv).astype(F32) * frequencies((rows, width))
-        tab[0] = jnp.cos(angle)
-        tab[1] = jnp.sin(angle) * half_sign((rows, width))
+
+    runs = span // RUN
+    start = (base % stretch).astype(F32)
+    far = start + (RUN * lax.broadcasted_iota(jnp.int32, (runs, width), 0)).astype(F32)
+    far = far * frequencies((runs, width))
+    far_c, far_s = jnp.cos(far), jnp.sin(far) * half_sign((runs, width))
+    near = lax.broadcasted_iota(jnp.int32, (RUN, width), 0).astype(F32) * frequencies((RUN, width))
+    near_c, near_signed = jnp.cos(near), jnp.sin(near) * half_sign((RUN, width))
+    for i in range(runs):
+        c_i, s_i = far_c[i : i + 1], far_s[i : i + 1]
+        cos_part = c_i * near_c - s_i * near_signed
+        sin_part = s_i * near_c + c_i * near_signed
+        for j in range(kv):
+            at = pl.ds(RUN * kv * i + j, RUN, stride=kv)
+            tab[0, at, :] = cos_part
+            tab[1, at, :] = sin_part
 
     for copy in small:
         copy.wait()
-    if whole_stretch:
-        tcopy.wait()
-        lower = lax.broadcasted_iota(jnp.int32, (8, width), 1) < width // 2
-        for i in range(span // 8):
-            t = tab_raw[8 * i : 8 * i + 8, :]
-            other = pltpu.roll(t, width // 2, 1)
-            cos_part, sin_part = jnp.where(lower, t, other), jnp.where(lower, -other, t)
-            for j in range(kv):
-                at = pl.ds(8 * kv * i + j, 8, stride=kv)
-                tab[0, at, :] = cos_part
-                tab[1, at, :] = sin_part
     picked, intra, limit = [], [], []
     for b in range(batch):
         p = lens[b]
@@ -142,28 +139,27 @@
     for b in range(batch):
         bound = jnp.where(lane1 // SLOT == b, limit[b], bound)
     lane_kv = jnp.minimum((lane1 % SLOT) // group, kv - 1)
-    row_c = lax.broadcasted_iota(jnp.int32, (chunk, lanes), 0)
-    fits = row_c % kv == lane_kv
 
     def rotate_keys(c):
-        part = slice(c * chunk, (c + 1) * chunk)
+        part = parts_at[c]
         for b in range(batch):
             k = kbuf[b, part, :]
             turned = pltpu.roll(k, width // 2, 1).astype(F32)
             k = k.astype(F32) * tab[0, part, :] + turned * tab[1, part, :]
-            kcats[c % 2][b] = k.astype(BF16)
+            kcats[c % 2][b, : sizes[c], :] = k.astype(BF16)
 
     def score(c, top):
+        half = sizes[c] // 2
         sums = []
-        for g in range(2):
-            keys = jnp.concatenate([kcats[c % 2][b, g*chunk//2:(g+1)*chunk//2] for b in range(batch)], axis=1)
+        for part in (slice(0, half), slice(half, sizes[c])):
+            keys = jnp.concatenate([kcats[c % 2][b, part, :] for b in range(batch)], axis=1)
             sums.append(lax.dot_general(
-                keys, qbd[...],
-                (((1,), (1,)), ((), ())), preferred_element_type=F32,
+                keys, qbd[...], (((1,), (1,)), ((), ())), preferred_element_type=F32
             ))
         s = jnp.concatenate(sums, axis=0) * scaling
-        s = jnp.where(fits & (row_c + c * chunk < bound), s, F32(NEG_FILL))
-        scores[c * chunk : (c + 1) * chunk, :] = s
+        row = parts_at[c].start + lax.broadcasted_iota(jnp.int32, s.shape, 0)
+        s = jnp.where((row % kv == lane_kv) & (row < bound), s, F32(NEG_FILL))
+        scores[parts_at[c], :] = s
         return jnp.maximum(top, jnp.max(s, axis=0, keepdims=True))
 
     for c in range(chunks):
@@ -196,7 +192,7 @@
     total = own_w
     parts = []
     for c in range(chunks):
-        s = scores[c * chunk : (c + 1) * chunk, :]
+        s = scores[parts_at[c], :]
         w = jnp.where(s > F32(0.5 * NEG_FILL), jnp.exp(s - top), 0.0)
         total = total + jnp.sum(w, axis=0, keepdims=True)
         parts.append(jnp.transpose(w.astype(BF16)))
@@ -288,35 +284,22 @@
     return [value] + [lax.ppermute(value, axis, [(i, i ^ d) for i in range(size)]) for d in distances]
 
 
-def rope_table(span, width):
-    half = width // 2
-    index = np.arange(half, dtype=np.float32)
-    freq = np.exp(index * np.float32(-2.0 * math.log(THETA_BASE) / width)).astype(np.float32)
-    angle = (np.arange(span, dtype=np.float32)[:, None] * freq).astype(np.float64)
-    return np.concatenate([np.cos(angle), np.sin(angle)], axis=1).astype(np.float32)
-
-
 def body(query, key_cache, value_cache, new_key, new_value, lengths, out_weight):
     seq_count = lax.axis_size("seq")
     batch, span, kv, width = key_cache.shape
     heads = query.shape[1]
     stretch = span * seq_count // 8
     rows = span * kv
-    chunks = 4
+    sizes = [rows * n // 16 for n in (4, 5, 7)]
     lanes = batch * SLOT
     packed_rows = heads * batch + batch
-    if span == stretch:
-        tables = jnp.asarray(rope_table(span, width))
-    else:
-        tables = jnp.zeros((8, width), F32)
     dma = pltpu.SemaphoreType.DMA
     packed, weight = pl.pallas_call(
-        functools.partial(attention_kernel, stretch=stretch, kv=kv, chunks=chunks),
+        functools.partial(attention_kernel, stretch=stretch, kv=kv, sizes=sizes),
         out_shape=[pltpu.VMEM((packed_rows, width), F32), pltpu.VMEM(out_weight.shape, BF16)],
-        in_specs=[pl.BlockSpec(memory_space=pl.ANY)] * 8,
+        in_specs=[pl.BlockSpec(memory_space=pl.ANY)] * 7,
         out_specs=in_vmem(2),
         scratch_shapes=[
-            pltpu.VMEM(tables.shape, F32),
             pltpu.VMEM((2, rows, width), F32),
             pltpu.SMEM((batch,), jnp.int32),
             pltpu.VMEM((heads, batch, width), BF16),
@@ -324,17 +307,17 @@
             pltpu.VMEM((batch, kv, width), BF16),
             pltpu.VMEM((batch, rows, width), BF16),
             pltpu.VMEM((batch, rows, width), BF16),
-            pltpu.VMEM((batch, rows // chunks, width), BF16),
-            pltpu.VMEM((batch, rows // chunks, width), BF16),
+            pltpu.VMEM((batch, max(sizes), width), BF16),
+            pltpu.VMEM((batch, max(sizes), width), BF16),
             pltpu.VMEM((lanes, batch * width), BF16),
             pltpu.VMEM((lanes, width), BF16),
             pltpu.VMEM((2, heads * batch, width), F32),
             pltpu.VMEM((rows, lanes), F32),
-            dma, dma((chunks,)), dma, dma, dma, dma, dma, dma, pltpu.SemaphoreType.REGULAR,
+            dma((len(sizes),)), dma, dma, dma, dma, dma, dma, pltpu.SemaphoreType.REGULAR,
         ],
         name="attention",
     )(
-        tables, lengths, jnp.transpose(query, (1, 0, 2)), new_key, new_value,
+        lengths, jnp.transpose(query, (1, 0, 2)), new_key, new_value,
         key_cache.reshape(batch, rows, width), value_cache.reshape(batch, rows, width),
         out_weight,
     )

time: 22.6 us -> 22.3 us (0.987)
  Pallas kernels: 4.36 us -> 4 us
    pallas_call x1, Pallas kernels: 3.77 us -> 3.41 us  [body(): pl.pallas_call(functools.partial(attention_kernel, stretch=stretch, kv=kv...]
where the time goes in v5:
time: 22.3 us; the launch traced here: 22.1 us
  starting transfers between devices  9.28 us (42%)
  waiting for transfers between devices  8.2 us (37%)
  Pallas kernels  4 us (18%)
  other arithmetic  0.61 us (3%)
    ppermute x7, starting transfers between devices, gather_from(): lax.ppermute(value, axis, [(i, i ^ d) for i in range(size)])  9.28 us
    ppermute x7, waiting for transfers between devices, gather_from(): lax.ppermute(value, axis, [(i, i ^ d) for i in range(size)])  8.2 us
    pallas_call x1, Pallas kernels, body(): pl.pallas_call(functools.partial(attention_kernel, stretch=stretch, kv=kv...  3.41 us
    add x1, other arithmetic, balanced_sum(): values = [values[i] + values[i + 1] for i in range(0, len(values), 2)]  0.61 us
    pallas_call x1, Pallas kernels, body(): pl.pallas_call(functools.partial(project_kernel, heads=heads, batch=batch...  0.45 us
  transfers between devices with their start and end apart: 7, of which 6 were waited for; matrix products, arithmetic and copies ran while one was open for 0% of the time, Pallas kernels for 0%

profile of v5, /device:TPU:0, one launch (start us, length us, event | category | flops | bytes accessed | tf_op | source)
XLA Modules:
  0.0 22.1 jit_solution(7993391885152887779)
XLA Ops:
  0.0 3.4 %attention.1 = (f32[88,128]{1,0:T(8,128)S(1)}, bf16[1280,640]{1,0:T(8,128)(2,1)S(1)}) custom-call(s32[8]{0:T(128)} %lens_hbm.1, bf16[10,8,128]{2,1,0:T(8,128)(2,1)} %bitcast.5, bf16[8,2,128]{2,1,0:T(2,128)(2,1)} %nk_hbm.1, bf16[8,2,128]{2,1,0:T(2,128)(2,1)} %nv_hbm.1, bf16[8,1024,128]{2,1,0:T(8,128)(2,1)} %bitcast.3, bf16[8,1024,128]{2,1,0:T(8,128)(2,1)} %bitcast.4, ...), custom_call_target="tpu_custom_call" | custom-call | tf_op jit(solution)/shard_map/attention/pallas_call | solution.py:297
  3.4 4.1 %collective-permute-start.2 = (f32[88,128]{1,0:T(8,128)S(1)}, f32[88,128]{1,0:T(8,128)S(1)}, u32[]{:S(2)}, u32[]{:S(2)}) collective-permute-start(f32[88,128]{1,0:T(8,128)S(1)} %get-tuple-element.7.refs_0_), channel_id=1, source_target_pairs={{0,12},{4,8},{8,4},{12,0},{16,28},{20,24},{24,20},{28,16},{1,13},{... | collective-permute-start | bytes 135176 | tf_op jit(solution)/shard_map/ppermute | solution.py:284
  7.5 0.4 %collective-permute-start.1 = (f32[88,128]{1,0:T(8,128)S(1)}, f32[88,128]{1,0:T(8,128)S(1)}, u32[]{:S(2)}, u32[]{:S(2)}) collective-permute-start(f32[88,128]{1,0:T(8,128)S(1)} %get-tuple-element.7.refs_0_), channel_id=1, source_target_pairs={{0,8},{4,12},{8,0},{12,4},{16,24},{20,28},{24,16},{28,20},{1,9},{5... | collective-permute-start | bytes 135176 | tf_op jit(solution)/shard_map/ppermute | solution.py:284
  7.9 0.2 collective-permute-start
  8.1 1.4 %collective-permute-done.2.refs_3_ = f32[88,128]{1,0:T(8,128)S(1)} collective-permute-done((f32[88,128]{1,0:T(8,128)S(1)}, f32[88,128]{1,0:T(8,128)S(1)}, u32[]{:S(2)}, u32[]{:S(2)}) %collective-permute-start.2) | collective-permute-done | bytes 45088 | tf_op jit(solution)/shard_map/ppermute | solution.py:284
  9.5 2.0 %collective-permute-done.1.refs_2_ = f32[88,128]{1,0:T(8,128)S(1)} collective-permute-done((f32[88,128]{1,0:T(8,128)S(1)}, f32[88,128]{1,0:T(8,128)S(1)}, u32[]{:S(2)}, u32[]{:S(2)}) %collective-permute-start.1) | collective-permute-done | bytes 45088 | tf_op jit(solution)/shard_map/ppermute | solution.py:284
  11.5 0.4 %collective-permute-done.refs_1_ = f32[88,128]{1,0:T(8,128)S(1)} collective-permute-done((f32[88,128]{1,0:T(8,128)S(1)}, f32[88,128]{1,0:T(8,128)S(1)}, u32[]{:S(2)}, u32[]{:S(2)}) %collective-permute-start) | collective-permute-done | bytes 45088 | tf_op jit(solution)/shard_map/ppermute | solution.py:284
  12.0 0.1 merge.1.refs_0_
  12.1 2.7 %collective-permute-start.3 = (f32[88,128]{1,0:T(8,128)S(1)}, f32[88,128]{1,0:T(8,128)S(1)}, u32[]{:S(2)}, u32[]{:S(2)}) collective-permute-start(f32[88,128]{1,0:T(8,128)S(1)} %merge.1.refs_0_), channel_id=1, source_target_pairs={{0,16},{4,20},{8,24},{12,28},{16,0},{20,4},{24,8},{28,12},{1,17},{... | collective-permute-start | bytes 135176 | tf_op jit(solution)/shard_map/ppermute | solution.py:284
  14.8 2.4 %collective-permute-done.3.refs_1_ = f32[88,128]{1,0:T(8,128)S(1)} collective-permute-done((f32[88,128]{1,0:T(8,128)S(1)}, f32[88,128]{1,0:T(8,128)S(1)}, u32[]{:S(2)}, u32[]{:S(2)}) %collective-permute-start.3) | collective-permute-done | bytes 45088 | tf_op jit(solution)/shard_map/ppermute | solution.py:284
  17.1 0.4 %project.1 = f32[8,640]{1,0:T(8,128)S(1)} custom-call(f32[88,128]{1,0:T(8,128)S(1)} %merge.1.refs_0_, f32[88,128]{1,0:T(8,128)S(1)} %collective-permute-done.3.refs_1_, bf16[1280,640]{1,0:T(8,128)(2,1)S(1)} %get-tuple-element.8.refs_2_), custom_call_target="tpu_custom_call" | custom-call | tf_op jit(solution)/shard_map/project/pallas_call | solution.py:335
  17.6 0.1 collective-permute-start.6
  17.7 1.6 %collective-permute-start.5 = (f32[8,640]{1,0:T(8,128)S(1)}, f32[8,640]{1,0:T(8,128)S(1)}, u32[]{:S(2)}, u32[]{:S(2)}) collective-permute-start(f32[8,640]{1,0:T(8,128)S(1)} %project.1), channel_id=1, source_target_pairs={{0,2},{1,3},{2,0},{3,1},{4,6},{5,7},{6,4},{7,5},{8,10},{9,11},{10,... | collective-permute-start | bytes 61448 | tf_op jit(solution)/shard_map/ppermute | solution.py:284
  19.2 0.3 %collective-permute-start.4 = (f32[8,640]{1,0:T(8,128)S(1)}, f32[8,640]{1,0:T(8,128)S(1)}, u32[]{:S(2)}, u32[]{:S(2)}) collective-permute-start(f32[8,640]{1,0:T(8,128)S(1)} %project.1), channel_id=1, source_target_pairs={{0,1},{1,0},{2,3},{3,2},{4,5},{5,4},{6,7},{7,6},{8,9},{9,8},{10,11... | collective-permute-start | bytes 61448 | tf_op jit(solution)/shard_map/ppermute | solution.py:284
  19.5 1.5 %collective-permute-done.6 = f32[8,640]{1,0:T(8,128)S(1)} collective-permute-done((f32[8,640]{1,0:T(8,128)S(1)}, f32[8,640]{1,0:T(8,128)S(1)}, u32[]{:S(2)}, u32[]{:S(2)}) %collective-permute-start.6) | collective-permute-done | bytes 20512 | tf_op jit(solution)/shard_map/ppermute | solution.py:284
  21.0 0.5 %collective-permute-done.5 = f32[8,640]{1,0:T(8,128)S(1)} collective-permute-done((f32[8,640]{1,0:T(8,128)S(1)}, f32[8,640]{1,0:T(8,128)S(1)}, u32[]{:S(2)}, u32[]{:S(2)}) %collective-permute-start.5) | collective-permute-done | bytes 20512 | tf_op jit(solution)/shard_map/ppermute | solution.py:284
  21.5 0.0 collective-permute-done.4
  21.5 0.6 %add_add_fusion = f32[8,640]{1,0:T(8,128)} fusion(f32[8,640]{1,0:T(8,128)S(1)} %collective-permute-done.5, f32[8,640]{1,0:T(8,128)S(1)} %collective-permute-done.6, f32[8,640]{1,0:T(8,128)S(1)} %project.1, f32[8,640]{1,0:T(8,128)S(1)} %collective-permute-done.4), kind=kLoop, calls=%fused_computation | loop fusion | flops 15360 | bytes 102400 | tf_op jit(solution)/shard_map/add | solution.py:230
Async XLA Ops:
  3.4 6.1 %collective-permute-start.2 = (f32[88,128]{1,0:T(8,128)S(1)}, f32[88,128]{1,0:T(8,128)S(1)}, u32[]{:S(2)}, u32[]{:S(2)}) collective-permute-start(f32[88,128]{1,0:T(8,128)S(1)} %get-tuple-element.7.refs_0_), channel_id=1, source_target_pairs={{0,12},{4,8},{8,4},{12,0},{16,28},{20,24},{24,20},{28,16},{1,13},{... | collective-permute-start | bytes 135176 | tf_op jit(solution)/shard_map/ppermute | solution.py:284
  7.5 4.0 %collective-permute-start.1 = (f32[88,128]{1,0:T(8,128)S(1)}, f32[88,128]{1,0:T(8,128)S(1)}, u32[]{:S(2)}, u32[]{:S(2)}) collective-permute-start(f32[88,128]{1,0:T(8,128)S(1)} %get-tuple-element.7.refs_0_), channel_id=1, source_target_pairs={{0,8},{4,12},{8,0},{12,4},{16,24},{20,28},{24,16},{28,20},{1,9},{5... | collective-permute-start | bytes 135176 | tf_op jit(solution)/shard_map/ppermute | solution.py:284
  7.9 4.0 %collective-permute-start = (f32[88,128]{1,0:T(8,128)S(1)}, f32[88,128]{1,0:T(8,128)S(1)}, u32[]{:S(2)}, u32[]{:S(2)}) collective-permute-start(f32[88,128]{1,0:T(8,128)S(1)} %get-tuple-element.7.refs_0_), channel_id=1, source_target_pairs={{0,4},{4,0},{8,12},{12,8},{16,20},{20,16},{24,28},{28,24},{1,5},{5... | collective-permute-start | bytes 135176 | tf_op jit(solution)/shard_map/ppermute | solution.py:284
  12.1 5.0 %collective-permute-start.3 = (f32[88,128]{1,0:T(8,128)S(1)}, f32[88,128]{1,0:T(8,128)S(1)}, u32[]{:S(2)}, u32[]{:S(2)}) collective-permute-start(f32[88,128]{1,0:T(8,128)S(1)} %merge.1.refs_0_), channel_id=1, source_target_pairs={{0,16},{4,20},{8,24},{12,28},{16,0},{20,4},{24,8},{28,12},{1,17},{... | collective-permute-start | bytes 135176 | tf_op jit(solution)/shard_map/ppermute | solution.py:284
  17.6 3.4 %collective-permute-start.6 = (f32[8,640]{1,0:T(8,128)S(1)}, f32[8,640]{1,0:T(8,128)S(1)}, u32[]{:S(2)}, u32[]{:S(2)}) collective-permute-start(f32[8,640]{1,0:T(8,128)S(1)} %project.1), channel_id=1, source_target_pairs={{0,3},{1,2},{2,1},{3,0},{4,7},{5,6},{6,5},{7,4},{8,11},{9,10},{10,... | collective-permute-start | bytes 61448 | tf_op jit(solution)/shard_map/ppermute | solution.py:284
  17.7 3.8 %collective-permute-start.5 = (f32[8,640]{1,0:T(8,128)S(1)}, f32[8,640]{1,0:T(8,128)S(1)}, u32[]{:S(2)}, u32[]{:S(2)}) collective-permute-start(f32[8,640]{1,0:T(8,128)S(1)} %project.1), channel_id=1, source_target_pairs={{0,2},{1,3},{2,0},{3,1},{4,6},{5,7},{6,4},{7,5},{8,10},{9,11},{10,... | collective-permute-start | bytes 61448 | tf_op jit(solution)/shard_map/ppermute | solution.py:284
  19.2 2.3 %collective-permute-start.4 = (f32[8,640]{1,0:T(8,128)S(1)}, f32[8,640]{1,0:T(8,128)S(1)}, u32[]{:S(2)}, u32[]{:S(2)}) collective-permute-start(f32[8,640]{1,0:T(8,128)S(1)} %project.1), channel_id=1, source_target_pairs={{0,1},{1,0},{2,3},{3,2},{4,5},{5,4},{6,7},{7,6},{8,9},{9,8},{10,11... | collective-permute-start | bytes 61448 | tf_op jit(solution)/shard_map/ppermute | solution.py:284

commit v6 on v5

--- a/solution.py
+++ b/solution.py
@@ -279,9 +279,15 @@
     return steps
 
 
-def gather_from(value, axis, distances):
+def gather_from(value, axis, distances, ring=False):
     size = lax.axis_size(axis)
-    return [value] + [lax.ppermute(value, axis, [(i, i ^ d) for i in range(size)]) for d in distances]
+    moves = [[(i, i ^ d) for i in range(size)] for d in distances]
+    if ring and len(distances) == 3:
+        low = distances[0]
+        after = (1, 3, 0, 2)
+        onward = [(i, i + low * (after[i // low % 4] - i // low % 4)) for i in range(size)]
+        moves = [moves[2], onward, [(b, a) for a, b in onward]]
+    return [value] + [lax.ppermute(value, axis, pairs) for pairs in moves]
 
 
 def body(query, key_cache, value_cache, new_key, new_value, lengths, out_weight):
@@ -323,7 +329,7 @@
     )
     steps = exchange_steps("seq")
     for distances in steps[:-1]:
-        parts = gather_from(packed, "seq", distances)
+        parts = gather_from(packed, "seq", distances, ring=True)
         packed = pl.pallas_call(
             functools.partial(merge_kernel, heads=heads, batch=batch),
             out_shape=pltpu.VMEM(packed.shape, F32),
@@ -331,7 +337,7 @@
             out_specs=in_vmem(1)[0],
             name="merge",
         )(*map(vmem, parts))
-    parts = gather_from(packed, "seq", steps[-1])
+    parts = gather_from(packed, "seq", steps[-1], ring=True)
     share = pl.pallas_call(
         functools.partial(project_kernel, heads=heads, batch=batch),
         out_shape=pltpu.VMEM((batch, out_weight.shape[1]), F32),

time: 22.3 us -> 22.1 us (level)
  waiting for transfers between devices: 8.2 us -> 5.97 us
  starting transfers between devices: 9.28 us -> 11.1 us
    ppermute x7, waiting for transfers between devices: 8.2 us -> 5.97 us  [gather_from(): return [value] + [lax.ppermute(value, axis, pairs) for pairs in moves]]
    ppermute x7, starting transfers between devices: 9.28 us -> 11.1 us  [gather_from(): return [value] + [lax.ppermute(value, axis, pairs) for pairs in moves]]
  transfers between devices with their start and end apart: 7 -> 7, of which waited for: 6 -> 5; matrix products, arithmetic and copies ran while one was open for 0% -> 0% of each run, Pallas kernels for 0% -> 0%
where the time goes in v6:
time: 22.1 us; the launch traced here: 21.7 us
  starting transfers between devices  11.1 us (50%)
  waiting for transfers between devices  5.97 us (27%)
  Pallas kernels  4 us (18%)
  other arithmetic  0.61 us (3%)
    ppermute x7, starting transfers between devices, gather_from(): return [value] + [lax.ppermute(value, axis, pairs) for pairs in moves]  11.1 us
    ppermute x7, waiting for transfers between devices, gather_from(): return [value] + [lax.ppermute(value, axis, pairs) for pairs in moves]  5.97 us
    pallas_call x1, Pallas kernels, body(): pl.pallas_call(functools.partial(attention_kernel, stretch=stretch, kv=kv...  3.41 us
    add x1, other arithmetic, balanced_sum(): values = [values[i] + values[i + 1] for i in range(0, len(values), 2)]  0.61 us
    pallas_call x1, Pallas kernels, body(): pl.pallas_call(functools.partial(project_kernel, heads=heads, batch=batch...  0.45 us
  transfers between devices with their start and end apart: 7, of which 5 were waited for; matrix products, arithmetic and copies ran while one was open for 0% of the time, Pallas kernels for 0%

profile of v6, /device:TPU:0, one launch (start us, length us, event | category | flops | bytes accessed | tf_op | source)
XLA Modules:
  0.0 21.7 jit_solution(891511263606711543)
XLA Ops:
  0.0 3.4 %attention.1 = (f32[88,128]{1,0:T(8,128)S(1)}, bf16[1280,640]{1,0:T(8,128)(2,1)S(1)}) custom-call(s32[8]{0:T(128)} %lens_hbm.1, bf16[10,8,128]{2,1,0:T(8,128)(2,1)} %bitcast.5, bf16[8,2,128]{2,1,0:T(2,128)(2,1)} %nk_hbm.1, bf16[8,2,128]{2,1,0:T(2,128)(2,1)} %nv_hbm.1, bf16[8,1024,128]{2,1,0:T(8,128)(2,1)} %bitcast.3, bf16[8,1024,128]{2,1,0:T(8,128)(2,1)} %bitcast.4, ...), custom_call_target="tpu_custom_call" | custom-call | tf_op jit(solution)/shard_map/attention/pallas_call | solution.py:303
  3.4 3.1 %collective-permute-start.2 = (f32[88,128]{1,0:T(8,128)S(1)}, f32[88,128]{1,0:T(8,128)S(1)}, u32[]{:S(2)}, u32[]{:S(2)}) collective-permute-start(f32[88,128]{1,0:T(8,128)S(1)} %get-tuple-element.7.refs_0_), channel_id=1, source_target_pairs={{4,0},{12,4},{0,8},{8,12},{20,16},{28,20},{16,24},{24,28},{5,1},{1... | collective-permute-start | bytes 135176 | tf_op jit(solution)/shard_map/ppermute | solution.py:290
  6.5 0.0 collective-permute-start.1
  6.5 3.0 %collective-permute-start = (f32[88,128]{1,0:T(8,128)S(1)}, f32[88,128]{1,0:T(8,128)S(1)}, u32[]{:S(2)}, u32[]{:S(2)}) collective-permute-start(f32[88,128]{1,0:T(8,128)S(1)} %get-tuple-element.7.refs_0_), channel_id=1, source_target_pairs={{0,12},{4,8},{8,4},{12,0},{16,28},{20,24},{24,20},{28,16},{1,13},{... | collective-permute-start | bytes 135176 | tf_op jit(solution)/shard_map/ppermute | solution.py:290
  9.5 0.0 collective-permute-done.2.refs_3_
  9.5 1.3 %collective-permute-done.1.refs_2_ = f32[88,128]{1,0:T(8,128)S(1)} collective-permute-done((f32[88,128]{1,0:T(8,128)S(1)}, f32[88,128]{1,0:T(8,128)S(1)}, u32[]{:S(2)}, u32[]{:S(2)}) %collective-permute-start.1) | collective-permute-done | bytes 45088 | tf_op jit(solution)/shard_map/ppermute | solution.py:290
  10.8 0.8 %collective-permute-done.refs_1_ = f32[88,128]{1,0:T(8,128)S(1)} collective-permute-done((f32[88,128]{1,0:T(8,128)S(1)}, f32[88,128]{1,0:T(8,128)S(1)}, u32[]{:S(2)}, u32[]{:S(2)}) %collective-permute-start) | collective-permute-done | bytes 45088 | tf_op jit(solution)/shard_map/ppermute | solution.py:290
  11.5 0.1 merge.1.refs_0_
  11.7 3.0 %collective-permute-start.3 = (f32[88,128]{1,0:T(8,128)S(1)}, f32[88,128]{1,0:T(8,128)S(1)}, u32[]{:S(2)}, u32[]{:S(2)}) collective-permute-start(f32[88,128]{1,0:T(8,128)S(1)} %merge.1.refs_0_), channel_id=1, source_target_pairs={{0,16},{4,20},{8,24},{12,28},{16,0},{20,4},{24,8},{28,12},{1,17},{... | collective-permute-start | bytes 135176 | tf_op jit(solution)/shard_map/ppermute | solution.py:290
  14.7 2.0 %collective-permute-done.3.refs_1_ = f32[88,128]{1,0:T(8,128)S(1)} collective-permute-done((f32[88,128]{1,0:T(8,128)S(1)}, f32[88,128]{1,0:T(8,128)S(1)}, u32[]{:S(2)}, u32[]{:S(2)}) %collective-permute-start.3) | collective-permute-done | bytes 45088 | tf_op jit(solution)/shard_map/ppermute | solution.py:290
  16.7 0.4 %project.1 = f32[8,640]{1,0:T(8,128)S(1)} custom-call(f32[88,128]{1,0:T(8,128)S(1)} %merge.1.refs_0_, f32[88,128]{1,0:T(8,128)S(1)} %collective-permute-done.3.refs_1_, bf16[1280,640]{1,0:T(8,128)(2,1)S(1)} %get-tuple-element.8.refs_2_), custom_call_target="tpu_custom_call" | custom-call | tf_op jit(solution)/shard_map/project/pallas_call | solution.py:341
  17.2 0.1 collective-permute-start.6
  17.3 1.9 %collective-permute-start.5 = (f32[8,640]{1,0:T(8,128)S(1)}, f32[8,640]{1,0:T(8,128)S(1)}, u32[]{:S(2)}, u32[]{:S(2)}) collective-permute-start(f32[8,640]{1,0:T(8,128)S(1)} %project.1), channel_id=1, source_target_pairs={{0,2},{1,3},{2,0},{3,1},{4,6},{5,7},{6,4},{7,5},{8,10},{9,11},{10,... | collective-permute-start | bytes 61448 | tf_op jit(solution)/shard_map/ppermute | solution.py:290
  19.1 0.0 collective-permute-start.4
  19.2 1.3 %collective-permute-done.6 = f32[8,640]{1,0:T(8,128)S(1)} collective-permute-done((f32[8,640]{1,0:T(8,128)S(1)}, f32[8,640]{1,0:T(8,128)S(1)}, u32[]{:S(2)}, u32[]{:S(2)}) %collective-permute-start.6) | collective-permute-done | bytes 20512 | tf_op jit(solution)/shard_map/ppermute | solution.py:290
  20.4 0.7 %collective-permute-done.5 = f32[8,640]{1,0:T(8,128)S(1)} collective-permute-done((f32[8,640]{1,0:T(8,128)S(1)}, f32[8,640]{1,0:T(8,128)S(1)}, u32[]{:S(2)}, u32[]{:S(2)}) %collective-permute-start.5) | collective-permute-done | bytes 20512 | tf_op jit(solution)/shard_map/ppermute | solution.py:290
  21.1 0.0 collective-permute-done.4
  21.1 0.6 %add_add_fusion = f32[8,640]{1,0:T(8,128)} fusion(f32[8,640]{1,0:T(8,128)S(1)} %collective-permute-done.5, f32[8,640]{1,0:T(8,128)S(1)} %collective-permute-done.6, f32[8,640]{1,0:T(8,128)S(1)} %project.1, f32[8,640]{1,0:T(8,128)S(1)} %collective-permute-done.4), kind=kLoop, calls=%fused_computation | loop fusion | flops 15360 | bytes 102400 | tf_op jit(solution)/shard_map/add | solution.py:230
Async XLA Ops:
  3.4 6.1 %collective-permute-start.2 = (f32[88,128]{1,0:T(8,128)S(1)}, f32[88,128]{1,0:T(8,128)S(1)}, u32[]{:S(2)}, u32[]{:S(2)}) collective-permute-start(f32[88,128]{1,0:T(8,128)S(1)} %get-tuple-element.7.refs_0_), channel_id=1, source_target_pairs={{4,0},{12,4},{0,8},{8,12},{20,16},{28,20},{16,24},{24,28},{5,1},{1... | collective-permute-start | bytes 135176 | tf_op jit(solution)/shard_map/ppermute | solution.py:290
  6.5 4.2 %collective-permute-start.1 = (f32[88,128]{1,0:T(8,128)S(1)}, f32[88,128]{1,0:T(8,128)S(1)}, u32[]{:S(2)}, u32[]{:S(2)}) collective-permute-start(f32[88,128]{1,0:T(8,128)S(1)} %get-tuple-element.7.refs_0_), channel_id=1, source_target_pairs={{0,4},{4,12},{8,0},{12,8},{16,20},{20,28},{24,16},{28,24},{1,5},{5... | collective-permute-start | bytes 135176 | tf_op jit(solution)/shard_map/ppermute | solution.py:290
  6.5 5.0 %collective-permute-start = (f32[88,128]{1,0:T(8,128)S(1)}, f32[88,128]{1,0:T(8,128)S(1)}, u32[]{:S(2)}, u32[]{:S(2)}) collective-permute-start(f32[88,128]{1,0:T(8,128)S(1)} %get-tuple-element.7.refs_0_), channel_id=1, source_target_pairs={{0,12},{4,8},{8,4},{12,0},{16,28},{20,24},{24,20},{28,16},{1,13},{... | collective-permute-start | bytes 135176 | tf_op jit(solution)/shard_map/ppermute | solution.py:290
  11.7 5.1 %collective-permute-start.3 = (f32[88,128]{1,0:T(8,128)S(1)}, f32[88,128]{1,0:T(8,128)S(1)}, u32[]{:S(2)}, u32[]{:S(2)}) collective-permute-start(f32[88,128]{1,0:T(8,128)S(1)} %merge.1.refs_0_), channel_id=1, source_target_pairs={{0,16},{4,20},{8,24},{12,28},{16,0},{20,4},{24,8},{28,12},{1,17},{... | collective-permute-start | bytes 135176 | tf_op jit(solution)/shard_map/ppermute | solution.py:290
  17.2 3.3 %collective-permute-start.6 = (f32[8,640]{1,0:T(8,128)S(1)}, f32[8,640]{1,0:T(8,128)S(1)}, u32[]{:S(2)}, u32[]{:S(2)}) collective-permute-start(f32[8,640]{1,0:T(8,128)S(1)} %project.1), channel_id=1, source_target_pairs={{0,3},{1,2},{2,1},{3,0},{4,7},{5,6},{6,5},{7,4},{8,11},{9,10},{10,... | collective-permute-start | bytes 61448 | tf_op jit(solution)/shard_map/ppermute | solution.py:290
  17.3 3.8 %collective-permute-start.5 = (f32[8,640]{1,0:T(8,128)S(1)}, f32[8,640]{1,0:T(8,128)S(1)}, u32[]{:S(2)}, u32[]{:S(2)}) collective-permute-start(f32[8,640]{1,0:T(8,128)S(1)} %project.1), channel_id=1, source_target_pairs={{0,2},{1,3},{2,0},{3,1},{4,6},{5,7},{6,4},{7,5},{8,10},{9,11},{10,... | collective-permute-start | bytes 61448 | tf_op jit(solution)/shard_map/ppermute | solution.py:290
  19.1 2.0 %collective-permute-start.4 = (f32[8,640]{1,0:T(8,128)S(1)}, f32[8,640]{1,0:T(8,128)S(1)}, u32[]{:S(2)}, u32[]{:S(2)}) collective-permute-start(f32[8,640]{1,0:T(8,128)S(1)} %project.1), channel_id=1, source_target_pairs={{0,1},{1,0},{2,3},{3,2},{4,5},{5,4},{6,7},{7,6},{8,9},{9,8},{10,11... | collective-permute-start | bytes 61448 | tf_op jit(solution)/shard_map/ppermute | solution.py:290

commit v7 on v6

--- a/solution.py
+++ b/solution.py
@@ -139,6 +139,8 @@
     for b in range(batch):
         bound = jnp.where(lane1 // SLOT == b, limit[b], bound)
     lane_kv = jnp.minimum((lane1 % SLOT) // group, kv - 1)
+    row8 = lax.broadcasted_iota(jnp.int32, (8, lanes), 0)
+    bound8 = jnp.where(row8 % kv == lane_kv, bound - row8, -1)
 
     def rotate_keys(c):
         part = parts_at[c]
@@ -157,8 +159,9 @@
                 keys, qbd[...], (((1,), (1,)), ((), ())), preferred_element_type=F32
             ))
         s = jnp.concatenate(sums, axis=0) * scaling
-        row = parts_at[c].start + lax.broadcasted_iota(jnp.int32, s.shape, 0)
-        s = jnp.where((row % kv == lane_kv) & (row < bound), s, F32(NEG_FILL))
+        s = s.reshape(sizes[c] // 8, 8, lanes)
+        row = parts_at[c].start + 8 * lax.broadcasted_iota(jnp.int32, s.shape, 0)
+        s = jnp.where(row < bound8[None], s, F32(NEG_FILL)).reshape(sizes[c], lanes)
         scores[parts_at[c], :] = s
         return jnp.maximum(top, jnp.max(s, axis=0, keepdims=True))
 
@@ -193,7 +196,7 @@
     parts = []
     for c in range(chunks):
         s = scores[parts_at[c], :]
-        w = jnp.where(s > F32(0.5 * NEG_FILL), jnp.exp(s - top), 0.0)
+        w = jnp.exp(s - jnp.maximum(top, F32(0.5 * NEG_FILL)))
         total = total + jnp.sum(w, axis=0, keepdims=True)
         parts.append(jnp.transpose(w.astype(BF16)))
     wt = jnp.concatenate(parts, axis=1)

time: 22.1 us -> 22.1 us (level)
  no operation moved by 1% of the time
where the time goes in v7:
time: 22.1 us; the launch traced here: 21.7 us
  starting transfers between devices  11.1 us (50%)
  waiting for transfers between devices  5.97 us (27%)
  Pallas kernels  4.02 us (18%)
  other arithmetic  0.61 us (3%)
    ppermute x7, starting transfers between devices, gather_from(): return [value] + [lax.ppermute(value, axis, pairs) for pairs in moves]  11.1 us
    ppermute x7, waiting for transfers between devices, gather_from(): return [value] + [lax.ppermute(value, axis, pairs) for pairs in moves]  5.97 us
    pallas_call x1, Pallas kernels, body(): pl.pallas_call(functools.partial(attention_kernel, stretch=stretch, kv=kv...  3.43 us
    add x1, other arithmetic, balanced_sum(): values = [values[i] + values[i + 1] for i in range(0, len(values), 2)]  0.61 us
    pallas_call x1, Pallas kernels, body(): pl.pallas_call(functools.partial(project_kernel, heads=heads, batch=batch...  0.45 us
  transfers between devices with their start and end apart: 7, of which 5 were waited for; matrix products, arithmetic and copies ran while one was open for 0% of the time, Pallas kernels for 0%

profile of v7, /device:TPU:0, one launch (start us, length us, event | category | flops | bytes accessed | tf_op | source)
XLA Modules:
  0.0 21.7 jit_solution(5420823382893996210)
XLA Ops:
  0.0 3.4 %attention.1 = (f32[88,128]{1,0:T(8,128)S(1)}, bf16[1280,640]{1,0:T(8,128)(2,1)S(1)}) custom-call(s32[8]{0:T(128)} %lens_hbm.1, bf16[10,8,128]{2,1,0:T(8,128)(2,1)} %bitcast.5, bf16[8,2,128]{2,1,0:T(2,128)(2,1)} %nk_hbm.1, bf16[8,2,128]{2,1,0:T(2,128)(2,1)} %nv_hbm.1, bf16[8,1024,128]{2,1,0:T(8,128)(2,1)} %bitcast.3, bf16[8,1024,128]{2,1,0:T(8,128)(2,1)} %bitcast.4, ...), custom_call_target="tpu_custom_call" | custom-call | tf_op jit(solution)/shard_map/attention/pallas_call | solution.py:306
  3.4 3.1 %collective-permute-start.2 = (f32[88,128]{1,0:T(8,128)S(1)}, f32[88,128]{1,0:T(8,128)S(1)}, u32[]{:S(2)}, u32[]{:S(2)}) collective-permute-start(f32[88,128]{1,0:T(8,128)S(1)} %get-tuple-element.7.refs_0_), channel_id=1, source_target_pairs={{4,0},{12,4},{0,8},{8,12},{20,16},{28,20},{16,24},{24,28},{5,1},{1... | collective-permute-start | bytes 135176 | tf_op jit(solution)/shard_map/ppermute | solution.py:293
  6.5 0.0 collective-permute-start.1
  6.6 3.0 %collective-permute-start = (f32[88,128]{1,0:T(8,128)S(1)}, f32[88,128]{1,0:T(8,128)S(1)}, u32[]{:S(2)}, u32[]{:S(2)}) collective-permute-start(f32[88,128]{1,0:T(8,128)S(1)} %get-tuple-element.7.refs_0_), channel_id=1, source_target_pairs={{0,12},{4,8},{8,4},{12,0},{16,28},{20,24},{24,20},{28,16},{1,13},{... | collective-permute-start | bytes 135176 | tf_op jit(solution)/shard_map/ppermute | solution.py:293
  9.5 0.0 collective-permute-done.2.refs_3_
  9.5 1.3 %collective-permute-done.1.refs_2_ = f32[88,128]{1,0:T(8,128)S(1)} collective-permute-done((f32[88,128]{1,0:T(8,128)S(1)}, f32[88,128]{1,0:T(8,128)S(1)}, u32[]{:S(2)}, u32[]{:S(2)}) %collective-permute-start.1) | collective-permute-done | bytes 45088 | tf_op jit(solution)/shard_map/ppermute | solution.py:293
  10.8 0.8 %collective-permute-done.refs_1_ = f32[88,128]{1,0:T(8,128)S(1)} collective-permute-done((f32[88,128]{1,0:T(8,128)S(1)}, f32[88,128]{1,0:T(8,128)S(1)}, u32[]{:S(2)}, u32[]{:S(2)}) %collective-permute-start) | collective-permute-done | bytes 45088 | tf_op jit(solution)/shard_map/ppermute | solution.py:293
  11.6 0.1 merge.1.refs_0_
  11.7 3.0 %collective-permute-start.3 = (f32[88,128]{1,0:T(8,128)S(1)}, f32[88,128]{1,0:T(8,128)S(1)}, u32[]{:S(2)}, u32[]{:S(2)}) collective-permute-start(f32[88,128]{1,0:T(8,128)S(1)} %merge.1.refs_0_), channel_id=1, source_target_pairs={{0,16},{4,20},{8,24},{12,28},{16,0},{20,4},{24,8},{28,12},{1,17},{... | collective-permute-start | bytes 135176 | tf_op jit(solution)/shard_map/ppermute | solution.py:293
  14.7 2.0 %collective-permute-done.3.refs_1_ = f32[88,128]{1,0:T(8,128)S(1)} collective-permute-done((f32[88,128]{1,0:T(8,128)S(1)}, f32[88,128]{1,0:T(8,128)S(1)}, u32[]{:S(2)}, u32[]{:S(2)}) %collective-permute-start.3) | collective-permute-done | bytes 45088 | tf_op jit(solution)/shard_map/ppermute | solution.py:293
  16.8 0.4 %project.1 = f32[8,640]{1,0:T(8,128)S(1)} custom-call(f32[88,128]{1,0:T(8,128)S(1)} %merge.1.refs_0_, f32[88,128]{1,0:T(8,128)S(1)} %collective-permute-done.3.refs_1_, bf16[1280,640]{1,0:T(8,128)(2,1)S(1)} %get-tuple-element.8.refs_2_), custom_call_target="tpu_custom_call" | custom-call | tf_op jit(solution)/shard_map/project/pallas_call | solution.py:344
  17.2 0.1 collective-permute-start.6
  17.3 1.9 %collective-permute-start.5 = (f32[8,640]{1,0:T(8,128)S(1)}, f32[8,640]{1,0:T(8,128)S(1)}, u32[]{:S(2)}, u32[]{:S(2)}) collective-permute-start(f32[8,640]{1,0:T(8,128)S(1)} %project.1), channel_id=1, source_target_pairs={{0,2},{1,3},{2,0},{3,1},{4,6},{5,7},{6,4},{7,5},{8,10},{9,11},{10,... | collective-permute-start | bytes 61448 | tf_op jit(solution)/shard_map/ppermute | solution.py:293
  19.2 0.0 collective-permute-start.4
  19.2 1.3 %collective-permute-done.6 = f32[8,640]{1,0:T(8,128)S(1)} collective-permute-done((f32[8,640]{1,0:T(8,128)S(1)}, f32[8,640]{1,0:T(8,128)S(1)}, u32[]{:S(2)}, u32[]{:S(2)}) %collective-permute-start.6) | collective-permute-done | bytes 20512 | tf_op jit(solution)/shard_map/ppermute | solution.py:293
  20.5 0.7 %collective-permute-done.5 = f32[8,640]{1,0:T(8,128)S(1)} collective-permute-done((f32[8,640]{1,0:T(8,128)S(1)}, f32[8,640]{1,0:T(8,128)S(1)}, u32[]{:S(2)}, u32[]{:S(2)}) %collective-permute-start.5) | collective-permute-done | bytes 20512 | tf_op jit(solution)/shard_map/ppermute | solution.py:293
  21.1 0.0 collective-permute-done.4
  21.1 0.6 %add_add_fusion = f32[8,640]{1,0:T(8,128)} fusion(f32[8,640]{1,0:T(8,128)S(1)} %collective-permute-done.5, f32[8,640]{1,0:T(8,128)S(1)} %collective-permute-done.6, f32[8,640]{1,0:T(8,128)S(1)} %project.1, f32[8,640]{1,0:T(8,128)S(1)} %collective-permute-done.4), kind=kLoop, calls=%fused_computation | loop fusion | flops 15360 | bytes 102400 | tf_op jit(solution)/shard_map/add | solution.py:233
Async XLA Ops:
  3.4 6.1 %collective-permute-start.2 = (f32[88,128]{1,0:T(8,128)S(1)}, f32[88,128]{1,0:T(8,128)S(1)}, u32[]{:S(2)}, u32[]{:S(2)}) collective-permute-start(f32[88,128]{1,0:T(8,128)S(1)} %get-tuple-element.7.refs_0_), channel_id=1, source_target_pairs={{4,0},{12,4},{0,8},{8,12},{20,16},{28,20},{16,24},{24,28},{5,1},{1... | collective-permute-start | bytes 135176 | tf_op jit(solution)/shard_map/ppermute | solution.py:293
  6.5 4.2 %collective-permute-start.1 = (f32[88,128]{1,0:T(8,128)S(1)}, f32[88,128]{1,0:T(8,128)S(1)}, u32[]{:S(2)}, u32[]{:S(2)}) collective-permute-start(f32[88,128]{1,0:T(8,128)S(1)} %get-tuple-element.7.refs_0_), channel_id=1, source_target_pairs={{0,4},{4,12},{8,0},{12,8},{16,20},{20,28},{24,16},{28,24},{1,5},{5... | collective-permute-start | bytes 135176 | tf_op jit(solution)/shard_map/ppermute | solution.py:293
  6.6 5.0 %collective-permute-start = (f32[88,128]{1,0:T(8,128)S(1)}, f32[88,128]{1,0:T(8,128)S(1)}, u32[]{:S(2)}, u32[]{:S(2)}) collective-permute-start(f32[88,128]{1,0:T(8,128)S(1)} %get-tuple-element.7.refs_0_), channel_id=1, source_target_pairs={{0,12},{4,8},{8,4},{12,0},{16,28},{20,24},{24,20},{28,16},{1,13},{... | collective-permute-start | bytes 135176 | tf_op jit(solution)/shard_map/ppermute | solution.py:293
  11.7 5.1 %collective-permute-start.3 = (f32[88,128]{1,0:T(8,128)S(1)}, f32[88,128]{1,0:T(8,128)S(1)}, u32[]{:S(2)}, u32[]{:S(2)}) collective-permute-start(f32[88,128]{1,0:T(8,128)S(1)} %merge.1.refs_0_), channel_id=1, source_target_pairs={{0,16},{4,20},{8,24},{12,28},{16,0},{20,4},{24,8},{28,12},{1,17},{... | collective-permute-start | bytes 135176 | tf_op jit(solution)/shard_map/ppermute | solution.py:293
  17.2 3.3 %collective-permute-start.6 = (f32[8,640]{1,0:T(8,128)S(1)}, f32[8,640]{1,0:T(8,128)S(1)}, u32[]{:S(2)}, u32[]{:S(2)}) collective-permute-start(f32[8,640]{1,0:T(8,128)S(1)} %project.1), channel_id=1, source_target_pairs={{0,3},{1,2},{2,1},{3,0},{4,7},{5,6},{6,5},{7,4},{8,11},{9,10},{10,... | collective-permute-start | bytes 61448 | tf_op jit(solution)/shard_map/ppermute | solution.py:293
  17.3 3.8 %collective-permute-start.5 = (f32[8,640]{1,0:T(8,128)S(1)}, f32[8,640]{1,0:T(8,128)S(1)}, u32[]{:S(2)}, u32[]{:S(2)}) collective-permute-start(f32[8,640]{1,0:T(8,128)S(1)} %project.1), channel_id=1, source_target_pairs={{0,2},{1,3},{2,0},{3,1},{4,6},{5,7},{6,4},{7,5},{8,10},{9,11},{10,... | collective-permute-start | bytes 61448 | tf_op jit(solution)/shard_map/ppermute | solution.py:293
  19.2 2.0 %collective-permute-start.4 = (f32[8,640]{1,0:T(8,128)S(1)}, f32[8,640]{1,0:T(8,128)S(1)}, u32[]{:S(2)}, u32[]{:S(2)}) collective-permute-start(f32[8,640]{1,0:T(8,128)S(1)} %project.1), channel_id=1, source_target_pairs={{0,1},{1,0},{2,3},{3,2},{4,5},{5,4},{6,7},{7,6},{8,9},{9,8},{10,11... | collective-permute-start | bytes 61448 | tf_op jit(solution)/shard_map/ppermute | solution.py:293

commit v8 on v7

--- a/solution.py
+++ b/solution.py
@@ -82,7 +82,6 @@
     base = place * span
     key_stretch = base // stretch
 
-    qbd[...] = jnp.zeros_like(qbd)
     qin[...] = jnp.zeros_like(qin)
     freq8 = frequencies((batch, width))
     sign8 = half_sign((batch, width))
@@ -129,8 +128,12 @@
     for b in range(batch):
         mine = pl.ds(b, heads, stride=batch)
         at = slice(b * SLOT, b * SLOT + heads)
-        qbd[at, b * width : (b + 1) * width] = qrot[0, mine, :].astype(BF16)
-        qin[at, :] = qrot[1, mine, :].astype(BF16)
+        qin[0, at, :] = qrot[0, mine, :].astype(BF16)
+        qin[1, at, :] = qrot[1, mine, :].astype(BF16)
+    turned_q = jnp.transpose(qin[0])
+    q_lane = lax.broadcasted_iota(jnp.int32, (width, lanes), 1) // SLOT
+    for b in range(batch):
+        qbd[b * width : (b + 1) * width, :] = jnp.where(q_lane == b, turned_q, jnp.zeros_like(turned_q))
 
     scaling = F32(1.0 / math.sqrt(width))
 
@@ -155,9 +158,7 @@
         sums = []
         for part in (slice(0, half), slice(half, sizes[c])):
             keys = jnp.concatenate([kcats[c % 2][b, part, :] for b in range(batch)], axis=1)
-            sums.append(lax.dot_general(
-                keys, qbd[...], (((1,), (1,)), ((), ())), preferred_element_type=F32
-            ))
+            sums.append(jnp.dot(keys, qbd[...], preferred_element_type=F32))
         s = jnp.concatenate(sums, axis=0) * scaling
         s = s.reshape(sizes[c] // 8, 8, lanes)
         row = parts_at[c].start + 8 * lax.broadcasted_iota(jnp.int32, s.shape, 0)
@@ -176,7 +177,7 @@
                 [rotate(nkbuf[b].astype(F32), cr[b : b + 1], sr[b : b + 1]) for b in range(batch)], axis=0
             ).astype(BF16)
             own_all = lax.dot_general(
-                knew, qin[...], (((1,), (1,)), ((), ())), preferred_element_type=F32
+                knew, qin[1], (((1,), (1,)), ((), ())), preferred_element_type=F32
             ) * scaling
             own_row = lax.broadcasted_iota(jnp.int32, (own_rows, lanes), 0)
             own_lane = lax.broadcasted_iota(jnp.int32, (own_rows, lanes), 1)
@@ -318,8 +319,8 @@
             pltpu.VMEM((batch, rows, width), BF16),
             pltpu.VMEM((batch, max(sizes), width), BF16),
             pltpu.VMEM((batch, max(sizes), width), BF16),
-            pltpu.VMEM((lanes, batch * width), BF16),
-            pltpu.VMEM((lanes, width), BF16),
+            pltpu.VMEM((batch * width, lanes), BF16),
+            pltpu.VMEM((2, lanes, width), BF16),
             pltpu.VMEM((2, heads * batch, width), F32),
             pltpu.VMEM((rows, lanes), F32),
             dma((len(sizes),)), dma, dma, dma, dma, dma, dma, pltpu.SemaphoreType.REGULAR,

time: 22.1 us -> 22.1 us (level)
  no operation moved by 1% of the time
where the time goes in v8:
time: 22.1 us; the launch traced here: 21.7 us
  starting transfers between devices  11.1 us (50%)
  waiting for transfers between devices  5.97 us (27%)
  Pallas kernels  4.02 us (18%)
  other arithmetic  0.61 us (3%)
    ppermute x7, starting transfers between devices, gather_from(): return [value] + [lax.ppermute(value, axis, pairs) for pairs in moves]  11.1 us
    ppermute x7, waiting for transfers between devices, gather_from(): return [value] + [lax.ppermute(value, axis, pairs) for pairs in moves]  5.97 us
    pallas_call x1, Pallas kernels, body(): pl.pallas_call(functools.partial(attention_kernel, stretch=stretch, kv=kv...  3.44 us
    add x1, other arithmetic, balanced_sum(): values = [values[i] + values[i + 1] for i in range(0, len(values), 2)]  0.61 us
    pallas_call x1, Pallas kernels, body(): pl.pallas_call(functools.partial(project_kernel, heads=heads, batch=batch...  0.45 us
  transfers between devices with their start and end apart: 7, of which 5 were waited for; matrix products, arithmetic and copies ran while one was open for 0% of the time, Pallas kernels for 0%

profile of v8, /device:TPU:0, one launch (start us, length us, event | category | flops | bytes accessed | tf_op | source)
XLA Modules:
  0.0 21.7 jit_solution(7291245775171549881)
XLA Ops:
  0.0 3.4 %attention.1 = (f32[88,128]{1,0:T(8,128)S(1)}, bf16[1280,640]{1,0:T(8,128)(2,1)S(1)}) custom-call(s32[8]{0:T(128)} %lens_hbm.1, bf16[10,8,128]{2,1,0:T(8,128)(2,1)} %bitcast.5, bf16[8,2,128]{2,1,0:T(2,128)(2,1)} %nk_hbm.1, bf16[8,2,128]{2,1,0:T(2,128)(2,1)} %nv_hbm.1, bf16[8,1024,128]{2,1,0:T(8,128)(2,1)} %bitcast.3, bf16[8,1024,128]{2,1,0:T(8,128)(2,1)} %bitcast.4, ...), custom_call_target="tpu_custom_call" | custom-call | tf_op jit(solution)/shard_map/attention/pallas_call | solution.py:307
  3.4 3.1 %collective-permute-start.2 = (f32[88,128]{1,0:T(8,128)S(1)}, f32[88,128]{1,0:T(8,128)S(1)}, u32[]{:S(2)}, u32[]{:S(2)}) collective-permute-start(f32[88,128]{1,0:T(8,128)S(1)} %get-tuple-element.7.refs_0_), channel_id=1, source_target_pairs={{4,0},{12,4},{0,8},{8,12},{20,16},{28,20},{16,24},{24,28},{5,1},{1... | collective-permute-start | bytes 135176 | tf_op jit(solution)/shard_map/ppermute | solution.py:294
  6.5 0.0 collective-permute-start.1
  6.6 3.0 %collective-permute-start = (f32[88,128]{1,0:T(8,128)S(1)}, f32[88,128]{1,0:T(8,128)S(1)}, u32[]{:S(2)}, u32[]{:S(2)}) collective-permute-start(f32[88,128]{1,0:T(8,128)S(1)} %get-tuple-element.7.refs_0_), channel_id=1, source_target_pairs={{0,12},{4,8},{8,4},{12,0},{16,28},{20,24},{24,20},{28,16},{1,13},{... | collective-permute-start | bytes 135176 | tf_op jit(solution)/shard_map/ppermute | solution.py:294
  9.5 0.0 collective-permute-done.2.refs_3_
  9.5 1.3 %collective-permute-done.1.refs_2_ = f32[88,128]{1,0:T(8,128)S(1)} collective-permute-done((f32[88,128]{1,0:T(8,128)S(1)}, f32[88,128]{1,0:T(8,128)S(1)}, u32[]{:S(2)}, u32[]{:S(2)}) %collective-permute-start.1) | collective-permute-done | bytes 45088 | tf_op jit(solution)/shard_map/ppermute | solution.py:294
  10.8 0.8 %collective-permute-done.refs_1_ = f32[88,128]{1,0:T(8,128)S(1)} collective-permute-done((f32[88,128]{1,0:T(8,128)S(1)}, f32[88,128]{1,0:T(8,128)S(1)}, u32[]{:S(2)}, u32[]{:S(2)}) %collective-permute-start) | collective-permute-done | bytes 45088 | tf_op jit(solution)/shard_map/ppermute | solution.py:294
  11.6 0.1 merge.1.refs_0_
  11.7 3.0 %collective-permute-start.3 = (f32[88,128]{1,0:T(8,128)S(1)}, f32[88,128]{1,0:T(8,128)S(1)}, u32[]{:S(2)}, u32[]{:S(2)}) collective-permute-start(f32[88,128]{1,0:T(8,128)S(1)} %merge.1.refs_0_), channel_id=1, source_target_pairs={{0,16},{4,20},{8,24},{12,28},{16,0},{20,4},{24,8},{28,12},{1,17},{... | collective-permute-start | bytes 135176 | tf_op jit(solution)/shard_map/ppermute | solution.py:294
  14.7 2.0 %collective-permute-done.3.refs_1_ = f32[88,128]{1,0:T(8,128)S(1)} collective-permute-done((f32[88,128]{1,0:T(8,128)S(1)}, f32[88,128]{1,0:T(8,128)S(1)}, u32[]{:S(2)}, u32[]{:S(2)}) %collective-permute-start.3) | collective-permute-done | bytes 45088 | tf_op jit(solution)/shard_map/ppermute | solution.py:294
  16.8 0.4 %project.1 = f32[8,640]{1,0:T(8,128)S(1)} custom-call(f32[88,128]{1,0:T(8,128)S(1)} %merge.1.refs_0_, f32[88,128]{1,0:T(8,128)S(1)} %collective-permute-done.3.refs_1_, bf16[1280,640]{1,0:T(8,128)(2,1)S(1)} %get-tuple-element.8.refs_2_), custom_call_target="tpu_custom_call" | custom-call | tf_op jit(solution)/shard_map/project/pallas_call | solution.py:345
  17.2 0.1 collective-permute-start.6
  17.3 1.9 %collective-permute-start.5 = (f32[8,640]{1,0:T(8,128)S(1)}, f32[8,640]{1,0:T(8,128)S(1)}, u32[]{:S(2)}, u32[]{:S(2)}) collective-permute-start(f32[8,640]{1,0:T(8,128)S(1)} %project.1), channel_id=1, source_target_pairs={{0,2},{1,3},{2,0},{3,1},{4,6},{5,7},{6,4},{7,5},{8,10},{9,11},{10,... | collective-permute-start | bytes 61448 | tf_op jit(solution)/shard_map/ppermute | solution.py:294
  19.2 0.0 collective-permute-start.4
  19.2 1.3 %collective-permute-done.6 = f32[8,640]{1,0:T(8,128)S(1)} collective-permute-done((f32[8,640]{1,0:T(8,128)S(1)}, f32[8,640]{1,0:T(8,128)S(1)}, u32[]{:S(2)}, u32[]{:S(2)}) %collective-permute-start.6) | collective-permute-done | bytes 20512 | tf_op jit(solution)/shard_map/ppermute | solution.py:294
  20.5 0.7 %collective-permute-done.5 = f32[8,640]{1,0:T(8,128)S(1)} collective-permute-done((f32[8,640]{1,0:T(8,128)S(1)}, f32[8,640]{1,0:T(8,128)S(1)}, u32[]{:S(2)}, u32[]{:S(2)}) %collective-permute-start.5) | collective-permute-done | bytes 20512 | tf_op jit(solution)/shard_map/ppermute | solution.py:294
  21.1 0.0 collective-permute-done.4
  21.1 0.6 %add_add_fusion = f32[8,640]{1,0:T(8,128)} fusion(f32[8,640]{1,0:T(8,128)S(1)} %collective-permute-done.5, f32[8,640]{1,0:T(8,128)S(1)} %collective-permute-done.6, f32[8,640]{1,0:T(8,128)S(1)} %project.1, f32[8,640]{1,0:T(8,128)S(1)} %collective-permute-done.4), kind=kLoop, calls=%fused_computation | loop fusion | flops 15360 | bytes 102400 | tf_op jit(solution)/shard_map/add | solution.py:234
Async XLA Ops:
  3.4 6.1 %collective-permute-start.2 = (f32[88,128]{1,0:T(8,128)S(1)}, f32[88,128]{1,0:T(8,128)S(1)}, u32[]{:S(2)}, u32[]{:S(2)}) collective-permute-start(f32[88,128]{1,0:T(8,128)S(1)} %get-tuple-element.7.refs_0_), channel_id=1, source_target_pairs={{4,0},{12,4},{0,8},{8,12},{20,16},{28,20},{16,24},{24,28},{5,1},{1... | collective-permute-start | bytes 135176 | tf_op jit(solution)/shard_map/ppermute | solution.py:294
  6.5 4.2 %collective-permute-start.1 = (f32[88,128]{1,0:T(8,128)S(1)}, f32[88,128]{1,0:T(8,128)S(1)}, u32[]{:S(2)}, u32[]{:S(2)}) collective-permute-start(f32[88,128]{1,0:T(8,128)S(1)} %get-tuple-element.7.refs_0_), channel_id=1, source_target_pairs={{0,4},{4,12},{8,0},{12,8},{16,20},{20,28},{24,16},{28,24},{1,5},{5... | collective-permute-start | bytes 135176 | tf_op jit(solution)/shard_map/ppermute | solution.py:294
  6.6 5.0 %collective-permute-start = (f32[88,128]{1,0:T(8,128)S(1)}, f32[88,128]{1,0:T(8,128)S(1)}, u32[]{:S(2)}, u32[]{:S(2)}) collective-permute-start(f32[88,128]{1,0:T(8,128)S(1)} %get-tuple-element.7.refs_0_), channel_id=1, source_target_pairs={{0,12},{4,8},{8,4},{12,0},{16,28},{20,24},{24,20},{28,16},{1,13},{... | collective-permute-start | bytes 135176 | tf_op jit(solution)/shard_map/ppermute | solution.py:294
  11.7 5.1 %collective-permute-start.3 = (f32[88,128]{1,0:T(8,128)S(1)}, f32[88,128]{1,0:T(8,128)S(1)}, u32[]{:S(2)}, u32[]{:S(2)}) collective-permute-start(f32[88,128]{1,0:T(8,128)S(1)} %merge.1.refs_0_), channel_id=1, source_target_pairs={{0,16},{4,20},{8,24},{12,28},{16,0},{20,4},{24,8},{28,12},{1,17},{... | collective-permute-start | bytes 135176 | tf_op jit(solution)/shard_map/ppermute | solution.py:294
  17.2 3.3 %collective-permute-start.6 = (f32[8,640]{1,0:T(8,128)S(1)}, f32[8,640]{1,0:T(8,128)S(1)}, u32[]{:S(2)}, u32[]{:S(2)}) collective-permute-start(f32[8,640]{1,0:T(8,128)S(1)} %project.1), channel_id=1, source_target_pairs={{0,3},{1,2},{2,1},{3,0},{4,7},{5,6},{6,5},{7,4},{8,11},{9,10},{10,... | collective-permute-start | bytes 61448 | tf_op jit(solution)/shard_map/ppermute | solution.py:294
  17.3 3.8 %collective-permute-start.5 = (f32[8,640]{1,0:T(8,128)S(1)}, f32[8,640]{1,0:T(8,128)S(1)}, u32[]{:S(2)}, u32[]{:S(2)}) collective-permute-start(f32[8,640]{1,0:T(8,128)S(1)} %project.1), channel_id=1, source_target_pairs={{0,2},{1,3},{2,0},{3,1},{4,6},{5,7},{6,4},{7,5},{8,10},{9,11},{10,... | collective-permute-start | bytes 61448 | tf_op jit(solution)/shard_map/ppermute | solution.py:294
  19.2 2.0 %collective-permute-start.4 = (f32[8,640]{1,0:T(8,128)S(1)}, f32[8,640]{1,0:T(8,128)S(1)}, u32[]{:S(2)}, u32[]{:S(2)}) collective-permute-start(f32[8,640]{1,0:T(8,128)S(1)} %project.1), channel_id=1, source_target_pairs={{0,1},{1,0},{2,3},{3,2},{4,5},{5,4},{6,7},{7,6},{8,9},{9,8},{10,11... | collective-permute-start | bytes 61448 | tf_op jit(solution)/shard_map/ppermute | solution.py:294

commit v9 on v8

--- a/solution.py
+++ b/solution.py
@@ -259,8 +259,9 @@
 def project_kernel(*refs, heads, batch):
     w_ref, out_ref = refs[-2:]
     sums, stats = merge(refs[:-2], heads, batch)
+    inverse = 1.0 / stats
     attended = jnp.concatenate(
-        [(sums[h] / stats[:, SLOT + h : SLOT + h + 1]).astype(BF16) for h in range(heads)], axis=1
+        [(sums[h] * inverse[:, SLOT + h : SLOT + h + 1]).astype(BF16) for h in range(heads)], axis=1
     )
     out_ref[...] = jnp.dot(attended, w_ref[...], preferred_element_type=F32)
 

time: 22.1 us -> 22.1 us (level)
  no operation moved by 1% of the time
where the time goes in v9:
time: 22.1 us; the launch traced here: 21.7 us
  starting transfers between devices  11.1 us (50%)
  waiting for transfers between devices  5.97 us (27%)
  Pallas kernels  4.02 us (18%)
  other arithmetic  0.61 us (3%)
    ppermute x7, starting transfers between devices, gather_from(): return [value] + [lax.ppermute(value, axis, pairs) for pairs in moves]  11.1 us
    ppermute x7, waiting for transfers between devices, gather_from(): return [value] + [lax.ppermute(value, axis, pairs) for pairs in moves]  5.97 us
    pallas_call x1, Pallas kernels, body(): pl.pallas_call(functools.partial(attention_kernel, stretch=stretch, kv=kv...  3.44 us
    add x1, other arithmetic, balanced_sum(): values = [values[i] + values[i + 1] for i in range(0, len(values), 2)]  0.61 us
    pallas_call x1, Pallas kernels, body(): pl.pallas_call(functools.partial(project_kernel, heads=heads, batch=batch...  0.45 us
  transfers between devices with their start and end apart: 7, of which 5 were waited for; matrix products, arithmetic and copies ran while one was open for 0% of the time, Pallas kernels for 0%

profile of v9, /device:TPU:0, one launch (start us, length us, event | category | flops | bytes accessed | tf_op | source)
XLA Modules:
  0.0 21.7 jit_solution(13517490297019469812)
XLA Ops:
  0.0 3.4 %attention.1 = (f32[88,128]{1,0:T(8,128)S(1)}, bf16[1280,640]{1,0:T(8,128)(2,1)S(1)}) custom-call(s32[8]{0:T(128)} %lens_hbm.1, bf16[10,8,128]{2,1,0:T(8,128)(2,1)} %bitcast.5, bf16[8,2,128]{2,1,0:T(2,128)(2,1)} %nk_hbm.1, bf16[8,2,128]{2,1,0:T(2,128)(2,1)} %nv_hbm.1, bf16[8,1024,128]{2,1,0:T(8,128)(2,1)} %bitcast.3, bf16[8,1024,128]{2,1,0:T(8,128)(2,1)} %bitcast.4, ...), custom_call_target="tpu_custom_call" | custom-call | tf_op jit(solution)/shard_map/attention/pallas_call | solution.py:308
  3.4 3.1 %collective-permute-start.2 = (f32[88,128]{1,0:T(8,128)S(1)}, f32[88,128]{1,0:T(8,128)S(1)}, u32[]{:S(2)}, u32[]{:S(2)}) collective-permute-start(f32[88,128]{1,0:T(8,128)S(1)} %get-tuple-element.7.refs_0_), channel_id=1, source_target_pairs={{4,0},{12,4},{0,8},{8,12},{20,16},{28,20},{16,24},{24,28},{5,1},{1... | collective-permute-start | bytes 135176 | tf_op jit(solution)/shard_map/ppermute | solution.py:295
  6.5 0.0 collective-permute-start.1
  6.6 3.0 %collective-permute-start = (f32[88,128]{1,0:T(8,128)S(1)}, f32[88,128]{1,0:T(8,128)S(1)}, u32[]{:S(2)}, u32[]{:S(2)}) collective-permute-start(f32[88,128]{1,0:T(8,128)S(1)} %get-tuple-element.7.refs_0_), channel_id=1, source_target_pairs={{0,12},{4,8},{8,4},{12,0},{16,28},{20,24},{24,20},{28,16},{1,13},{... | collective-permute-start | bytes 135176 | tf_op jit(solution)/shard_map/ppermute | solution.py:295
  9.5 0.0 collective-permute-done.2.refs_3_
  9.5 1.3 %collective-permute-done.1.refs_2_ = f32[88,128]{1,0:T(8,128)S(1)} collective-permute-done((f32[88,128]{1,0:T(8,128)S(1)}, f32[88,128]{1,0:T(8,128)S(1)}, u32[]{:S(2)}, u32[]{:S(2)}) %collective-permute-start.1) | collective-permute-done | bytes 45088 | tf_op jit(solution)/shard_map/ppermute | solution.py:295
  10.8 0.8 %collective-permute-done.refs_1_ = f32[88,128]{1,0:T(8,128)S(1)} collective-permute-done((f32[88,128]{1,0:T(8,128)S(1)}, f32[88,128]{1,0:T(8,128)S(1)}, u32[]{:S(2)}, u32[]{:S(2)}) %collective-permute-start) | collective-permute-done | bytes 45088 | tf_op jit(solution)/shard_map/ppermute | solution.py:295
  11.6 0.1 merge.1.refs_0_
  11.7 3.0 %collective-permute-start.3 = (f32[88,128]{1,0:T(8,128)S(1)}, f32[88,128]{1,0:T(8,128)S(1)}, u32[]{:S(2)}, u32[]{:S(2)}) collective-permute-start(f32[88,128]{1,0:T(8,128)S(1)} %merge.1.refs_0_), channel_id=1, source_target_pairs={{0,16},{4,20},{8,24},{12,28},{16,0},{20,4},{24,8},{28,12},{1,17},{... | collective-permute-start | bytes 135176 | tf_op jit(solution)/shard_map/ppermute | solution.py:295
  14.7 2.0 %collective-permute-done.3.refs_1_ = f32[88,128]{1,0:T(8,128)S(1)} collective-permute-done((f32[88,128]{1,0:T(8,128)S(1)}, f32[88,128]{1,0:T(8,128)S(1)}, u32[]{:S(2)}, u32[]{:S(2)}) %collective-permute-start.3) | collective-permute-done | bytes 45088 | tf_op jit(solution)/shard_map/ppermute | solution.py:295
  16.8 0.4 %project.1 = f32[8,640]{1,0:T(8,128)S(1)} custom-call(f32[88,128]{1,0:T(8,128)S(1)} %merge.1.refs_0_, f32[88,128]{1,0:T(8,128)S(1)} %collective-permute-done.3.refs_1_, bf16[1280,640]{1,0:T(8,128)(2,1)S(1)} %get-tuple-element.8.refs_2_), custom_call_target="tpu_custom_call" | custom-call | tf_op jit(solution)/shard_map/project/pallas_call | solution.py:346
  17.2 0.1 collective-permute-start.6
  17.3 1.9 %collective-permute-start.5 = (f32[8,640]{1,0:T(8,128)S(1)}, f32[8,640]{1,0:T(8,128)S(1)}, u32[]{:S(2)}, u32[]{:S(2)}) collective-permute-start(f32[8,640]{1,0:T(8,128)S(1)} %project.1), channel_id=1, source_target_pairs={{0,2},{1,3},{2,0},{3,1},{4,6},{5,7},{6,4},{7,5},{8,10},{9,11},{10,... | collective-permute-start | bytes 61448 | tf_op jit(solution)/shard_map/ppermute | solution.py:295
  19.2 0.0 collective-permute-start.4
  19.2 1.3 %collective-permute-done.6 = f32[8,640]{1,0:T(8,128)S(1)} collective-permute-done((f32[8,640]{1,0:T(8,128)S(1)}, f32[8,640]{1,0:T(8,128)S(1)}, u32[]{:S(2)}, u32[]{:S(2)}) %collective-permute-start.6) | collective-permute-done | bytes 20512 | tf_op jit(solution)/shard_map/ppermute | solution.py:295
  20.5 0.7 %collective-permute-done.5 = f32[8,640]{1,0:T(8,128)S(1)} collective-permute-done((f32[8,640]{1,0:T(8,128)S(1)}, f32[8,640]{1,0:T(8,128)S(1)}, u32[]{:S(2)}, u32[]{:S(2)}) %collective-permute-start.5) | collective-permute-done | bytes 20512 | tf_op jit(solution)/shard_map/ppermute | solution.py:295
  21.1 0.0 collective-permute-done.4
  21.1 0.6 %add_add_fusion = f32[8,640]{1,0:T(8,128)} fusion(f32[8,640]{1,0:T(8,128)S(1)} %collective-permute-done.5, f32[8,640]{1,0:T(8,128)S(1)} %collective-permute-done.6, f32[8,640]{1,0:T(8,128)S(1)} %project.1, f32[8,640]{1,0:T(8,128)S(1)} %collective-permute-done.4), kind=kLoop, calls=%fused_computation | loop fusion | flops 15360 | bytes 102400 | tf_op jit(solution)/shard_map/add | solution.py:234
Async XLA Ops:
  3.4 6.1 %collective-permute-start.2 = (f32[88,128]{1,0:T(8,128)S(1)}, f32[88,128]{1,0:T(8,128)S(1)}, u32[]{:S(2)}, u32[]{:S(2)}) collective-permute-start(f32[88,128]{1,0:T(8,128)S(1)} %get-tuple-element.7.refs_0_), channel_id=1, source_target_pairs={{4,0},{12,4},{0,8},{8,12},{20,16},{28,20},{16,24},{24,28},{5,1},{1... | collective-permute-start | bytes 135176 | tf_op jit(solution)/shard_map/ppermute | solution.py:295
  6.5 4.2 %collective-permute-start.1 = (f32[88,128]{1,0:T(8,128)S(1)}, f32[88,128]{1,0:T(8,128)S(1)}, u32[]{:S(2)}, u32[]{:S(2)}) collective-permute-start(f32[88,128]{1,0:T(8,128)S(1)} %get-tuple-element.7.refs_0_), channel_id=1, source_target_pairs={{0,4},{4,12},{8,0},{12,8},{16,20},{20,28},{24,16},{28,24},{1,5},{5... | collective-permute-start | bytes 135176 | tf_op jit(solution)/shard_map/ppermute | solution.py:295
  6.6 5.0 %collective-permute-start = (f32[88,128]{1,0:T(8,128)S(1)}, f32[88,128]{1,0:T(8,128)S(1)}, u32[]{:S(2)}, u32[]{:S(2)}) collective-permute-start(f32[88,128]{1,0:T(8,128)S(1)} %get-tuple-element.7.refs_0_), channel_id=1, source_target_pairs={{0,12},{4,8},{8,4},{12,0},{16,28},{20,24},{24,20},{28,16},{1,13},{... | collective-permute-start | bytes 135176 | tf_op jit(solution)/shard_map/ppermute | solution.py:295
  11.7 5.1 %collective-permute-start.3 = (f32[88,128]{1,0:T(8,128)S(1)}, f32[88,128]{1,0:T(8,128)S(1)}, u32[]{:S(2)}, u32[]{:S(2)}) collective-permute-start(f32[88,128]{1,0:T(8,128)S(1)} %merge.1.refs_0_), channel_id=1, source_target_pairs={{0,16},{4,20},{8,24},{12,28},{16,0},{20,4},{24,8},{28,12},{1,17},{... | collective-permute-start | bytes 135176 | tf_op jit(solution)/shard_map/ppermute | solution.py:295
  17.2 3.3 %collective-permute-start.6 = (f32[8,640]{1,0:T(8,128)S(1)}, f32[8,640]{1,0:T(8,128)S(1)}, u32[]{:S(2)}, u32[]{:S(2)}) collective-permute-start(f32[8,640]{1,0:T(8,128)S(1)} %project.1), channel_id=1, source_target_pairs={{0,3},{1,2},{2,1},{3,0},{4,7},{5,6},{6,5},{7,4},{8,11},{9,10},{10,... | collective-permute-start | bytes 61448 | tf_op jit(solution)/shard_map/ppermute | solution.py:295
  17.3 3.8 %collective-permute-start.5 = (f32[8,640]{1,0:T(8,128)S(1)}, f32[8,640]{1,0:T(8,128)S(1)}, u32[]{:S(2)}, u32[]{:S(2)}) collective-permute-start(f32[8,640]{1,0:T(8,128)S(1)} %project.1), channel_id=1, source_target_pairs={{0,2},{1,3},{2,0},{3,1},{4,6},{5,7},{6,4},{7,5},{8,10},{9,11},{10,... | collective-permute-start | bytes 61448 | tf_op jit(solution)/shard_map/ppermute | solution.py:295
  19.2 2.0 %collective-permute-start.4 = (f32[8,640]{1,0:T(8,128)S(1)}, f32[8,640]{1,0:T(8,128)S(1)}, u32[]{:S(2)}, u32[]{:S(2)}) collective-permute-start(f32[8,640]{1,0:T(8,128)S(1)} %project.1), channel_id=1, source_target_pairs={{0,1},{1,0},{2,3},{3,2},{4,5},{5,4},{6,7},{7,6},{8,9},{9,8},{10,11... | collective-permute-start | bytes 61448 | tf_op jit(solution)/shard_map/ppermute | solution.py:295
